TPU v7x, 128 devices: a whole 4x4x4 slice. The times are simulated.
128 devices in a mesh: seq: 64 (over x, z, y), head: 2 (over core).
Axes of the slice: x: 4, y: 4, z: 4, core: 2. Of those that a mesh axis runs over, the one named last changes fastest.
Arguments:
- queries: bfloat16 [16384, 4096], P('seq', 'head'), may hold values from -210 to 210
- keys: bfloat16 [16384, 1024], P('seq', 'head'), may hold values from -7 to 7
- values: bfloat16 [16384, 1024], P('seq', 'head'), may hold values from -6 to 6
- vertical: int32 [8, 64], P('head'), may hold values from 0 to 255, as said below
- slash: int32 [8, 2], P('head'), may hold values from 1 to 4, as said below
- out_weight: bfloat16 [4096, 4096], P('head'), may hold values from -1 to 1
Outputs:
- mixed: bfloat16 [16384, 4096], P(('seq', 'head'))
Inputs may be any that keep to these rules, and one draw needn't show every extreme that they name: `vertical`: for each key-value head, 64 different key blocks in increasing order; block b lies in slab b // 4; no slab holds more than 2 of one head's blocks, and for every head some slab holds exactly 2. `slash`: for each key-value head, 2 different offsets in increasing order; some head has the offset 256 // 64.
All inputs are finite; a program needn't handle non-finite values.
Results may differ from a plain program's by a relative error of at most 0.01.
Values may be sent and summed in bfloat16 or wider, within the bound.
No kernel may reach another device: no remote copies, remote signals or barrier semaphores. Data moves between devices by JAX's collectives and lax.ppermute only.
A program may use at most 128 MiB of HBM per device.

v0:
```python
import functools

import jax
import jax.numpy as jnp
from jax import lax
from jax.experimental import pallas as pl
from jax.experimental.pallas import tpu as pltpu
from jax.sharding import Mesh
from jax.sharding import PartitionSpec as P

HEAD_DIM = 128
BLK = 64
SLAB = 256
NV = 64
EXP2_SCALE = HEAD_DIM ** (-0.5) * 1.4426950408889634
NEGATIVE = -1e30
ALL = ("x", "z", "y", "c")
MIB = 1 << 20


def moved(value, target):
    pairs = []
    for x in range(4):
        for z in range(4):
            for y in range(4):
                for c in range(2):
                    tx, tz, ty, tc = target(x, z, y, c)
                    pairs.append((((x * 4 + z) * 4 + y) * 2 + c, (((tx % 4) * 4 + tz % 4) * 4 + ty % 4) * 2 + tc))
    return lax.ppermute(value, ALL, pairs)


def along_y(value, by):
    return moved(value, lambda x, z, y, c: (x, z, y + by, c))


def first_hop(value, by):
    return moved(value, lambda x, z, y, c: (x + by, z, y, c) if c == 0 else (x, z + by, y, c))


def second_hop(value, by):
    return moved(value, lambda x, z, y, c: (x, z + by, y, c) if c == 0 else (x + by, z, y, c))


def to_next_group(value):
    return moved(value, lambda x, z, y, c: (x + (z + 1) // 4, z + 1, y, c))


def to_partner(value):
    return moved(value, lambda x, z, y, c: (x, z, y, 1 - c))


def rank_of(vert_ref, head, block):
    at = jnp.int32(0)
    for width in (32, 16, 8, 4, 2, 1):
        at = at + jnp.where(vert_ref[head, at + width - 1] < block, width, 0)
    return at + jnp.where(vert_ref[head, at] < block, 1, 0)


def kv_kernel(place_ref, keys_ref, values_ref, *out_refs):
    y = place_ref[1]
    for by in range(4):
        lanes = pl.ds(pl.multiple_of((y + by) % 4 * HEAD_DIM, HEAD_DIM), HEAD_DIM)
        out_refs[by][:, 0:128] = keys_ref[:, lanes]
        out_refs[by][:, 128:256] = values_ref[:, lanes]


def q_kernel(place_ref, queries_ref, *out_refs):
    y = place_ref[1]
    for by in range(4):
        out_refs[by][...] = queries_ref[:, pl.ds(pl.multiple_of((y + by) % 4 * 512, 512), 512)]


def slots_kernel(place_ref, vert_ref, kv0, kv1, kv2, kv3, own_ref, last_ref):
    group, y = place_ref[0], place_ref[1]
    for by, kv in enumerate((kv0, kv1, kv2, kv3)):
        slab = (y - by + 4) % 4
        first = (group * 4 + slab) * 4
        at = rank_of(vert_ref, y, first)
        for slot in range(2):
            entry = jnp.minimum(at + slot, NV - 1)
            block = vert_ref[y, entry] - first
            block = jnp.where((block >= 0) & (block < 4), block, 0)
            rows = pl.ds(pl.multiple_of(block * BLK, BLK), BLK)
            to = by * 256 + slot * BLK
            own_ref[to : to + BLK, :] = kv[rows, 0:128]
            own_ref[to + 128 : to + 128 + BLK, :] = kv[rows, 128:256]

        @pl.when(slab == 3)
        def _():
            last_ref[...] = kv[...]


CHUNK = 1024
PER_CHUNK = CHUNK // BLK


def scores_of(keys, q):
    return lax.dot_general(keys, q, (((1,), (1,)), ((), ())), preferred_element_type=jnp.float32)


def top_of(load, pieces):
    top = load(0)
    for t in range(1, pieces):
        top = jnp.maximum(top, load(t))
    eight = top[0:8]
    for r in range(1, 8):
        eight = jnp.maximum(eight, top[8 * r : 8 * r + 8])
    return eight


def weigh(i, load, pieces, eight, values, top, tot, acc):
    old = top[i]
    new = jnp.maximum(old, jnp.max(eight, axis=0, keepdims=True))
    level = new[0:1]
    rounded, part = [], None
    for t in range(pieces):
        weights = jnp.exp2((load(t) - level) * EXP2_SCALE)
        for r in range(8):
            piece = weights[8 * r : 8 * r + 8]
            part = piece if part is None else part + piece
        rounded.append(weights.astype(jnp.bfloat16))
    product = jnp.dot(values, jnp.concatenate(rounded, axis=0), preferred_element_type=jnp.float32)
    shrink = jnp.exp2((old - new) * EXP2_SCALE)
    top[i] = new
    tot[i] = tot[i] * shrink + part
    acc[i] = acc[i] * shrink[0:1] + product


def block_of(place_ref, i):
    return place_ref[0] * 16 + ((place_ref[1] - i // 4 + 4) % 4) * 4 + i % 4


def find_bounds(vert_ref, head, bounds):
    bounds[0] = 0
    for g in range(1, 16):
        bounds[g] = rank_of(vert_ref, head, 16 * g)
    bounds[16] = NV


def walk(place_ref, vert_ref, bounds, order, outer, at, sources, kc, vc):
    y, mine1, mine2, core = (place_ref[i] for i in range(1, 5))
    head = y
    second = (mine2 - outer + 4) % 4
    for inner in range(4):
        first = (mine1 - inner + 4) % 4
        g = jnp.where(core == 0, first * 4 + second, second * 4 + first)
        start, end = bounds[g], bounds[g + 1]
        shift = at - start

        def one(entry, carry):
            block = vert_ref[head, entry]
            to = entry + shift
            order[to] = block
            if sources is not None:
                source = sources[inner * len(sources) // 4]
                skip = inner % (4 // len(sources))
                slab = block // 4
                before = vert_ref[head, jnp.maximum(entry - 1, 0)] // 4
                rank = jnp.where((entry > 0) & (before == slab), BLK, 0)
                row = (skip * 4 + (y - slab % 4 + 4) % 4) * 256 + rank
                rows = pl.ds(pl.multiple_of(to * BLK, BLK), BLK)
                kc[rows, :] = source[pl.ds(pl.multiple_of(row, BLK), BLK), :]
                vc[rows, :] = source[pl.ds(pl.multiple_of(row + 128, BLK), BLK), :]
            return carry

        lax.fori_loop(start, end, one, 0)
        at = at + end - start
    return at


def chunks(place_ref, order, begin, end, ql, kc, vc, top, tot, acc, vt, sa, sb, ma, mb):
    def one_chunk(n, carry):
        rows = pl.ds(pl.multiple_of(n * CHUNK, CHUNK), CHUNK)
        last = order[n * PER_CHUNK]
        for j in range(1, PER_CHUNK):
            last = jnp.maximum(last, order[n * PER_CHUNK + j])
        vt[...] = vc[rows, :].T

        def score(i, buffer, eight):
            scores = scores_of(kc[rows, :], ql[i])
            buffer[...] = scores
            eight[...] = top_of(lambda t: scores[BLK * t : BLK * (t + 1)], PER_CHUNK)

        def run(masked):
            def finish(i, buffer, eight):
                def plain(t):
                    return buffer[BLK * t : BLK * (t + 1), :]

                if masked:
                    mine = block_of(place_ref, i)

                    def load(t):
                        return jnp.where(order[n * PER_CHUNK + t] < mine, plain(t), NEGATIVE)

                    weigh(i, load, PER_CHUNK, top_of(load, PER_CHUNK), vt[...], top, tot, acc)
                else:
                    weigh(i, plain, PER_CHUNK, eight[...], vt[...], top, tot, acc)

            score(0, sa, ma)
            score(1, sb, mb)

            def two(j, carry):
                finish(2 * j, sa, ma)
                score((2 * j + 2) % 16, sa, ma)
                finish(2 * j + 1, sb, mb)
                score((2 * j + 3) % 16, sb, mb)
                return carry

            lax.fori_loop(0, 8, two, 0)

        free = last < place_ref[0] * 16
        pl.when(free)(lambda: run(False))
        pl.when(jnp.logical_not(free))(lambda: run(True))
        return carry

    lax.fori_loop(begin, end, one_chunk, 0)


def part_kernel(done, fresh, splits, final, place_ref, vert_ref, *refs):
    sources, refs = list(refs[: sum(splits)]), refs[sum(splits) :]
    ql = refs[0]
    refs = refs[6:] if done else refs[4:]
    kc, vc, top, tot, acc = refs[:5]
    outs, refs = (refs[5:9], refs[9:]) if final else (None, refs[5:])
    bounds, order = refs[:2]
    find_bounds(vert_ref, place_ref[1], bounds)
    at = jnp.int32(0)
    for outer in done:
        at = walk(place_ref, vert_ref, bounds, order, outer, at, None, kc, vc)
    begin = at // PER_CHUNK
    for outer, count in zip(fresh, splits):
        at = walk(place_ref, vert_ref, bounds, order, outer, at, sources[:count], kc, vc)
        sources = sources[count:]
    chunks(place_ref, order, begin, at // PER_CHUNK, ql, kc, vc, top, tot, acc, *refs[2:])
    if final:
        for by in range(4):
            for block in range(4):
                i = by * 4 + block
                o = (acc[i] / jnp.sum(tot[i], axis=0, keepdims=True)).T.astype(jnp.bfloat16)
                for g in range(4):
                    outs[by][block * BLK : (block + 1) * BLK, g * 128 : (g + 1) * 128] = o[g * BLK : (g + 1) * BLK, :]


def local_kernel(
    place_ref, vert_ref, slash_ref, q0, q1, q2, q3, kv0, kv1, kv2, kv3, prev_ref, ql, top, tot, acc, kl, vl
):
    group, y = place_ref[0], place_ref[1]
    head = y
    kl[0:SLAB, :] = prev_ref[:, 0:128]
    vl[0:SLAB, :] = prev_ref[:, 128:256]
    for by, (q, kv) in enumerate(((q0, kv0), (q1, kv1), (q2, kv2), (q3, kv3))):
        slab = (y - by + 4) % 4
        rows = pl.ds(pl.multiple_of(SLAB + slab * SLAB, SLAB), SLAB)
        kl[rows, :] = kv[:, 0:128]
        vl[rows, :] = kv[:, 128:256]
        for block in range(4):
            for g in range(4):
                ql[by * 4 + block, g * BLK : (g + 1) * BLK, :] = q[block * BLK : (block + 1) * BLK, g * 128 : (g + 1) * 128]
    top[...] = jnp.full(top.shape, NEGATIVE, jnp.float32)
    tot[...] = jnp.zeros_like(tot)
    acc[...] = jnp.zeros_like(acc)
    key = lax.broadcasted_iota(jnp.int32, (BLK, 256), 0)
    row = lax.broadcasted_iota(jnp.int32, (BLK, 256), 1) % BLK

    def two(j, carry):
        for u in range(2):
            i = 2 * j + u
            block = block_of(place_ref, i)
            here = block - group * 16
            starts, valid = [here], []
            for s in range(2):
                offset = slash_ref[head, s]
                behind = block - offset
                at = jnp.minimum(rank_of(vert_ref, head, behind), NV - 1)
                valid.append((behind >= 0) & (vert_ref[head, at] != behind))
                starts.append(here - offset)
            rows = [pl.ds(pl.multiple_of(SLAB + at * BLK, BLK), BLK) for at in starts]
            keys = jnp.concatenate([kl[r, :] for r in rows] + [kl[rows[0], :]], axis=0)
            values = jnp.concatenate([vl[r, :] for r in rows] + [vl[rows[0], :]], axis=0).T
            scores = scores_of(keys, ql[i])

            def load(t):
                if t == 3:
                    return jnp.full((BLK, 256), NEGATIVE, jnp.float32)
                here = scores[BLK * t : BLK * (t + 1)]
                return jnp.where(key <= row if t == 0 else valid[t - 1], here, NEGATIVE)

            weigh(i, load, 4, top_of(load, 4), values, top, tot, acc)
        return carry

    lax.fori_loop(0, 8, two, 0)


def project(place_ref, a, weight_ref, by, rows, keep):
    head = (place_ref[1] + by) % 4
    depth = pl.ds(pl.multiple_of(head * 512, 512), 512)

    def tile(n, carry):
        columns = pl.ds(pl.multiple_of(n * 512, 512), 512)
        keep(columns, jnp.dot(a[rows, :], weight_ref[depth, columns], preferred_element_type=jnp.float32))
        return carry

    lax.fori_loop(0, 8, tile, 0)


def first_piece_kernel(place_ref, a, weight_ref, total_ref):
    def keep(columns, product):
        total_ref[:, columns] = product

    project(place_ref, a, weight_ref, 0, slice(None), keep)


def next_piece_kernel(by, place_ref, a, weight_ref, total_in, total_ref):
    def keep(columns, product):
        total_ref[:, columns] = total_ref[:, columns] + product

    project(place_ref, a, weight_ref, by, slice(None), keep)


def last_piece_kernel(by, mine, place_ref, a, weight_ref, total_ref, out_ref):
    core = place_ref[4]
    half = core if mine else 1 - core
    rows = pl.ds(pl.multiple_of(half * 128, 128), 128)

    def keep(columns, product):
        out_ref[:, columns] = (total_ref[rows, columns] + product).astype(out_ref.dtype)

    project(place_ref, a, weight_ref, by, rows, keep)


SMEM = pl.BlockSpec(memory_space=pltpu.SMEM)
VMEM = pl.BlockSpec(memory_space=pltpu.VMEM)


def bf16(*shape):
    return jax.ShapeDtypeStruct(shape, jnp.bfloat16)


def f32(*shape):
    return jax.ShapeDtypeStruct(shape, jnp.float32)


STATE = [f32(16, 8, 256), f32(16, 8, 256), f32(16, 128, 256)]
PACKED = [bf16(NV * BLK, 128)] * 2
WORK = [
    pltpu.SMEM((17,), jnp.int32),
    pltpu.SMEM((NV,), jnp.int32),
    pltpu.VMEM((128, CHUNK), jnp.bfloat16),
    pltpu.VMEM((CHUNK, 256), jnp.float32),
    pltpu.VMEM((CHUNK, 256), jnp.float32),
    pltpu.VMEM((8, 256), jnp.float32),
    pltpu.VMEM((8, 256), jnp.float32),
]


def call(kernel, outs, scalars, arrays, flops, limit, scratch=(), aliases=None):
    return pl.pallas_call(
        kernel,
        out_shape=outs,
        in_specs=[SMEM] * len(scalars) + [VMEM] * len(arrays),
        out_specs=[VMEM] * len(outs),
        scratch_shapes=list(scratch),
        input_output_aliases=aliases or {},
        compiler_params=pltpu.CompilerParams(vmem_limit_bytes=limit * MIB),
        cost_estimate=pl.CostEstimate(flops=int(flops), bytes_accessed=10**6, transcendentals=0),
    )(*scalars, *arrays)


def layer(queries, keys, values, vertical, slash, out_weight):
    x, z, y, c = (lax.axis_index(a) for a in ALL)
    place = jnp.stack([x * 4 + z, y, jnp.where(c == 0, x, z), jnp.where(c == 0, z, x), c]).astype(jnp.int32)
    kv = call(kv_kernel, [bf16(SLAB, 256)] * 4, [place], [keys, values], 1e6, 4)
    kv = [kv[0]] + [along_y(kv[by], by) for by in (1, 2, 3)]
    q = call(q_kernel, [bf16(SLAB, 512)] * 4, [place], [queries], 1e6, 4)
    q = [q[0]] + [along_y(q[by], by) for by in (1, 2, 3)]
    own, last = call(slots_kernel, [bf16(1024, 128), bf16(SLAB, 256)], [place, vertical], kv, 1e6, 4)
    hops = [first_hop(own, by) for by in (1, 2, 3)]
    prev = to_next_group(last)
    near = jnp.concatenate([own] + hops, axis=0)
    plus, minus = second_hop(near, 1), second_hop(near, 3)
    beyond = [second_hop(plus[:2048], 1), second_hop(minus[2048:], 3)]
    ql, *state = call(
        local_kernel, [bf16(16, 256, 128)] + STATE, [place, vertical, slash], [*q, *kv, prev], 3e9, 6,
        [pltpu.VMEM((5 * SLAB, 128), jnp.bfloat16)] * 2,
    )
    state = call(
        functools.partial(part_kernel, (), (0,), (1,), False), PACKED + STATE, [place, vertical],
        [near, ql, *state], 5e9, 8, WORK, {4 + n: 2 + n for n in range(3)},
    )
    state = call(
        functools.partial(part_kernel, (0,), (1, 3), (1, 1), False), PACKED + STATE, [place, vertical],
        [plus, minus, ql, *state], 1e10, 8, WORK, {5 + n: n for n in range(5)},
    )
    state = call(
        functools.partial(part_kernel, (0, 1, 3), (2,), (2,), True), PACKED + STATE + [bf16(SLAB, 512)] * 4,
        [place, vertical], [*beyond, ql, *state], 5e9, 8, WORK, {5 + n: n for n in range(5)},
    )
    attention = state[5:]
    back = [attention[0]] + [along_y(attention[by], -by) for by in (1, 2, 3)]
    total = call(first_piece_kernel, [f32(SLAB, 4096)], [place], [back[0], out_weight], 1e9, 6)[0]
    for by in (1, 3):
        total = call(
            functools.partial(next_piece_kernel, by), [f32(SLAB, 4096)], [place],
            [back[by], out_weight, total], 1e9, 6, (), {3: 0},
        )[0]
    theirs, mine = (
        call(
            functools.partial(last_piece_kernel, 2, own), [out], [place],
            [back[2], out_weight, total], 1e9, 6,
        )[0]
        for own, out in ((False, bf16(128, 4096)), (True, f32(128, 4096)))
    )
    other = to_partner(theirs)
    return (mine + other.astype(jnp.float32)).astype(jnp.bfloat16)


def solution(mesh):
    torus = Mesh(mesh.devices.reshape(4, 4, 4, 2), ALL)
    rows = ("x", "z", "y")
    placed = (P(rows, "c"), P(rows, "c"), P(rows, "c"), P("c", None), P("c", None), P("c", None))
    return jax.shard_map(layer, mesh=torus, in_specs=placed, out_specs=P(ALL, None), check_vma=False)
```

profile of v0, /device:TPU:97, one launch (start us, length us, event | category | flops | bytes accessed | tf_op | source)
XLA Modules:
  0.0 126.1 jit_solution(9758719534318726599)
XLA Ops:
  0.0 0.1 stack.23.place_ref
  0.1 1.0 copy-done.1
  1.1 0.9 copy-done.2
  2.1 0.6 shard_map.64
  2.7 1.4 %collective-permute-start = (bf16[256,256]{1,0:T(8,128)(2,1)S(1)}, bf16[256,256]{1,0:T(8,128)(2,1)S(1)}, u32[]{:S(2)}, u32[]{:S(2)}) collective-permute-start(bf16[256,256]{1,0:T(8,128)(2,1)S(1)} %get-tuple-element.34), channel_id=1, source_target_pairs={{0,2},{1,3},{2,4},{3,5},{4,6},{5,7},{6,0},{7,1},{8,10},{9,11},{10,... | collective-permute-start | bytes 393224 | tf_op jit(solution)/shard_map/ppermute | solution.py:29
  4.1 2.6 %collective-permute-start.1 = (bf16[256,256]{1,0:T(8,128)(2,1)S(1)}, bf16[256,256]{1,0:T(8,128)(2,1)S(1)}, u32[]{:S(2)}, u32[]{:S(2)}) collective-permute-start(bf16[256,256]{1,0:T(8,128)(2,1)S(1)} %get-tuple-element.35), channel_id=1, source_target_pairs={{0,4},{1,5},{2,6},{3,7},{4,0},{5,1},{6,2},{7,3},{8,12},{9,13},{10,... | collective-permute-start | bytes 393224 | tf_op jit(solution)/shard_map/ppermute | solution.py:29
  6.7 1.1 collective-permute-start.2
  7.8 0.7 collective-permute-done.kv1
  8.5 3.9 %collective-permute-done.1.kv2 = bf16[256,256]{1,0:T(8,128)(2,1)S(1)} collective-permute-done((bf16[256,256]{1,0:T(8,128)(2,1)S(1)}, bf16[256,256]{1,0:T(8,128)(2,1)S(1)}, u32[]{:S(2)}, u32[]{:S(2)}) %collective-permute-start.1) | collective-permute-done | bytes 131104 | tf_op jit(solution)/shard_map/ppermute | solution.py:29
  12.4 0.7 copy-done.5
  13.1 0.9 shard_map.65
  14.0 0.1 collective-permute-start.3
  14.1 1.9 %collective-permute-start.4 = (bf16[1024,128]{1,0:T(8,128)(2,1)S(1)}, bf16[1024,128]{1,0:T(8,128)(2,1)S(1)}, u32[]{:S(2)}, u32[]{:S(2)}) collective-permute-start(bf16[1024,128]{1,0:T(8,128)(2,1)S(1)} %get-tuple-element.37), channel_id=1, source_target_pairs={{0,64},{1,17},{2,66},{3,19},{4,68},{5,21},{6,70},{7,23},{8,72},{9,... | collective-permute-start | bytes 786440 | tf_op jit(solution)/shard_map/ppermute | solution.py:29
  16.0 0.7 constant_dynamic-update-slice_fusion.3
  16.7 3.6 %collective-permute-start.13 = (bf16[256,256]{1,0:T(8,128)(2,1)S(1)}, bf16[256,256]{1,0:T(8,128)(2,1)S(1)}, u32[]{:S(2)}, u32[]{:S(2)}) collective-permute-start(bf16[256,256]{1,0:T(8,128)(2,1)S(1)} %get-tuple-element.42), channel_id=1, source_target_pairs={{0,8},{1,9},{2,10},{3,11},{4,12},{5,13},{6,14},{7,15},{8,16},{9,17... | collective-permute-start | bytes 393224 | tf_op jit(solution)/shard_map/ppermute | solution.py:29
  20.3 0.7 constant_dynamic-update-slice_fusion.2
  21.1 0.7 constant_dynamic-update-slice_fusion.1
  21.8 2.2 %collective-permute-done.5 = bf16[1024,128]{1,0:T(8,128)(2,1)S(1)} collective-permute-done((bf16[1024,128]{1,0:T(8,128)(2,1)S(1)}, bf16[1024,128]{1,0:T(8,128)(2,1)S(1)}, u32[]{:S(2)}, u32[]{:S(2)}) %collective-permute-start.5) | collective-permute-done | bytes 262176 | tf_op jit(solution)/shard_map/ppermute | solution.py:29
  24.0 0.7 constant_dynamic-update-slice_fusion.refs_0_
  24.7 1.1 collective-permute-start.6
  25.8 1.6 %collective-permute-start.8 = (bf16[4096,128]{1,0:T(8,128)(2,1)}, bf16[4096,128]{1,0:T(8,128)(2,1)S(1)}, u32[]{:S(2)}, u32[]{:S(2)}) collective-permute-start(bf16[4096,128]{1,0:T(8,128)(2,1)} %constant_dynamic-update-slice_fusion.refs_0_), channel_id=1, source_target_pairs={{0,24},{1,97},{2,26},{3,99},{4,28},{5,101},{6,30},{7,103},{8,0},{9... | collective-permute-start | bytes 3145736 | tf_op jit(solution)/shard_map/ppermute | solution.py:29
  27.4 1.5 %shard_map.66 = (bf16[256,512]{1,0:T(8,128)(2,1)S(1)}, bf16[256,512]{1,0:T(8,128)(2,1)}, bf16[256,512]{1,0:T(8,128)(2,1)}, bf16[256,512]{1,0:T(8,128)(2,1)}) custom-call(s32[5]{0:T(128)S(1)} %stack.23.place_ref, bf16[256,2048]{1,0:T(8,128)(2,1)S(1)} %copy-done), custom_call_target="tpu_custom_call" | custom-call | flops 1000000 | bytes 1000000 | tf_op jit(solution)/shard_map/pallas_call | solution.py:357
  28.9 0.7 copy-done.7
  29.6 1.2 collective-permute-start.10
  30.8 2.2 %collective-permute-start.11 = (bf16[256,512]{1,0:T(8,128)(2,1)}, bf16[256,512]{1,0:T(8,128)(2,1)S(1)}, u32[]{:S(2)}, u32[]{:S(2)}) collective-permute-start(bf16[256,512]{1,0:T(8,128)(2,1)} %get-tuple-element.40), channel_id=1, source_target_pairs={{0,4},{1,5},{2,6},{3,7},{4,0},{5,1},{6,2},{7,3},{8,12},{9,13},{10,... | collective-permute-start | bytes 786440 | tf_op jit(solution)/shard_map/ppermute | solution.py:29
  33.0 0.7 copy-done.9
  33.7 0.5 collective-permute-start.12
  34.2 0.1 copy.22.slash_ref
  34.3 2.2 %collective-permute-done.10.q1 = bf16[256,512]{1,0:T(8,128)(2,1)S(1)} collective-permute-done((bf16[256,512]{1,0:T(8,128)(2,1)}, bf16[256,512]{1,0:T(8,128)(2,1)S(1)}, u32[]{:S(2)}, u32[]{:S(2)}) %collective-permute-start.10) | collective-permute-done | bytes 262176 | tf_op jit(solution)/shard_map/ppermute | solution.py:29
  36.6 4.3 %collective-permute-done.11.q2 = bf16[256,512]{1,0:T(8,128)(2,1)S(1)} collective-permute-done((bf16[256,512]{1,0:T(8,128)(2,1)}, bf16[256,512]{1,0:T(8,128)(2,1)S(1)}, u32[]{:S(2)}, u32[]{:S(2)}) %collective-permute-start.11) | collective-permute-done | bytes 262176 | tf_op jit(solution)/shard_map/ppermute | solution.py:29
  40.8 0.9 copy-done.4
  41.7 0.9 copy-done.8
  42.7 0.9 copy-done.10
  43.6 6.5 %shard_map.67 = (bf16[16,256,128]{2,1,0:T(8,128)(2,1)S(1)}, f32[16,8,256]{2,1,0:T(8,128)S(1)}, f32[16,8,256]{2,1,0:T(8,128)S(1)}, f32[16,128,256]{2,1,0:T(8,128)S(1)}) custom-call(s32[5]{0:T(128)S(1)} %stack.23.place_ref, s32[4,64]{1,0:T(4,128)S(1)} %copy-done.6, s32[4,2]{1,0:T(4,128)S(1)} %copy.22.slash_ref, bf16[256,512]{1,0:T(8,128)(2,1)S(1)} %copy-done.8, ...), custom_call_target="tpu_custom_call" | custom-call | flops 3000000000 | bytes 1000000 | tf_op jit(solution)/shard_map/pallas_call | solution.py:357
  50.1 16.5 %shard_map.68 = (bf16[4096,128]{1,0:T(8,128)(2,1)S(1)}, bf16[4096,128]{1,0:T(8,128)(2,1)S(1)}, f32[16,8,256]{2,1,0:T(8,128)S(1)}, f32[16,8,256]{2,1,0:T(8,128)S(1)}, f32[16,128,256]{2,1,0:T(8,128)S(1)}) custom-call(s32[5]{0:T(128)S(1)} %stack.23.place_ref, s32[4,64]{1,0:T(4,128)S(1)} %copy-done.6, ...), custom_call_target="tpu_custom_call", output_to_operand_aliasing={{2}: (4, {}), {3}: (5, {}), {4}: (6, {})} | custom-call | flops 5000000000 | bytes 1000000 | tf_op jit(solution)/shard_map/pallas_call | solution.py:357
  66.8 2.7 %collective-permute-start.9 = (bf16[2048,128]{1,0:T(8,128)(2,1)S(1)}, bf16[2048,128]{1,0:T(8,128)(2,1)S(1)}, u32[]{:S(2)}, u32[]{:S(2)}) collective-permute-start(bf16[2048,128]{1,0:T(8,128)(2,1)S(1)} %slice.9), channel_id=1, source_target_pairs={{0,24},{1,97},{2,26},{3,99},{4,28},{5,101},{6,30},{7,103},{8,0},{9... | collective-permute-start | bytes 1572872 | tf_op jit(solution)/shard_map/ppermute | solution.py:29
  69.6 10.1 %shard_map.69 = (bf16[4096,128]{1,0:T(8,128)(2,1)S(1)}, bf16[4096,128]{1,0:T(8,128)(2,1)S(1)}, f32[16,8,256]{2,1,0:T(8,128)S(1)}, f32[16,8,256]{2,1,0:T(8,128)S(1)}, f32[16,128,256]{2,1,0:T(8,128)S(1)}) custom-call(s32[5]{0:T(128)S(1)} %stack.23.place_ref, ...), custom_call_target="tpu_custom_call", output_to_operand_aliasing={{0}: (5, {}), {1}: (6, {}), {2}: (7, {}), {3}: (8, {}), {4}... | custom-call | flops 10000000000 | bytes 1000000 | tf_op jit(solution)/shard_map/pallas_call | solution.py:357
  79.7 10.1 %shard_map.70 = (bf16[4096,128]{1,0:T(8,128)(2,1)S(1)}, bf16[4096,128]{1,0:T(8,128)(2,1)S(1)}, f32[16,8,256]{2,1,0:T(8,128)S(1)}, f32[16,8,256]{2,1,0:T(8,128)S(...) custom-call(s32[5]{0:T(128)S(1)} %stack.23.place_ref, ...), custom_call_target="tpu_custom_call", output_to_operand_aliasing={{0}: (5, {}), {1}: (6, {}), {2}: (7, {}), {3}: (8, {}), {4}... | custom-call | flops 5000000000 | bytes 1000000 | tf_op jit(solution)/shard_map/pallas_call | solution.py:357
  89.8 2.0 %collective-permute-start.16 = (bf16[256,512]{1,0:T(8,128)(2,1)S(1)}, bf16[256,512]{1,0:T(8,128)(2,1)S(1)}, u32[]{:S(2)}, u32[]{:S(2)}) collective-permute-start(bf16[256,512]{1,0:T(8,128)(2,1)S(1)} %get-tuple-element.59), channel_id=1, source_target_pairs={{0,6},{1,7},{2,0},{3,1},{4,2},{5,3},{6,4},{7,5},{8,14},{9,15},{10,... | collective-permute-start | bytes 786440 | tf_op jit(solution)/shard_map/ppermute | solution.py:29
  91.7 1.3 %collective-permute-start.14 = (bf16[256,512]{1,0:T(8,128)(2,1)S(1)}, bf16[256,512]{1,0:T(8,128)(2,1)S(1)}, u32[]{:S(2)}, u32[]{:S(2)}) collective-permute-start(bf16[256,512]{1,0:T(8,128)(2,1)S(1)} %get-tuple-element.57), channel_id=1, source_target_pairs={{0,4},{1,5},{2,6},{3,7},{4,0},{5,1},{6,2},{7,3},{8,12},{9,13},{10,... | collective-permute-start | bytes 786440 | tf_op jit(solution)/shard_map/ppermute | solution.py:29
  93.0 3.0 %shard_map.71.total_in = f32[256,4096]{1,0:T(8,128)S(1)} custom-call(s32[5]{0:T(128)S(1)} %stack.23.place_ref, bf16[256,512]{1,0:T(8,128)(2,1)S(1)} %get-tuple-element.60.a, bf16[2048,4096]{1,0:T(8,128)(2,1)S(1)} %bitcast.6), custom_call_target="tpu_custom_call" | custom-call | flops 1000000000 | bytes 1000000 | tf_op jit(solution)/shard_map/pallas_call | solution.py:357
  96.0 3.0 %shard_map.72.total_in = f32[256,4096]{1,0:T(8,128)S(1)} custom-call(s32[5]{0:T(128)S(1)} %stack.23.place_ref, bf16[256,512]{1,0:T(8,128)(2,1)S(1)} %collective-permute-done.16.a, bf16[2048,4096]{1,0:T(8,128)(2,1)S(1)} %bitcast.6, f32[256,4096]{1,0:T(8,128)S(1)} %shard_map.71.total_in), custom_call_target="tpu_custom_call", output_to_operand_aliasing={{}: (3, {})} | custom-call | flops 1000000000 | bytes 1000000 | tf_op jit(solution)/shard_map/pallas_call | solution.py:357
  99.0 1.9 %collective-permute-done.15.a = bf16[256,512]{1,0:T(8,128)(2,1)S(1)} collective-permute-done((bf16[256,512]{1,0:T(8,128)(2,1)S(1)}, bf16[256,512]{1,0:T(8,128)(2,1)S(1)}, u32[]{:S(2)}, u32[]{:S(2)}) %collective-permute-start.15) | collective-permute-done | bytes 262176 | tf_op jit(solution)/shard_map/ppermute | solution.py:29
  101.0 3.0 %shard_map.73.total_ref = f32[256,4096]{1,0:T(8,128)S(1)} custom-call(s32[5]{0:T(128)S(1)} %stack.23.place_ref, bf16[256,512]{1,0:T(8,128)(2,1)S(1)} %collective-permute-done.15.a, bf16[2048,4096]{1,0:T(8,128)(2,1)S(1)} %bitcast.6, f32[256,4096]{1,0:T(8,128)S(1)} %shard_map.72.total_in), custom_call_target="tpu_custom_call", output_to_operand_aliasing={{}: (3, {})} | custom-call | flops 1000000000 | bytes 1000000 | tf_op jit(solution)/shard_map/pallas_call | solution.py:357
  104.0 2.5 %shard_map.75 = bf16[128,4096]{1,0:T(8,128)(2,1)S(1)} custom-call(s32[5]{0:T(128)S(1)} %stack.23.place_ref, bf16[256,512]{1,0:T(8,128)(2,1)S(1)} %collective-permute-done.14.a, bf16[2048,4096]{1,0:T(8,128)(2,1)S(1)} %bitcast.6, f32[256,4096]{1,0:T(8,128)S(1)} %shard_map.73.total_ref), custom_call_target="tpu_custom_call" | custom-call | flops 1000000000 | bytes 1000000 | tf_op jit(solution)/shard_map/pallas_call | solution.py:357
  106.4 16.0 %collective-permute-start.17 = (bf16[128,4096]{1,0:T(8,128)(2,1)S(1)}, bf16[128,4096]{1,0:T(8,128)(2,1)S(1)}, u32[]{:S(2)}, u32[]{:S(2)}) collective-permute-start(bf16[128,4096]{1,0:T(8,128)(2,1)S(1)} %shard_map.75), channel_id=1, source_target_pairs={{0,1},{1,0},{2,3},{3,2},{4,5},{5,4},{6,7},{7,6},{8,9},{9,8},{10,11... | collective-permute-start | bytes 3145736 | tf_op jit(solution)/shard_map/ppermute | solution.py:29
  122.4 2.4 %shard_map.74 = f32[128,4096]{1,0:T(8,128)S(1)} custom-call(s32[5]{0:T(128)S(1)} %stack.23.place_ref, bf16[256,512]{1,0:T(8,128)(2,1)S(1)} %collective-permute-done.14.a, bf16[2048,4096]{1,0:T(8,128)(2,1)S(1)} %bitcast.6, f32[256,4096]{1,0:T(8,128)S(1)} %shard_map.73.total_ref), custom_call_target="tpu_custom_call" | custom-call | flops 1000000000 | bytes 1000000 | tf_op jit(solution)/shard_map/pallas_call | solution.py:357
  124.9 1.2 add_convert_fusion
  (42 shorter events, 0.2 us)
Async XLA Ops:
  0.0 27.4 %copy-start = (bf16[256,2048]{1,0:T(8,128)(2,1)S(1)}, bf16[256,2048]{1,0:T(8,128)(2,1)}, u32[]{:S(2)}) copy-start(bf16[256,2048]{1,0:T(8,128)(2,1)} %queries_ref.1) | copy-start | bytes 3145732
  0.1 1.0 copy-start.1
  1.1 0.9 copy-start.2
  2.7 5.8 %collective-permute-start = (bf16[256,256]{1,0:T(8,128)(2,1)S(1)}, bf16[256,256]{1,0:T(8,128)(2,1)S(1)}, u32[]{:S(2)}, u32[]{:S(2)}) collective-permute-start(bf16[256,256]{1,0:T(8,128)(2,1)S(1)} %get-tuple-element.34), channel_id=1, source_target_pairs={{0,2},{1,3},{2,4},{3,5},{4,6},{5,7},{6,0},{7,1},{8,10},{9,11},{10,... | collective-permute-start | bytes 393224 | tf_op jit(solution)/shard_map/ppermute | solution.py:29
  4.1 8.3 %collective-permute-start.1 = (bf16[256,256]{1,0:T(8,128)(2,1)S(1)}, bf16[256,256]{1,0:T(8,128)(2,1)S(1)}, u32[]{:S(2)}, u32[]{:S(2)}) collective-permute-start(bf16[256,256]{1,0:T(8,128)(2,1)S(1)} %get-tuple-element.35), channel_id=1, source_target_pairs={{0,4},{1,5},{2,6},{3,7},{4,0},{5,1},{6,2},{7,3},{8,12},{9,13},{10,... | collective-permute-start | bytes 393224 | tf_op jit(solution)/shard_map/ppermute | solution.py:29
  6.7 5.7 %collective-permute-start.2 = (bf16[256,256]{1,0:T(8,128)(2,1)S(1)}, bf16[256,256]{1,0:T(8,128)(2,1)S(1)}, u32[]{:S(2)}, u32[]{:S(2)}) collective-permute-start(bf16[256,256]{1,0:T(8,128)(2,1)S(1)} %get-tuple-element.36), channel_id=1, source_target_pairs={{0,6},{1,7},{2,0},{3,1},{4,2},{5,3},{6,4},{7,5},{8,14},{9,15},{10,... | collective-permute-start | bytes 393224 | tf_op jit(solution)/shard_map/ppermute | solution.py:29
  12.4 1.7 %copy-start.3 = (bf16[256,256]{1,0:T(8,128)(2,1)}, bf16[256,256]{1,0:T(8,128)(2,1)S(1)}, u32[]{:S(2)}) copy-start(bf16[256,256]{1,0:T(8,128)(2,1)S(1)} %collective-permute-done.2.kv3) | copy-start | bytes 393220
  12.4 0.7 copy-start.5
  13.1 21.1 %copy-start.11 = (s32[4,2]{0,1:T(2,128)S(1)}, s32[4,2]{0,1:T(2,128)}, u32[]{:S(2)}) copy-start(s32[4,2]{0,1:T(2,128)} %param.10) | copy-start | bytes 100
  13.1 27.7 %copy-start.6 = (s32[4,64]{1,0:T(4,128)S(1)}, s32[4,64]{1,0:T(4,128)}, u32[]{:S(2)}) copy-start(s32[4,64]{1,0:T(4,128)} %vert_ref.9) | copy-start | bytes 3076
  14.0 6.3 %collective-permute-start.3 = (bf16[1024,128]{1,0:T(8,128)(2,1)S(1)}, bf16[1024,128]{1,0:T(8,128)(2,1)S(1)}, u32[]{:S(2)}, u32[]{:S(2)}) collective-permute-start(bf16[1024,128]{1,0:T(8,128)(2,1)S(1)} %get-tuple-element.37), channel_id=1, source_target_pairs={{0,32},{1,9},{2,34},{3,11},{4,36},{5,13},{6,38},{7,15},{8,40},{9,1... | collective-permute-start | bytes 786440 | tf_op jit(solution)/shard_map/ppermute | solution.py:29
  14.1 6.9 %collective-permute-start.4 = (bf16[1024,128]{1,0:T(8,128)(2,1)S(1)}, bf16[1024,128]{1,0:T(8,128)(2,1)S(1)}, u32[]{:S(2)}, u32[]{:S(2)}) collective-permute-start(bf16[1024,128]{1,0:T(8,128)(2,1)S(1)} %get-tuple-element.37), channel_id=1, source_target_pairs={{0,64},{1,17},{2,66},{3,19},{4,68},{5,21},{6,70},{7,23},{8,72},{9,... | collective-permute-start | bytes 786440 | tf_op jit(solution)/shard_map/ppermute | solution.py:29
  16.0 8.0 %collective-permute-start.5 = (bf16[1024,128]{1,0:T(8,128)(2,1)S(1)}, bf16[1024,128]{1,0:T(8,128)(2,1)S(1)}, u32[]{:S(2)}, u32[]{:S(2)}) collective-permute-start(bf16[1024,128]{1,0:T(8,128)(2,1)S(1)} %get-tuple-element.37), channel_id=1, source_target_pairs={{0,96},{1,25},{2,98},{3,27},{4,100},{5,29},{6,102},{7,31},{8,104},... | collective-permute-start | bytes 786440 | tf_op jit(solution)/shard_map/ppermute | solution.py:29
  16.7 16.3 %collective-permute-start.13 = (bf16[256,256]{1,0:T(8,128)(2,1)S(1)}, bf16[256,256]{1,0:T(8,128)(2,1)S(1)}, u32[]{:S(2)}, u32[]{:S(2)}) collective-permute-start(bf16[256,256]{1,0:T(8,128)(2,1)S(1)} %get-tuple-element.42), channel_id=1, source_target_pairs={{0,8},{1,9},{2,10},{3,11},{4,12},{5,13},{6,14},{7,15},{8,16},{9,17... | collective-permute-start | bytes 393224 | tf_op jit(solution)/shard_map/ppermute | solution.py:29
  24.7 41.9 %collective-permute-start.6 = (bf16[4096,128]{1,0:T(8,128)(2,1)}, bf16[4096,128]{1,0:T(8,128)(2,1)S(1)}, u32[]{:S(2)}, u32[]{:S(2)}) collective-permute-start(bf16[4096,128]{1,0:T(8,128)(2,1)} %constant_dynamic-update-slice_fusion.refs_0_), channel_id=1, source_target_pairs={{0,8},{1,33},{2,10},{3,35},{4,12},{5,37},{6,14},{7,39},{8,16},{9,4... | collective-permute-start | bytes 3145736 | tf_op jit(solution)/shard_map/ppermute | solution.py:29
  25.8 41.0 %collective-permute-start.8 = (bf16[4096,128]{1,0:T(8,128)(2,1)}, bf16[4096,128]{1,0:T(8,128)(2,1)S(1)}, u32[]{:S(2)}, u32[]{:S(2)}) collective-permute-start(bf16[4096,128]{1,0:T(8,128)(2,1)} %constant_dynamic-update-slice_fusion.refs_0_), channel_id=1, source_target_pairs={{0,24},{1,97},{2,26},{3,99},{4,28},{5,101},{6,30},{7,103},{8,0},{9... | collective-permute-start | bytes 3145736 | tf_op jit(solution)/shard_map/ppermute | solution.py:29
  28.9 0.7 copy-start.7
  29.6 6.9 %collective-permute-start.10 = (bf16[256,512]{1,0:T(8,128)(2,1)}, bf16[256,512]{1,0:T(8,128)(2,1)S(1)}, u32[]{:S(2)}, u32[]{:S(2)}) collective-permute-start(bf16[256,512]{1,0:T(8,128)(2,1)} %get-tuple-element.39), channel_id=1, source_target_pairs={{0,2},{1,3},{2,4},{3,5},{4,6},{5,7},{6,0},{7,1},{8,10},{9,11},{10,... | collective-permute-start | bytes 786440 | tf_op jit(solution)/shard_map/ppermute | solution.py:29
  30.8 10.0 %collective-permute-start.11 = (bf16[256,512]{1,0:T(8,128)(2,1)}, bf16[256,512]{1,0:T(8,128)(2,1)S(1)}, u32[]{:S(2)}, u32[]{:S(2)}) collective-permute-start(bf16[256,512]{1,0:T(8,128)(2,1)} %get-tuple-element.40), channel_id=1, source_target_pairs={{0,4},{1,5},{2,6},{3,7},{4,0},{5,1},{6,2},{7,3},{8,12},{9,13},{10,... | collective-permute-start | bytes 786440 | tf_op jit(solution)/shard_map/ppermute | solution.py:29
  33.0 0.7 copy-start.9
  33.7 7.2 %collective-permute-start.12 = (bf16[256,512]{1,0:T(8,128)(2,1)}, bf16[256,512]{1,0:T(8,128)(2,1)S(1)}, u32[]{:S(2)}, u32[]{:S(2)}) collective-permute-start(bf16[256,512]{1,0:T(8,128)(2,1)} %get-tuple-element.41), channel_id=1, source_target_pairs={{0,6},{1,7},{2,0},{3,1},{4,2},{5,3},{6,4},{7,5},{8,14},{9,15},{10,... | collective-permute-start | bytes 786440 | tf_op jit(solution)/shard_map/ppermute | solution.py:29
  40.8 0.9 copy-start.4
  41.7 0.9 copy-start.8
  42.7 0.9 copy-start.10
  66.7 13.0 %collective-permute-start.7 = (bf16[2048,128]{1,0:T(8,128)(2,1)S(1)}, bf16[2048,128]{1,0:T(8,128)(2,1)S(1)}, u32[]{:S(2)}, u32[]{:S(2)}) collective-permute-start(bf16[2048,128]{1,0:T(8,128)(2,1)S(1)} %slice.8), channel_id=1, source_target_pairs={{0,8},{1,33},{2,10},{3,35},{4,12},{5,37},{6,14},{7,39},{8,16},{9,4... | collective-permute-start | bytes 1572872 | tf_op jit(solution)/shard_map/ppermute | solution.py:29
  66.8 12.8 %collective-permute-start.9 = (bf16[2048,128]{1,0:T(8,128)(2,1)S(1)}, bf16[2048,128]{1,0:T(8,128)(2,1)S(1)}, u32[]{:S(2)}, u32[]{:S(2)}) collective-permute-start(bf16[2048,128]{1,0:T(8,128)(2,1)S(1)} %slice.9), channel_id=1, source_target_pairs={{0,24},{1,97},{2,26},{3,99},{4,28},{5,101},{6,30},{7,103},{8,0},{9... | collective-permute-start | bytes 1572872 | tf_op jit(solution)/shard_map/ppermute | solution.py:29
  69.6 23.4 %slice-start = ((s8[16777216]{0:T(1024)(128)(4,1)}), s8[4194304]{0:T(1024)(128)(4,1)S(1)}, s32[]{:S(2)}) async-start(s8[16777216]{0:T(1024)(128)(4,1)} %bitcast.5), calls=%async_computation | async-start | bytes 8388608
  69.6 23.4 %slice-start.1 = ((s8[16777216]{0:T(1024)(128)(4,1)}), s8[4194304]{0:T(1024)(128)(4,1)S(1)}, s32[]{:S(2)}) async-start(s8[16777216]{0:T(1024)(128)(4,1)} %bitcast.5), calls=%async_computation.1 | async-start | bytes 8388608
  69.6 23.4 %slice-start.2 = ((s8[16777216]{0:T(1024)(128)(4,1)}), s8[4194304]{0:T(1024)(128)(4,1)S(1)}, s32[]{:S(2)}) async-start(s8[16777216]{0:T(1024)(128)(4,1)} %bitcast.5), calls=%async_computation.2 | async-start | bytes 8388608
  79.7 13.3 %slice-start.3 = ((s8[16777216]{0:T(1024)(128)(4,1)}), s8[4194304]{0:T(1024)(128)(4,1)S(1)}, s32[]{:S(2)}) async-start(s8[16777216]{0:T(1024)(128)(4,1)} %bitcast.5), calls=%async_computation.3 | async-start | bytes 8388608
  89.8 6.3 %collective-permute-start.16 = (bf16[256,512]{1,0:T(8,128)(2,1)S(1)}, bf16[256,512]{1,0:T(8,128)(2,1)S(1)}, u32[]{:S(2)}, u32[]{:S(2)}) collective-permute-start(bf16[256,512]{1,0:T(8,128)(2,1)S(1)} %get-tuple-element.59), channel_id=1, source_target_pairs={{0,6},{1,7},{2,0},{3,1},{4,2},{5,3},{6,4},{7,5},{8,14},{9,15},{10,... | collective-permute-start | bytes 786440 | tf_op jit(solution)/shard_map/ppermute | solution.py:29
  91.7 9.2 %collective-permute-start.15 = (bf16[256,512]{1,0:T(8,128)(2,1)S(1)}, bf16[256,512]{1,0:T(8,128)(2,1)S(1)}, u32[]{:S(2)}, u32[]{:S(2)}) collective-permute-start(bf16[256,512]{1,0:T(8,128)(2,1)S(1)} %get-tuple-element.58), channel_id=1, source_target_pairs={{0,2},{1,3},{2,4},{3,5},{4,6},{5,7},{6,0},{7,1},{8,10},{9,11},{10,... | collective-permute-start | bytes 786440 | tf_op jit(solution)/shard_map/ppermute | solution.py:29
  91.7 12.2 %collective-permute-start.14 = (bf16[256,512]{1,0:T(8,128)(2,1)S(1)}, bf16[256,512]{1,0:T(8,128)(2,1)S(1)}, u32[]{:S(2)}, u32[]{:S(2)}) collective-permute-start(bf16[256,512]{1,0:T(8,128)(2,1)S(1)} %get-tuple-element.57), channel_id=1, source_target_pairs={{0,4},{1,5},{2,6},{3,7},{4,0},{5,1},{6,2},{7,3},{8,12},{9,13},{10,... | collective-permute-start | bytes 786440 | tf_op jit(solution)/shard_map/ppermute | solution.py:29
  106.4 18.4 %collective-permute-start.17 = (bf16[128,4096]{1,0:T(8,128)(2,1)S(1)}, bf16[128,4096]{1,0:T(8,128)(2,1)S(1)}, u32[]{:S(2)}, u32[]{:S(2)}) collective-permute-start(bf16[128,4096]{1,0:T(8,128)(2,1)S(1)} %shard_map.75), channel_id=1, source_target_pairs={{0,1},{1,0},{2,3},{3,2},{4,5},{5,4},{6,7},{7,6},{8,9},{9,8},{10,11... | collective-permute-start | bytes 3145736 | tf_op jit(solution)/shard_map/ppermute | solution.py:29
where the time goes:
time: 126 us
  Pallas kernels  60.1 us (48%)
  starting transfers between devices  39.2 us (31%)
  waiting for transfers between devices  15.4 us (12%)
  local copies, waits for them, and re-layouts  9.93 us (8%)
    pallas_call x12, Pallas kernels, call(): pl.pallas_call(kernel, out_shape=outs, in_specs=[SMEM] * len(scalars) + [...  60.1 us
    ppermute x18, starting transfers between devices, moved(): return lax.ppermute(value, ALL, pairs)  39.2 us
    ppermute x18, waiting for transfers between devices, moved(): return lax.ppermute(value, ALL, pairs)  15.4 us
    unnamed x36, local copies, waits for them, and re-layouts  9.05 us
  transfers between devices with their start and end apart: 18, of which 6 were waited for; matrix products, arithmetic and copies ran while one was open for 2% of the time, Pallas kernels for 36%

commit v1 on v0

--- a/solution.py
+++ b/solution.py
@@ -64,7 +64,7 @@
         out_refs[by][:, 128:256] = values_ref[:, lanes]
 
 
-def q_kernel(place_ref, queries_ref, *out_refs):
+def q_kernel(place_ref, vert_ref, queries_ref, *out_refs):
     y = place_ref[1]
     for by in range(4):
         out_refs[by][...] = queries_ref[:, pl.ds(pl.multiple_of((y + by) % 4 * 512, 512), 512)]
@@ -90,8 +90,13 @@
             last_ref[...] = kv[...]
 
 
+def join_kernel(a0, a1, a2, a3, out_ref):
+    for n, a in enumerate((a0, a1, a2, a3)):
+        out_ref[n * 1024 : (n + 1) * 1024, :] = a[...]
+
+
 CHUNK = 1024
-PER_CHUNK = CHUNK // BLK
+HALF = 512
 
 
 def scores_of(keys, q):
@@ -108,9 +113,11 @@
     return eight
 
 
-def weigh(i, load, pieces, eight, values, top, tot, acc):
-    old = top[i]
-    new = jnp.maximum(old, jnp.max(eight, axis=0, keepdims=True))
+def weigh(i, load, pieces, eight, values, top, tot, acc, start=False):
+    new = jnp.broadcast_to(jnp.max(eight, axis=0, keepdims=True), eight.shape)
+    if not start:
+        old = top[i]
+        new = jnp.maximum(old, new)
     level = new[0:1]
     rounded, part = [], None
     for t in range(pieces):
@@ -120,8 +127,12 @@
             part = piece if part is None else part + piece
         rounded.append(weights.astype(jnp.bfloat16))
     product = jnp.dot(values, jnp.concatenate(rounded, axis=0), preferred_element_type=jnp.float32)
+    top[i] = new
+    if start:
+        tot[i] = part
+        acc[i] = product
+        return
     shrink = jnp.exp2((old - new) * EXP2_SCALE)
-    top[i] = new
     tot[i] = tot[i] * shrink + part
     acc[i] = acc[i] * shrink[0:1] + product
 
@@ -168,18 +179,22 @@
     return at
 
 
-def chunks(place_ref, order, begin, end, ql, kc, vc, top, tot, acc, vt, sa, sb, ma, mb):
+def chunks(size, unroll, place_ref, order, begin, count, ql, kc, vc, top, tot, acc, vt_ref, sa_ref, sb_ref, ma, mb):
+    pieces = size // BLK
+    vt, sa, sb = vt_ref.at[:, 0:size], sa_ref.at[0:size, :], sb_ref.at[0:size, :]
+
     def one_chunk(n, carry):
-        rows = pl.ds(pl.multiple_of(n * CHUNK, CHUNK), CHUNK)
-        last = order[n * PER_CHUNK]
-        for j in range(1, PER_CHUNK):
-            last = jnp.maximum(last, order[n * PER_CHUNK + j])
+        first = begin + n * pieces
+        rows = pl.ds(pl.multiple_of(first * BLK, HALF), size)
+        last = order[first]
+        for j in range(1, pieces):
+            last = jnp.maximum(last, order[first + j])
         vt[...] = vc[rows, :].T
 
         def score(i, buffer, eight):
             scores = scores_of(kc[rows, :], ql[i])
             buffer[...] = scores
-            eight[...] = top_of(lambda t: scores[BLK * t : BLK * (t + 1)], PER_CHUNK)
+            eight[...] = top_of(lambda t: scores[BLK * t : BLK * (t + 1)], pieces)
 
         def run(masked):
             def finish(i, buffer, eight):
@@ -190,48 +205,67 @@
                     mine = block_of(place_ref, i)
 
                     def load(t):
-                        return jnp.where(order[n * PER_CHUNK + t] < mine, plain(t), NEGATIVE)
-
-                    weigh(i, load, PER_CHUNK, top_of(load, PER_CHUNK), vt[...], top, tot, acc)
+                        return jnp.where(order[first + t] < mine, plain(t), NEGATIVE)
+
+                    weigh(i, load, pieces, top_of(load, pieces), vt[...], top, tot, acc)
                 else:
-                    weigh(i, plain, PER_CHUNK, eight[...], vt[...], top, tot, acc)
+                    weigh(i, plain, pieces, eight[...], vt[...], top, tot, acc)
 
             score(0, sa, ma)
             score(1, sb, mb)
-
-            def two(j, carry):
-                finish(2 * j, sa, ma)
-                score((2 * j + 2) % 16, sa, ma)
-                finish(2 * j + 1, sb, mb)
-                score((2 * j + 3) % 16, sb, mb)
+            each = 1 if masked else unroll
+
+            def some(j, carry):
+                for u in range(each):
+                    i = 2 * (j * each + u)
+                    finish(i, sa, ma)
+                    score((i + 2) % 16, sa, ma)
+                    finish(i + 1, sb, mb)
+                    score((i + 3) % 16, sb, mb)
                 return carry
 
-            lax.fori_loop(0, 8, two, 0)
+            lax.fori_loop(0, 8 // each, some, 0)
 
         free = last < place_ref[0] * 16
         pl.when(free)(lambda: run(False))
         pl.when(jnp.logical_not(free))(lambda: run(True))
         return carry
 
-    lax.fori_loop(begin, end, one_chunk, 0)
-
-
-def part_kernel(done, fresh, splits, final, place_ref, vert_ref, *refs):
-    sources, refs = list(refs[: sum(splits)]), refs[sum(splits) :]
+    lax.fori_loop(0, count, one_chunk, 0)
+
+
+def part_kernel(stage, place_ref, vert_ref, *refs):
+    splits = ((1,), (1, 1), (2,))[stage]
+    sources, refs = refs[: sum(splits)], refs[sum(splits) :]
     ql = refs[0]
-    refs = refs[6:] if done else refs[4:]
-    kc, vc, top, tot, acc = refs[:5]
-    outs, refs = (refs[5:9], refs[9:]) if final else (None, refs[5:])
-    bounds, order = refs[:2]
+    refs = refs[6:] if stage else refs[4:]
+    final = stage == 2
+    outs = refs[5:9] if final else None
+    bounds, order = refs[9:11] if final else refs[5:7]
+    work = (ql, *refs[:5], *(refs[11:] if final else refs[7:]))
+    kc, vc, _, tot, acc = refs[:5]
     find_bounds(vert_ref, place_ref[1], bounds)
-    at = jnp.int32(0)
-    for outer in done:
-        at = walk(place_ref, vert_ref, bounds, order, outer, at, None, kc, vc)
-    begin = at // PER_CHUNK
-    for outer, count in zip(fresh, splits):
-        at = walk(place_ref, vert_ref, bounds, order, outer, at, sources[:count], kc, vc)
-        sources = sources[count:]
-    chunks(place_ref, order, begin, at // PER_CHUNK, ql, kc, vc, top, tot, acc, *refs[2:])
+
+    def add(outer, at, fresh):
+        return walk(place_ref, vert_ref, bounds, order, outer, at, fresh, kc, vc)
+
+    near = add(0, jnp.int32(0), sources if stage == 0 else None)
+    begin = near // 8 * 8
+    if stage == 0:
+        chunks(HALF, 2, place_ref, order, jnp.int32(0), near // 8, *work)
+    else:
+        at = add(1, near, sources[:1] if stage == 1 else None)
+        at = add(3, at, sources[1:] if stage == 1 else None)
+        whole = (at - begin) // 16
+        if stage == 1:
+            chunks(CHUNK, 2, place_ref, order, begin, whole, *work)
+        else:
+            add(2, at, sources)
+            begin = begin + whole * 16
+            left = (NV - begin) // 16
+            chunks(CHUNK, 2, place_ref, order, begin, left, *work)
+            begin = begin + left * 16
+            chunks(HALF, 1, place_ref, order, begin, (NV - begin) // 8, *work)
     if final:
         for by in range(4):
             for block in range(4):
@@ -256,15 +290,12 @@
         for block in range(4):
             for g in range(4):
                 ql[by * 4 + block, g * BLK : (g + 1) * BLK, :] = q[block * BLK : (block + 1) * BLK, g * 128 : (g + 1) * 128]
-    top[...] = jnp.full(top.shape, NEGATIVE, jnp.float32)
-    tot[...] = jnp.zeros_like(tot)
-    acc[...] = jnp.zeros_like(acc)
     key = lax.broadcasted_iota(jnp.int32, (BLK, 256), 0)
     row = lax.broadcasted_iota(jnp.int32, (BLK, 256), 1) % BLK
 
-    def two(j, carry):
-        for u in range(2):
-            i = 2 * j + u
+    def some(j, carry):
+        for u in range(4):
+            i = 4 * j + u
             block = block_of(place_ref, i)
             here = block - group * 16
             starts, valid = [here], []
@@ -285,22 +316,19 @@
                 here = scores[BLK * t : BLK * (t + 1)]
                 return jnp.where(key <= row if t == 0 else valid[t - 1], here, NEGATIVE)
 
-            weigh(i, load, 4, top_of(load, 4), values, top, tot, acc)
+            weigh(i, load, 4, top_of(load, 4), values, top, tot, acc, True)
         return carry
 
-    lax.fori_loop(0, 8, two, 0)
+    lax.fori_loop(0, 4, some, 0)
 
 
 def project(place_ref, a, weight_ref, by, rows, keep):
     head = (place_ref[1] + by) % 4
     depth = pl.ds(pl.multiple_of(head * 512, 512), 512)
 
-    def tile(n, carry):
-        columns = pl.ds(pl.multiple_of(n * 512, 512), 512)
+    for n in range(8):
+        columns = slice(n * 512, (n + 1) * 512)
         keep(columns, jnp.dot(a[rows, :], weight_ref[depth, columns], preferred_element_type=jnp.float32))
-        return carry
-
-    lax.fori_loop(0, 8, tile, 0)
 
 
 def first_piece_kernel(place_ref, a, weight_ref, total_ref):
@@ -371,12 +399,12 @@
     place = jnp.stack([x * 4 + z, y, jnp.where(c == 0, x, z), jnp.where(c == 0, z, x), c]).astype(jnp.int32)
     kv = call(kv_kernel, [bf16(SLAB, 256)] * 4, [place], [keys, values], 1e6, 4)
     kv = [kv[0]] + [along_y(kv[by], by) for by in (1, 2, 3)]
-    q = call(q_kernel, [bf16(SLAB, 512)] * 4, [place], [queries], 1e6, 4)
+    q = call(q_kernel, [bf16(SLAB, 512)] * 4, [place, vertical], [queries], 1e6, 4)
     q = [q[0]] + [along_y(q[by], by) for by in (1, 2, 3)]
     own, last = call(slots_kernel, [bf16(1024, 128), bf16(SLAB, 256)], [place, vertical], kv, 1e6, 4)
     hops = [first_hop(own, by) for by in (1, 2, 3)]
     prev = to_next_group(last)
-    near = jnp.concatenate([own] + hops, axis=0)
+    near = call(join_kernel, [bf16(4096, 128)], [], [own, *hops], 1e6, 4)[0]
     plus, minus = second_hop(near, 1), second_hop(near, 3)
     beyond = [second_hop(plus[:2048], 1), second_hop(minus[2048:], 3)]
     ql, *state = call(
@@ -384,15 +412,15 @@
         [pltpu.VMEM((5 * SLAB, 128), jnp.bfloat16)] * 2,
     )
     state = call(
-        functools.partial(part_kernel, (), (0,), (1,), False), PACKED + STATE, [place, vertical],
+        functools.partial(part_kernel, 0), PACKED + STATE, [place, vertical],
         [near, ql, *state], 5e9, 8, WORK, {4 + n: 2 + n for n in range(3)},
     )
     state = call(
-        functools.partial(part_kernel, (0,), (1, 3), (1, 1), False), PACKED + STATE, [place, vertical],
+        functools.partial(part_kernel, 1), PACKED + STATE, [place, vertical],
         [plus, minus, ql, *state], 1e10, 8, WORK, {5 + n: n for n in range(5)},
     )
     state = call(
-        functools.partial(part_kernel, (0, 1, 3), (2,), (2,), True), PACKED + STATE + [bf16(SLAB, 512)] * 4,
+        functools.partial(part_kernel, 2), PACKED + STATE + [bf16(SLAB, 512)] * 4,
         [place, vertical], [*beyond, ql, *state], 5e9, 8, WORK, {5 + n: n for n in range(5)},
     )
     attention = state[5:]

time: 126 us -> 125 us (level)
  the two profiles are of different devices: /device:TPU:97 before, /device:TPU:1 now
where the time goes in v1:
time: 125 us
  Pallas kernels  58.5 us (47%)
  starting transfers between devices  33.2 us (27%)
  waiting for transfers between devices  23.5 us (19%)
  local copies, waits for them, and re-layouts  8.11 us (6%)
    pallas_call x13, Pallas kernels, call(): pl.pallas_call(kernel, out_shape=outs, in_specs=[SMEM] * len(scalars) + [...  58.5 us
    ppermute x18, starting transfers between devices, moved(): return lax.ppermute(value, ALL, pairs)  33.2 us
    ppermute x18, waiting for transfers between devices, moved(): return lax.ppermute(value, ALL, pairs)  23.5 us
    unnamed x33, local copies, waits for them, and re-layouts  6.91 us
  transfers between devices with their start and end apart: 18, of which 10 were waited for; matrix products, arithmetic and copies ran while one was open for 1% of the time, Pallas kernels for 37%

profile of v1, /device:TPU:1, one launch (start us, length us, event | category | flops | bytes accessed | tf_op | source)
XLA Modules:
  0.0 124.7 jit_solution(10107645603080993834)
XLA Ops:
  0.1 1.0 copy-done.1
  1.1 0.9 copy-done.2
  2.1 0.6 shard_map.64
  2.7 2.2 %collective-permute-start = (bf16[256,256]{1,0:T(8,128)(2,1)S(1)}, bf16[256,256]{1,0:T(8,128)(2,1)S(1)}, u32[]{:S(2)}, u32[]{:S(2)}) collective-permute-start(bf16[256,256]{1,0:T(8,128)(2,1)S(1)} %get-tuple-element.34), channel_id=1, source_target_pairs={{0,2},{1,3},{2,4},{3,5},{4,6},{5,7},{6,0},{7,1},{8,10},{9,11},{10,... | collective-permute-start | bytes 393224 | tf_op jit(solution)/shard_map/ppermute | solution.py:29
  4.9 2.6 %collective-permute-start.1 = (bf16[256,256]{1,0:T(8,128)(2,1)S(1)}, bf16[256,256]{1,0:T(8,128)(2,1)S(1)}, u32[]{:S(2)}, u32[]{:S(2)}) collective-permute-start(bf16[256,256]{1,0:T(8,128)(2,1)S(1)} %get-tuple-element.35), channel_id=1, source_target_pairs={{0,4},{1,5},{2,6},{3,7},{4,0},{5,1},{6,2},{7,3},{8,12},{9,13},{10,... | collective-permute-start | bytes 393224 | tf_op jit(solution)/shard_map/ppermute | solution.py:29
  7.5 1.1 collective-permute-start.2
  8.6 0.8 collective-permute-done.kv1
  9.4 3.8 %collective-permute-done.1.kv2 = bf16[256,256]{1,0:T(8,128)(2,1)S(1)} collective-permute-done((bf16[256,256]{1,0:T(8,128)(2,1)S(1)}, bf16[256,256]{1,0:T(8,128)(2,1)S(1)}, u32[]{:S(2)}, u32[]{:S(2)}) %collective-permute-start.1) | collective-permute-done | bytes 131104 | tf_op jit(solution)/shard_map/ppermute | solution.py:29
  13.3 0.7 copy-done.5
  13.9 0.9 shard_map.65
  14.9 1.7 %collective-permute-start.3 = (bf16[1024,128]{1,0:T(8,128)(2,1)S(1)}, bf16[1024,128]{1,0:T(8,128)(2,1)S(1)}, u32[]{:S(2)}, u32[]{:S(2)}) collective-permute-start(bf16[1024,128]{1,0:T(8,128)(2,1)S(1)} %get-tuple-element.37.a0), channel_id=1, source_target_pairs={{0,32},{1,9},{2,34},{3,11},{4,36},{5,13},{6,38},{7,15},{8,40},{9,1... | collective-permute-start | bytes 786440 | tf_op jit(solution)/shard_map/ppermute | solution.py:29
  16.6 3.3 %collective-permute-start.4 = (bf16[1024,128]{1,0:T(8,128)(2,1)S(1)}, bf16[1024,128]{1,0:T(8,128)(2,1)S(1)}, u32[]{:S(2)}, u32[]{:S(2)}) collective-permute-start(bf16[1024,128]{1,0:T(8,128)(2,1)S(1)} %get-tuple-element.37.a0), channel_id=1, source_target_pairs={{0,64},{1,17},{2,66},{3,19},{4,68},{5,21},{6,70},{7,23},{8,72},{9,... | collective-permute-start | bytes 786440 | tf_op jit(solution)/shard_map/ppermute | solution.py:29
  19.9 0.7 collective-permute-start.5
  20.6 0.7 collective-permute-start.13
  21.3 1.4 %collective-permute-done.3.a1 = bf16[1024,128]{1,0:T(8,128)(2,1)S(1)} collective-permute-done((bf16[1024,128]{1,0:T(8,128)(2,1)S(1)}, bf16[1024,128]{1,0:T(8,128)(2,1)S(1)}, u32[]{:S(2)}, u32[]{:S(2)}) %collective-permute-start.3) | collective-permute-done | bytes 262176 | tf_op jit(solution)/shard_map/ppermute | solution.py:29
  22.7 4.0 %collective-permute-done.4.a2 = bf16[1024,128]{1,0:T(8,128)(2,1)S(1)} collective-permute-done((bf16[1024,128]{1,0:T(8,128)(2,1)S(1)}, bf16[1024,128]{1,0:T(8,128)(2,1)S(1)}, u32[]{:S(2)}, u32[]{:S(2)}) %collective-permute-start.4) | collective-permute-done | bytes 262176 | tf_op jit(solution)/shard_map/ppermute | solution.py:29
  26.8 1.7 %collective-permute-start.6 = (bf16[4096,128]{1,0:T(8,128)(2,1)S(1)}, bf16[4096,128]{1,0:T(8,128)(2,1)S(1)}, u32[]{:S(2)}, u32[]{:S(2)}) collective-permute-start(bf16[4096,128]{1,0:T(8,128)(2,1)S(1)} %shard_map.66.refs_0_), channel_id=1, source_target_pairs={{0,8},{1,33},{2,10},{3,35},{4,12},{5,37},{6,14},{7,39},{8,16},{9,4... | collective-permute-start | bytes 3145736 | tf_op jit(solution)/shard_map/ppermute | solution.py:29
  28.5 1.7 %collective-permute-start.8 = (bf16[4096,128]{1,0:T(8,128)(2,1)S(1)}, bf16[4096,128]{1,0:T(8,128)(2,1)}, u32[]{:S(2)}, u32[]{:S(2)}) collective-permute-start(bf16[4096,128]{1,0:T(8,128)(2,1)S(1)} %shard_map.66.refs_0_), channel_id=1, source_target_pairs={{0,24},{1,97},{2,26},{3,99},{4,28},{5,101},{6,30},{7,103},{8,0},{9... | collective-permute-start | bytes 3145736 | tf_op jit(solution)/shard_map/ppermute | solution.py:29
  30.2 1.5 %shard_map.67 = (bf16[256,512]{1,0:T(8,128)(2,1)S(1)}, bf16[256,512]{1,0:T(8,128)(2,1)}, bf16[256,512]{1,0:T(8,128)(2,1)}, bf16[256,512]{1,0:T(8,128)(2,1)}) custom-call(s32[5]{0:T(128)S(1)} %stack.23.place_ref, s32[4,64]{1,0:T(4,128)S(1)} %copy-done.6, bf16[256,2048]{1,0:T(8,128)(2,1)S(1)} %copy-done), custom_call_target="tpu_custom_call" | custom-call | flops 1000000 | bytes 1000000 | tf_op jit(solution)/shard_map/pallas_call | solution.py:385
  31.7 0.7 copy-done.7
  32.4 1.3 %collective-permute-start.10 = (bf16[256,512]{1,0:T(8,128)(2,1)}, bf16[256,512]{1,0:T(8,128)(2,1)S(1)}, u32[]{:S(2)}, u32[]{:S(2)}) collective-permute-start(bf16[256,512]{1,0:T(8,128)(2,1)} %get-tuple-element.39), channel_id=1, source_target_pairs={{0,2},{1,3},{2,4},{3,5},{4,6},{5,7},{6,0},{7,1},{8,10},{9,11},{10,... | collective-permute-start | bytes 786440 | tf_op jit(solution)/shard_map/ppermute | solution.py:29
  33.7 2.3 %collective-permute-start.11 = (bf16[256,512]{1,0:T(8,128)(2,1)}, bf16[256,512]{1,0:T(8,128)(2,1)S(1)}, u32[]{:S(2)}, u32[]{:S(2)}) collective-permute-start(bf16[256,512]{1,0:T(8,128)(2,1)} %get-tuple-element.40), channel_id=1, source_target_pairs={{0,4},{1,5},{2,6},{3,7},{4,0},{5,1},{6,2},{7,3},{8,12},{9,13},{10,... | collective-permute-start | bytes 786440 | tf_op jit(solution)/shard_map/ppermute | solution.py:29
  35.9 0.7 copy-done.9
  36.6 0.4 collective-permute-start.12
  37.1 2.2 %collective-permute-done.10.q1 = bf16[256,512]{1,0:T(8,128)(2,1)S(1)} collective-permute-done((bf16[256,512]{1,0:T(8,128)(2,1)}, bf16[256,512]{1,0:T(8,128)(2,1)S(1)}, u32[]{:S(2)}, u32[]{:S(2)}) %collective-permute-start.10) | collective-permute-done | bytes 262176 | tf_op jit(solution)/shard_map/ppermute | solution.py:29
  39.3 5.6 %collective-permute-done.11.q2 = bf16[256,512]{1,0:T(8,128)(2,1)S(1)} collective-permute-done((bf16[256,512]{1,0:T(8,128)(2,1)}, bf16[256,512]{1,0:T(8,128)(2,1)S(1)}, u32[]{:S(2)}, u32[]{:S(2)}) %collective-permute-start.11) | collective-permute-done | bytes 262176 | tf_op jit(solution)/shard_map/ppermute | solution.py:29
  44.9 0.9 copy-done.4
  45.8 0.9 copy-done.8
  46.8 0.9 copy-done.10
  47.7 5.7 %shard_map.68 = (bf16[16,256,128]{2,1,0:T(8,128)(2,1)S(1)}, f32[16,8,256]{2,1,0:T(8,128)S(1)}, f32[16,8,256]{2,1,0:T(8,128)S(1)}, f32[16,128,256]{2,1,0:T(8,128)S(1)}) custom-call(s32[5]{0:T(128)S(1)} %stack.23.place_ref, s32[4,64]{1,0:T(4,128)S(1)} %copy-done.6, s32[4,2]{1,0:T(4,128)S(1)} %copy.22.slash_ref, bf16[256,512]{1,0:T(8,128)(2,1)S(1)} %copy-done.8, ...), custom_call_target="tpu_custom_call" | custom-call | flops 3000000000 | bytes 1000000 | tf_op jit(solution)/shard_map/pallas_call | solution.py:385
  53.4 20.8 %shard_map.69 = (bf16[4096,128]{1,0:T(8,128)(2,1)S(1)}, bf16[4096,128]{1,0:T(8,128)(2,1)S(1)}, f32[16,8,256]{2,1,0:T(8,128)S(1)}, f32[16,8,256]{2,1,0:T(8,128)S(1)}, f32[16,128,256]{2,1,0:T(8,128)S(1)}) custom-call(s32[5]{0:T(128)S(1)} %stack.23.place_ref, s32[4,64]{1,0:T(4,128)S(1)} %copy-done.6, ...), custom_call_target="tpu_custom_call", output_to_operand_aliasing={{2}: (4, {}), {3}: (5, {}), {4}: (6, {})} | custom-call | flops 5000000000 | bytes 1000000 | tf_op jit(solution)/shard_map/pallas_call | solution.py:385
  74.4 1.1 slice.9
  75.4 2.7 %collective-permute-start.9 = (bf16[2048,128]{1,0:T(8,128)(2,1)S(1)}, bf16[2048,128]{1,0:T(8,128)(2,1)S(1)}, u32[]{:S(2)}, u32[]{:S(2)}) collective-permute-start(bf16[2048,128]{1,0:T(8,128)(2,1)S(1)} %slice.9), channel_id=1, source_target_pairs={{0,24},{1,97},{2,26},{3,99},{4,28},{5,101},{6,30},{7,103},{8,0},{9... | collective-permute-start | bytes 1572872 | tf_op jit(solution)/shard_map/ppermute | solution.py:29
  78.2 10.8 %shard_map.70 = (bf16[4096,128]{1,0:T(8,128)(2,1)S(1)}, bf16[4096,128]{1,0:T(8,128)(2,1)S(1)}, f32[16,8,256]{2,1,0:T(8,128)S(1)}, f32[16,8,256]{2,1,0:T(8,128)S(1)}, f32[16,128,256]{2,1,0:T(8,128)S(1)}) custom-call(s32[5]{0:T(128)S(1)} %stack.23.place_ref, ...), custom_call_target="tpu_custom_call", output_to_operand_aliasing={{0}: (5, {}), {1}: (6, {}), {2}: (7, {}), {3}: (8, {}), {4}... | custom-call | flops 10000000000 | bytes 1000000 | tf_op jit(solution)/shard_map/pallas_call | solution.py:385
  89.0 10.1 %shard_map.71 = (bf16[4096,128]{1,0:T(8,128)(2,1)S(1)}, bf16[4096,128]{1,0:T(8,128)(2,1)S(1)}, f32[16,8,256]{2,1,0:T(8,128)S(1)}, f32[16,8,256]{2,1,0:T(8,128)S(...) custom-call(s32[5]{0:T(128)S(1)} %stack.23.place_ref, ...), custom_call_target="tpu_custom_call", output_to_operand_aliasing={{0}: (5, {}), {1}: (6, {}), {2}: (7, {}), {3}: (8, {}), {4}... | custom-call | flops 5000000000 | bytes 1000000 | tf_op jit(solution)/shard_map/pallas_call | solution.py:385
  99.1 3.3 %collective-permute-start.16 = (bf16[256,512]{1,0:T(8,128)(2,1)S(1)}, bf16[256,512]{1,0:T(8,128)(2,1)S(1)}, u32[]{:S(2)}, u32[]{:S(2)}) collective-permute-start(bf16[256,512]{1,0:T(8,128)(2,1)S(1)} %get-tuple-element.59), channel_id=1, source_target_pairs={{0,6},{1,7},{2,0},{3,1},{4,2},{5,3},{6,4},{7,5},{8,14},{9,15},{10,... | collective-permute-start | bytes 786440 | tf_op jit(solution)/shard_map/ppermute | solution.py:29
  102.4 1.3 %collective-permute-start.14 = (bf16[256,512]{1,0:T(8,128)(2,1)S(1)}, bf16[256,512]{1,0:T(8,128)(2,1)S(1)}, u32[]{:S(2)}, u32[]{:S(2)}) collective-permute-start(bf16[256,512]{1,0:T(8,128)(2,1)S(1)} %get-tuple-element.57), channel_id=1, source_target_pairs={{0,4},{1,5},{2,6},{3,7},{4,0},{5,1},{6,2},{7,3},{8,12},{9,13},{10,... | collective-permute-start | bytes 786440 | tf_op jit(solution)/shard_map/ppermute | solution.py:29
  103.7 1.8 %shard_map.72.total_in = f32[256,4096]{1,0:T(8,128)S(1)} custom-call(s32[5]{0:T(128)S(1)} %stack.23.place_ref, bf16[256,512]{1,0:T(8,128)(2,1)S(1)} %get-tuple-element.60.a, bf16[2048,4096]{1,0:T(8,128)(2,1)S(1)} %bitcast.6), custom_call_target="tpu_custom_call" | custom-call | flops 1000000000 | bytes 1000000 | tf_op jit(solution)/shard_map/pallas_call | solution.py:385
  105.6 0.9 collective-permute-done.16.a
  106.5 1.8 %shard_map.73.total_in = f32[256,4096]{1,0:T(8,128)S(1)} custom-call(s32[5]{0:T(128)S(1)} %stack.23.place_ref, bf16[256,512]{1,0:T(8,128)(2,1)S(1)} %collective-permute-done.16.a, bf16[2048,4096]{1,0:T(8,128)(2,1)S(1)} %bitcast.6, f32[256,4096]{1,0:T(8,128)S(1)} %shard_map.72.total_in), custom_call_target="tpu_custom_call", output_to_operand_aliasing={{}: (3, {})} | custom-call | flops 1000000000 | bytes 1000000 | tf_op jit(solution)/shard_map/pallas_call | solution.py:385
  108.3 3.1 %collective-permute-done.15.a = bf16[256,512]{1,0:T(8,128)(2,1)S(1)} collective-permute-done((bf16[256,512]{1,0:T(8,128)(2,1)S(1)}, bf16[256,512]{1,0:T(8,128)(2,1)S(1)}, u32[]{:S(2)}, u32[]{:S(2)}) %collective-permute-start.15) | collective-permute-done | bytes 262176 | tf_op jit(solution)/shard_map/ppermute | solution.py:29
  111.4 1.8 %shard_map.74.total_ref = f32[256,4096]{1,0:T(8,128)S(1)} custom-call(s32[5]{0:T(128)S(1)} %stack.23.place_ref, bf16[256,512]{1,0:T(8,128)(2,1)S(1)} %collective-permute-done.15.a, bf16[2048,4096]{1,0:T(8,128)(2,1)S(1)} %bitcast.6, f32[256,4096]{1,0:T(8,128)S(1)} %shard_map.73.total_in), custom_call_target="tpu_custom_call", output_to_operand_aliasing={{}: (3, {})} | custom-call | flops 1000000000 | bytes 1000000 | tf_op jit(solution)/shard_map/pallas_call | solution.py:385
  113.2 0.6 collective-permute-done.14.a
  113.8 1.3 %shard_map.76 = bf16[128,4096]{1,0:T(8,128)(2,1)S(1)} custom-call(s32[5]{0:T(128)S(1)} %stack.23.place_ref, bf16[256,512]{1,0:T(8,128)(2,1)S(1)} %collective-permute-done.14.a, bf16[2048,4096]{1,0:T(8,128)(2,1)S(1)} %bitcast.6, f32[256,4096]{1,0:T(8,128)S(1)} %shard_map.74.total_ref), custom_call_target="tpu_custom_call" | custom-call | flops 1000000000 | bytes 1000000 | tf_op jit(solution)/shard_map/pallas_call | solution.py:385
  115.1 6.1 %collective-permute-start.17 = (bf16[128,4096]{1,0:T(8,128)(2,1)S(1)}, bf16[128,4096]{1,0:T(8,128)(2,1)S(1)}, u32[]{:S(2)}, u32[]{:S(2)}) collective-permute-start(bf16[128,4096]{1,0:T(8,128)(2,1)S(1)} %shard_map.76), channel_id=1, source_target_pairs={{0,1},{1,0},{2,3},{3,2},{4,5},{5,4},{6,7},{7,6},{8,9},{9,8},{10,11... | collective-permute-start | bytes 3145736 | tf_op jit(solution)/shard_map/ppermute | solution.py:29
  121.2 1.3 %shard_map.75 = f32[128,4096]{1,0:T(8,128)S(1)} custom-call(s32[5]{0:T(128)S(1)} %stack.23.place_ref, bf16[256,512]{1,0:T(8,128)(2,1)S(1)} %collective-permute-done.14.a, bf16[2048,4096]{1,0:T(8,128)(2,1)S(1)} %bitcast.6, f32[256,4096]{1,0:T(8,128)S(1)} %shard_map.74.total_ref), custom_call_target="tpu_custom_call" | custom-call | flops 1000000000 | bytes 1000000 | tf_op jit(solution)/shard_map/pallas_call | solution.py:385
  122.5 1.0 collective-permute-done.17
  123.5 1.2 add_convert_fusion
  (39 shorter events, 0.4 us)
Async XLA Ops:
  0.0 30.2 %copy-start = (bf16[256,2048]{1,0:T(8,128)(2,1)S(1)}, bf16[256,2048]{1,0:T(8,128)(2,1)}, u32[]{:S(2)}) copy-start(bf16[256,2048]{1,0:T(8,128)(2,1)} %queries_ref.1) | copy-start | bytes 3145732
  0.1 1.0 copy-start.1
  1.1 0.9 copy-start.2
  2.7 6.7 %collective-permute-start = (bf16[256,256]{1,0:T(8,128)(2,1)S(1)}, bf16[256,256]{1,0:T(8,128)(2,1)S(1)}, u32[]{:S(2)}, u32[]{:S(2)}) collective-permute-start(bf16[256,256]{1,0:T(8,128)(2,1)S(1)} %get-tuple-element.34), channel_id=1, source_target_pairs={{0,2},{1,3},{2,4},{3,5},{4,6},{5,7},{6,0},{7,1},{8,10},{9,11},{10,... | collective-permute-start | bytes 393224 | tf_op jit(solution)/shard_map/ppermute | solution.py:29
  4.9 8.3 %collective-permute-start.1 = (bf16[256,256]{1,0:T(8,128)(2,1)S(1)}, bf16[256,256]{1,0:T(8,128)(2,1)S(1)}, u32[]{:S(2)}, u32[]{:S(2)}) collective-permute-start(bf16[256,256]{1,0:T(8,128)(2,1)S(1)} %get-tuple-element.35), channel_id=1, source_target_pairs={{0,4},{1,5},{2,6},{3,7},{4,0},{5,1},{6,2},{7,3},{8,12},{9,13},{10,... | collective-permute-start | bytes 393224 | tf_op jit(solution)/shard_map/ppermute | solution.py:29
  7.5 5.7 %collective-permute-start.2 = (bf16[256,256]{1,0:T(8,128)(2,1)S(1)}, bf16[256,256]{1,0:T(8,128)(2,1)S(1)}, u32[]{:S(2)}, u32[]{:S(2)}) collective-permute-start(bf16[256,256]{1,0:T(8,128)(2,1)S(1)} %get-tuple-element.36), channel_id=1, source_target_pairs={{0,6},{1,7},{2,0},{3,1},{4,2},{5,3},{6,4},{7,5},{8,14},{9,15},{10,... | collective-permute-start | bytes 393224 | tf_op jit(solution)/shard_map/ppermute | solution.py:29
  13.2 1.6 %copy-start.3 = (bf16[256,256]{1,0:T(8,128)(2,1)}, bf16[256,256]{1,0:T(8,128)(2,1)S(1)}, u32[]{:S(2)}) copy-start(bf16[256,256]{1,0:T(8,128)(2,1)S(1)} %collective-permute-done.2.kv3) | copy-start | bytes 393220
  13.3 0.7 copy-start.5
  13.9 16.2 %copy-start.6 = (s32[4,64]{1,0:T(4,128)S(1)}, s32[4,64]{1,0:T(4,128)}, u32[]{:S(2)}) copy-start(s32[4,64]{1,0:T(4,128)} %vert_ref.11) | copy-start | bytes 3076
  13.9 23.1 %copy-start.11 = (s32[4,2]{0,1:T(2,128)S(1)}, s32[4,2]{0,1:T(2,128)}, u32[]{:S(2)}) copy-start(s32[4,2]{0,1:T(2,128)} %param.10) | copy-start | bytes 100
  14.9 7.9 %collective-permute-start.3 = (bf16[1024,128]{1,0:T(8,128)(2,1)S(1)}, bf16[1024,128]{1,0:T(8,128)(2,1)S(1)}, u32[]{:S(2)}, u32[]{:S(2)}) collective-permute-start(bf16[1024,128]{1,0:T(8,128)(2,1)S(1)} %get-tuple-element.37.a0), channel_id=1, source_target_pairs={{0,32},{1,9},{2,34},{3,11},{4,36},{5,13},{6,38},{7,15},{8,40},{9,1... | collective-permute-start | bytes 786440 | tf_op jit(solution)/shard_map/ppermute | solution.py:29
  16.6 10.2 %collective-permute-start.4 = (bf16[1024,128]{1,0:T(8,128)(2,1)S(1)}, bf16[1024,128]{1,0:T(8,128)(2,1)S(1)}, u32[]{:S(2)}, u32[]{:S(2)}) collective-permute-start(bf16[1024,128]{1,0:T(8,128)(2,1)S(1)} %get-tuple-element.37.a0), channel_id=1, source_target_pairs={{0,64},{1,17},{2,66},{3,19},{4,68},{5,21},{6,70},{7,23},{8,72},{9,... | collective-permute-start | bytes 786440 | tf_op jit(solution)/shard_map/ppermute | solution.py:29
  19.9 6.9 %collective-permute-start.5 = (bf16[1024,128]{1,0:T(8,128)(2,1)S(1)}, bf16[1024,128]{1,0:T(8,128)(2,1)S(1)}, u32[]{:S(2)}, u32[]{:S(2)}) collective-permute-start(bf16[1024,128]{1,0:T(8,128)(2,1)S(1)} %get-tuple-element.37.a0), channel_id=1, source_target_pairs={{0,96},{1,25},{2,98},{3,27},{4,100},{5,29},{6,102},{7,31},{8,104},... | collective-permute-start | bytes 786440 | tf_op jit(solution)/shard_map/ppermute | solution.py:29
  20.6 15.3 %collective-permute-start.13 = (bf16[256,256]{1,0:T(8,128)(2,1)S(1)}, bf16[256,256]{1,0:T(8,128)(2,1)S(1)}, u32[]{:S(2)}, u32[]{:S(2)}) collective-permute-start(bf16[256,256]{1,0:T(8,128)(2,1)S(1)} %get-tuple-element.42), channel_id=1, source_target_pairs={{0,8},{1,9},{2,10},{3,11},{4,12},{5,13},{6,14},{7,15},{8,16},{9,17... | collective-permute-start | bytes 393224 | tf_op jit(solution)/shard_map/ppermute | solution.py:29
  26.8 47.4 %collective-permute-start.6 = (bf16[4096,128]{1,0:T(8,128)(2,1)S(1)}, bf16[4096,128]{1,0:T(8,128)(2,1)S(1)}, u32[]{:S(2)}, u32[]{:S(2)}) collective-permute-start(bf16[4096,128]{1,0:T(8,128)(2,1)S(1)} %shard_map.66.refs_0_), channel_id=1, source_target_pairs={{0,8},{1,33},{2,10},{3,35},{4,12},{5,37},{6,14},{7,39},{8,16},{9,4... | collective-permute-start | bytes 3145736 | tf_op jit(solution)/shard_map/ppermute | solution.py:29
  28.5 45.8 %collective-permute-start.8 = (bf16[4096,128]{1,0:T(8,128)(2,1)S(1)}, bf16[4096,128]{1,0:T(8,128)(2,1)}, u32[]{:S(2)}, u32[]{:S(2)}) collective-permute-start(bf16[4096,128]{1,0:T(8,128)(2,1)S(1)} %shard_map.66.refs_0_), channel_id=1, source_target_pairs={{0,24},{1,97},{2,26},{3,99},{4,28},{5,101},{6,30},{7,103},{8,0},{9... | collective-permute-start | bytes 3145736 | tf_op jit(solution)/shard_map/ppermute | solution.py:29
  31.7 0.7 copy-start.7
  32.4 6.9 %collective-permute-start.10 = (bf16[256,512]{1,0:T(8,128)(2,1)}, bf16[256,512]{1,0:T(8,128)(2,1)S(1)}, u32[]{:S(2)}, u32[]{:S(2)}) collective-permute-start(bf16[256,512]{1,0:T(8,128)(2,1)} %get-tuple-element.39), channel_id=1, source_target_pairs={{0,2},{1,3},{2,4},{3,5},{4,6},{5,7},{6,0},{7,1},{8,10},{9,11},{10,... | collective-permute-start | bytes 786440 | tf_op jit(solution)/shard_map/ppermute | solution.py:29
  33.7 11.2 %collective-permute-start.11 = (bf16[256,512]{1,0:T(8,128)(2,1)}, bf16[256,512]{1,0:T(8,128)(2,1)S(1)}, u32[]{:S(2)}, u32[]{:S(2)}) collective-permute-start(bf16[256,512]{1,0:T(8,128)(2,1)} %get-tuple-element.40), channel_id=1, source_target_pairs={{0,4},{1,5},{2,6},{3,7},{4,0},{5,1},{6,2},{7,3},{8,12},{9,13},{10,... | collective-permute-start | bytes 786440 | tf_op jit(solution)/shard_map/ppermute | solution.py:29
  35.9 0.7 copy-start.9
  36.6 8.3 %collective-permute-start.12 = (bf16[256,512]{1,0:T(8,128)(2,1)}, bf16[256,512]{1,0:T(8,128)(2,1)S(1)}, u32[]{:S(2)}, u32[]{:S(2)}) collective-permute-start(bf16[256,512]{1,0:T(8,128)(2,1)} %get-tuple-element.41), channel_id=1, source_target_pairs={{0,6},{1,7},{2,0},{3,1},{4,2},{5,3},{6,4},{7,5},{8,14},{9,15},{10,... | collective-permute-start | bytes 786440 | tf_op jit(solution)/shard_map/ppermute | solution.py:29
  44.9 0.9 copy-start.4
  45.8 0.9 copy-start.8
  46.8 0.9 copy-start.10
  74.3 14.7 %collective-permute-start.7 = (bf16[2048,128]{1,0:T(8,128)(2,1)S(1)}, bf16[2048,128]{1,0:T(8,128)(2,1)S(1)}, u32[]{:S(2)}, u32[]{:S(2)}) collective-permute-start(bf16[2048,128]{1,0:T(8,128)(2,1)S(1)} %slice.8), channel_id=1, source_target_pairs={{0,8},{1,33},{2,10},{3,35},{4,12},{5,37},{6,14},{7,39},{8,16},{9,4... | collective-permute-start | bytes 1572872 | tf_op jit(solution)/shard_map/ppermute | solution.py:29
  75.4 13.6 %collective-permute-start.9 = (bf16[2048,128]{1,0:T(8,128)(2,1)S(1)}, bf16[2048,128]{1,0:T(8,128)(2,1)S(1)}, u32[]{:S(2)}, u32[]{:S(2)}) collective-permute-start(bf16[2048,128]{1,0:T(8,128)(2,1)S(1)} %slice.9), channel_id=1, source_target_pairs={{0,24},{1,97},{2,26},{3,99},{4,28},{5,101},{6,30},{7,103},{8,0},{9... | collective-permute-start | bytes 1572872 | tf_op jit(solution)/shard_map/ppermute | solution.py:29
  78.2 25.5 %slice-start = ((s8[16777216]{0:T(1024)(128)(4,1)}), s8[4194304]{0:T(1024)(128)(4,1)S(1)}, s32[]{:S(2)}) async-start(s8[16777216]{0:T(1024)(128)(4,1)} %bitcast.5), calls=%async_computation | async-start | bytes 8388608
  78.2 25.5 %slice-start.1 = ((s8[16777216]{0:T(1024)(128)(4,1)}), s8[4194304]{0:T(1024)(128)(4,1)S(1)}, s32[]{:S(2)}) async-start(s8[16777216]{0:T(1024)(128)(4,1)} %bitcast.5), calls=%async_computation.1 | async-start | bytes 8388608
  78.2 25.5 %slice-start.2 = ((s8[16777216]{0:T(1024)(128)(4,1)}), s8[4194304]{0:T(1024)(128)(4,1)S(1)}, s32[]{:S(2)}) async-start(s8[16777216]{0:T(1024)(128)(4,1)} %bitcast.5), calls=%async_computation.2 | async-start | bytes 8388608
  89.0 14.7 %slice-start.3 = ((s8[16777216]{0:T(1024)(128)(4,1)}), s8[4194304]{0:T(1024)(128)(4,1)S(1)}, s32[]{:S(2)}) async-start(s8[16777216]{0:T(1024)(128)(4,1)} %bitcast.5), calls=%async_computation.3 | async-start | bytes 8388608
  99.1 7.3 %collective-permute-start.16 = (bf16[256,512]{1,0:T(8,128)(2,1)S(1)}, bf16[256,512]{1,0:T(8,128)(2,1)S(1)}, u32[]{:S(2)}, u32[]{:S(2)}) collective-permute-start(bf16[256,512]{1,0:T(8,128)(2,1)S(1)} %get-tuple-element.59), channel_id=1, source_target_pairs={{0,6},{1,7},{2,0},{3,1},{4,2},{5,3},{6,4},{7,5},{8,14},{9,15},{10,... | collective-permute-start | bytes 786440 | tf_op jit(solution)/shard_map/ppermute | solution.py:29
  102.4 8.9 %collective-permute-start.15 = (bf16[256,512]{1,0:T(8,128)(2,1)S(1)}, bf16[256,512]{1,0:T(8,128)(2,1)S(1)}, u32[]{:S(2)}, u32[]{:S(2)}) collective-permute-start(bf16[256,512]{1,0:T(8,128)(2,1)S(1)} %get-tuple-element.58), channel_id=1, source_target_pairs={{0,2},{1,3},{2,4},{3,5},{4,6},{5,7},{6,0},{7,1},{8,10},{9,11},{10,... | collective-permute-start | bytes 786440 | tf_op jit(solution)/shard_map/ppermute | solution.py:29
  102.4 11.4 %collective-permute-start.14 = (bf16[256,512]{1,0:T(8,128)(2,1)S(1)}, bf16[256,512]{1,0:T(8,128)(2,1)S(1)}, u32[]{:S(2)}, u32[]{:S(2)}) collective-permute-start(bf16[256,512]{1,0:T(8,128)(2,1)S(1)} %get-tuple-element.57), channel_id=1, source_target_pairs={{0,4},{1,5},{2,6},{3,7},{4,0},{5,1},{6,2},{7,3},{8,12},{9,13},{10,... | collective-permute-start | bytes 786440 | tf_op jit(solution)/shard_map/ppermute | solution.py:29
  115.1 8.4 %collective-permute-start.17 = (bf16[128,4096]{1,0:T(8,128)(2,1)S(1)}, bf16[128,4096]{1,0:T(8,128)(2,1)S(1)}, u32[]{:S(2)}, u32[]{:S(2)}) collective-permute-start(bf16[128,4096]{1,0:T(8,128)(2,1)S(1)} %shard_map.76), channel_id=1, source_target_pairs={{0,1},{1,0},{2,3},{3,2},{4,5},{5,4},{6,7},{7,6},{8,9},{9,8},{10,11... | collective-permute-start | bytes 3145736 | tf_op jit(solution)/shard_map/ppermute | solution.py:29

commit v2 on v1

--- a/solution.py
+++ b/solution.py
@@ -14,6 +14,9 @@
 NV = 64
 EXP2_SCALE = HEAD_DIM ** (-0.5) * 1.4426950408889634
 NEGATIVE = -1e30
+SLASH = 8
+VERT = 16
+NEVER = 1 << 20
 ALL = ("x", "z", "y", "c")
 MIB = 1 << 20
 
@@ -49,11 +52,11 @@
     return moved(value, lambda x, z, y, c: (x, z, y, 1 - c))
 
 
-def rank_of(vert_ref, head, block):
-    at = jnp.int32(0)
+def row_rank(table_ref, block):
+    at = jnp.int32(VERT)
     for width in (32, 16, 8, 4, 2, 1):
-        at = at + jnp.where(vert_ref[head, at + width - 1] < block, width, 0)
-    return at + jnp.where(vert_ref[head, at] < block, 1, 0)
+        at = at + jnp.where(table_ref[at + width - 1] < block, width, 0)
+    return at - VERT + jnp.where(table_ref[at] < block, 1, 0)
 
 
 def kv_kernel(place_ref, keys_ref, values_ref, *out_refs):
@@ -64,21 +67,27 @@
         out_refs[by][:, 128:256] = values_ref[:, lanes]
 
 
-def q_kernel(place_ref, vert_ref, queries_ref, *out_refs):
+def q_kernel(place_ref, queries_ref, *out_refs):
     y = place_ref[1]
     for by in range(4):
         out_refs[by][...] = queries_ref[:, pl.ds(pl.multiple_of((y + by) % 4 * 512, 512), 512)]
 
 
-def slots_kernel(place_ref, vert_ref, kv0, kv1, kv2, kv3, own_ref, last_ref):
+def slots_kernel(place_ref, vert_ref, slash_ref, kv0, kv1, kv2, kv3, own_ref, last_ref, table_ref):
     group, y = place_ref[0], place_ref[1]
+    for n in range(5):
+        table_ref[n] = place_ref[n]
+    for n in range(2):
+        table_ref[SLASH + n] = slash_ref[y, n]
+    for n in range(NV):
+        table_ref[VERT + n] = vert_ref[y, n]
     for by, kv in enumerate((kv0, kv1, kv2, kv3)):
         slab = (y - by + 4) % 4
         first = (group * 4 + slab) * 4
-        at = rank_of(vert_ref, y, first)
+        at = row_rank(table_ref, first)
         for slot in range(2):
             entry = jnp.minimum(at + slot, NV - 1)
-            block = vert_ref[y, entry] - first
+            block = table_ref[VERT + entry] - first
             block = jnp.where((block >= 0) & (block < 4), block, 0)
             rows = pl.ds(pl.multiple_of(block * BLK, BLK), BLK)
             to = by * 256 + slot * BLK
@@ -141,32 +150,32 @@
     return place_ref[0] * 16 + ((place_ref[1] - i // 4 + 4) % 4) * 4 + i % 4
 
 
-def find_bounds(vert_ref, head, bounds):
+def find_bounds(place_ref, bounds):
     bounds[0] = 0
     for g in range(1, 16):
-        bounds[g] = rank_of(vert_ref, head, 16 * g)
+        bounds[g] = row_rank(place_ref, 16 * g)
     bounds[16] = NV
 
 
-def walk(place_ref, vert_ref, bounds, order, outer, at, sources, kc, vc):
-    y, mine1, mine2, core = (place_ref[i] for i in range(1, 5))
-    head = y
+def walk(place_ref, bounds, order, outer, at, sources, kc, vc):
+    group, y, mine1, mine2, core = (place_ref[i] for i in range(5))
     second = (mine2 - outer + 4) % 4
     for inner in range(4):
         first = (mine1 - inner + 4) % 4
         g = jnp.where(core == 0, first * 4 + second, second * 4 + first)
-        start, end = bounds[g], bounds[g + 1]
+        start = bounds[g]
+        end = jnp.where(g <= group, bounds[g + 1], start)
         shift = at - start
 
         def one(entry, carry):
-            block = vert_ref[head, entry]
+            block = place_ref[VERT + entry]
             to = entry + shift
             order[to] = block
             if sources is not None:
                 source = sources[inner * len(sources) // 4]
                 skip = inner % (4 // len(sources))
                 slab = block // 4
-                before = vert_ref[head, jnp.maximum(entry - 1, 0)] // 4
+                before = place_ref[VERT + jnp.maximum(entry - 1, 0)] // 4
                 rank = jnp.where((entry > 0) & (before == slab), BLK, 0)
                 row = (skip * 4 + (y - slab % 4 + 4) % 4) * 256 + rank
                 rows = pl.ds(pl.multiple_of(to * BLK, BLK), BLK)
@@ -234,7 +243,7 @@
     lax.fori_loop(0, count, one_chunk, 0)
 
 
-def part_kernel(stage, place_ref, vert_ref, *refs):
+def part_kernel(stage, place_ref, *refs):
     splits = ((1,), (1, 1), (2,))[stage]
     sources, refs = refs[: sum(splits)], refs[sum(splits) :]
     ql = refs[0]
@@ -244,10 +253,10 @@
     bounds, order = refs[9:11] if final else refs[5:7]
     work = (ql, *refs[:5], *(refs[11:] if final else refs[7:]))
     kc, vc, _, tot, acc = refs[:5]
-    find_bounds(vert_ref, place_ref[1], bounds)
+    find_bounds(place_ref, bounds)
 
     def add(outer, at, fresh):
-        return walk(place_ref, vert_ref, bounds, order, outer, at, fresh, kc, vc)
+        return walk(place_ref, bounds, order, outer, at, fresh, kc, vc)
 
     near = add(0, jnp.int32(0), sources if stage == 0 else None)
     begin = near // 8 * 8
@@ -260,12 +269,20 @@
         if stage == 1:
             chunks(CHUNK, 2, place_ref, order, begin, whole, *work)
         else:
-            add(2, at, sources)
+            at = add(2, at, sources)
             begin = begin + whole * 16
-            left = (NV - begin) // 16
+            left = (at - begin) // 16
             chunks(CHUNK, 2, place_ref, order, begin, left, *work)
             begin = begin + left * 16
-            chunks(HALF, 1, place_ref, order, begin, (NV - begin) // 8, *work)
+            left = (at - begin + 7) // 8
+
+            def clear(n, carry):
+                order[n] = NEVER
+                vc[pl.ds(pl.multiple_of(n * BLK, BLK), BLK), :] = jnp.zeros((BLK, 128), jnp.bfloat16)
+                return carry
+
+            lax.fori_loop(at, begin + left * 8, clear, 0)
+            chunks(HALF, 1, place_ref, order, begin, left, *work)
     if final:
         for by in range(4):
             for block in range(4):
@@ -276,10 +293,9 @@
 
 
 def local_kernel(
-    place_ref, vert_ref, slash_ref, q0, q1, q2, q3, kv0, kv1, kv2, kv3, prev_ref, ql, top, tot, acc, kl, vl
+    place_ref, q0, q1, q2, q3, kv0, kv1, kv2, kv3, prev_ref, ql, top, tot, acc, kl, vl
 ):
     group, y = place_ref[0], place_ref[1]
-    head = y
     kl[0:SLAB, :] = prev_ref[:, 0:128]
     vl[0:SLAB, :] = prev_ref[:, 128:256]
     for by, (q, kv) in enumerate(((q0, kv0), (q1, kv1), (q2, kv2), (q3, kv3))):
@@ -294,22 +310,23 @@
     row = lax.broadcasted_iota(jnp.int32, (BLK, 256), 1) % BLK
 
     def some(j, carry):
+        ready = []
         for u in range(4):
             i = 4 * j + u
             block = block_of(place_ref, i)
             here = block - group * 16
             starts, valid = [here], []
             for s in range(2):
-                offset = slash_ref[head, s]
+                offset = place_ref[SLASH + s]
                 behind = block - offset
-                at = jnp.minimum(rank_of(vert_ref, head, behind), NV - 1)
-                valid.append((behind >= 0) & (vert_ref[head, at] != behind))
+                at = jnp.minimum(row_rank(place_ref, behind), NV - 1)
+                valid.append((behind >= 0) & (place_ref[VERT + at] != behind))
                 starts.append(here - offset)
             rows = [pl.ds(pl.multiple_of(SLAB + at * BLK, BLK), BLK) for at in starts]
             keys = jnp.concatenate([kl[r, :] for r in rows] + [kl[rows[0], :]], axis=0)
             values = jnp.concatenate([vl[r, :] for r in rows] + [vl[rows[0], :]], axis=0).T
-            scores = scores_of(keys, ql[i])
-
+            ready.append((i, scores_of(keys, ql[i]), values, valid))
+        for i, scores, values, valid in ready:
             def load(t):
                 if t == 3:
                     return jnp.full((BLK, 256), NEGATIVE, jnp.float32)
@@ -399,29 +416,37 @@
     place = jnp.stack([x * 4 + z, y, jnp.where(c == 0, x, z), jnp.where(c == 0, z, x), c]).astype(jnp.int32)
     kv = call(kv_kernel, [bf16(SLAB, 256)] * 4, [place], [keys, values], 1e6, 4)
     kv = [kv[0]] + [along_y(kv[by], by) for by in (1, 2, 3)]
-    q = call(q_kernel, [bf16(SLAB, 512)] * 4, [place, vertical], [queries], 1e6, 4)
+    q = call(q_kernel, [bf16(SLAB, 512)] * 4, [place], [queries], 1e6, 4)
     q = [q[0]] + [along_y(q[by], by) for by in (1, 2, 3)]
-    own, last = call(slots_kernel, [bf16(1024, 128), bf16(SLAB, 256)], [place, vertical], kv, 1e6, 4)
+    own, last, table = pl.pallas_call(
+        slots_kernel,
+        out_shape=[bf16(1024, 128), bf16(SLAB, 256), jax.ShapeDtypeStruct((128,), jnp.int32)],
+        in_specs=[SMEM] * 3 + [VMEM] * 4,
+        out_specs=[VMEM, VMEM, SMEM],
+        compiler_params=pltpu.CompilerParams(vmem_limit_bytes=4 * MIB),
+        cost_estimate=pl.CostEstimate(flops=10**6, bytes_accessed=10**6, transcendentals=0),
+        name="slots",
+    )(place, vertical, slash, *kv)
     hops = [first_hop(own, by) for by in (1, 2, 3)]
     prev = to_next_group(last)
     near = call(join_kernel, [bf16(4096, 128)], [], [own, *hops], 1e6, 4)[0]
     plus, minus = second_hop(near, 1), second_hop(near, 3)
     beyond = [second_hop(plus[:2048], 1), second_hop(minus[2048:], 3)]
     ql, *state = call(
-        local_kernel, [bf16(16, 256, 128)] + STATE, [place, vertical, slash], [*q, *kv, prev], 3e9, 6,
+        local_kernel, [bf16(16, 256, 128)] + STATE, [table], [*q, *kv, prev], 3e9, 6,
         [pltpu.VMEM((5 * SLAB, 128), jnp.bfloat16)] * 2,
     )
     state = call(
-        functools.partial(part_kernel, 0), PACKED + STATE, [place, vertical],
-        [near, ql, *state], 5e9, 8, WORK, {4 + n: 2 + n for n in range(3)},
+        functools.partial(part_kernel, 0), PACKED + STATE, [table],
+        [near, ql, *state], 5e9, 8, WORK, {3 + n: 2 + n for n in range(3)},
     )
     state = call(
-        functools.partial(part_kernel, 1), PACKED + STATE, [place, vertical],
-        [plus, minus, ql, *state], 1e10, 8, WORK, {5 + n: n for n in range(5)},
+        functools.partial(part_kernel, 1), PACKED + STATE, [table],
+        [plus, minus, ql, *state], 1e10, 8, WORK, {4 + n: n for n in range(5)},
     )
     state = call(
         functools.partial(part_kernel, 2), PACKED + STATE + [bf16(SLAB, 512)] * 4,
-        [place, vertical], [*beyond, ql, *state], 5e9, 8, WORK, {5 + n: n for n in range(5)},
+        [table], [*beyond, ql, *state], 5e9, 8, WORK, {4 + n: n for n in range(5)},
     )
     attention = state[5:]
     back = [attention[0]] + [along_y(attention[by], -by) for by in (1, 2, 3)]

time: 125 us -> 109 us (0.87)
  the two profiles are of different devices: /device:TPU:1 before, /device:TPU:37 now
where the time goes in v2:
time: 109 us
  Pallas kernels  47.4 us (43%)
  waiting for transfers between devices  31.4 us (29%)
  starting transfers between devices  25.2 us (23%)
  local copies, waits for them, and re-layouts  3.59 us (3%)
  other arithmetic  1.22 us (1%)
    pallas_call x12, Pallas kernels, call(): pl.pallas_call(kernel, out_shape=outs, in_specs=[SMEM] * len(scalars) + [...  45.8 us
    ppermute x18, waiting for transfers between devices, moved(): return lax.ppermute(value, ALL, pairs)  31.4 us
    ppermute x18, starting transfers between devices, moved(): return lax.ppermute(value, ALL, pairs)  25.2 us
    unnamed x17, local copies, waits for them, and re-layouts  3.44 us
  transfers between devices with their start and end apart: 18, of which 11 were waited for; matrix products, arithmetic and copies ran while one was open for 1% of the time, Pallas kernels for 20%

profile of v2, /device:TPU:37, one launch (start us, length us, event | category | flops | bytes accessed | tf_op | source)
XLA Modules:
  0.0 108.9 jit_solution(4273795653800394426)
XLA Ops:
  0.0 0.1 stack.23.place_ref
  0.1 1.0 copy-done.1
  1.1 0.9 copy-done.2
  2.1 0.6 shard_map.64
  2.7 1.4 %collective-permute-start = (bf16[256,256]{1,0:T(8,128)(2,1)S(1)}, bf16[256,256]{1,0:T(8,128)(2,1)S(1)}, u32[]{:S(2)}, u32[]{:S(2)}) collective-permute-start(bf16[256,256]{1,0:T(8,128)(2,1)S(1)} %get-tuple-element.35), channel_id=1, source_target_pairs={{0,2},{1,3},{2,4},{3,5},{4,6},{5,7},{6,0},{7,1},{8,10},{9,11},{10,... | collective-permute-start | bytes 393224 | tf_op jit(solution)/shard_map/ppermute | solution.py:32
  4.1 2.6 %collective-permute-start.1 = (bf16[256,256]{1,0:T(8,128)(2,1)S(1)}, bf16[256,256]{1,0:T(8,128)(2,1)S(1)}, u32[]{:S(2)}, u32[]{:S(2)}) collective-permute-start(bf16[256,256]{1,0:T(8,128)(2,1)S(1)} %get-tuple-element.36), channel_id=1, source_target_pairs={{0,4},{1,5},{2,6},{3,7},{4,0},{5,1},{6,2},{7,3},{8,12},{9,13},{10,... | collective-permute-start | bytes 393224 | tf_op jit(solution)/shard_map/ppermute | solution.py:32
  6.7 1.1 collective-permute-start.2
  7.8 0.8 copy.22.slash_ref
  8.5 0.0 collective-permute-done.kv1
  8.5 3.9 %collective-permute-done.1.kv2 = bf16[256,256]{1,0:T(8,128)(2,1)S(1)} collective-permute-done((bf16[256,256]{1,0:T(8,128)(2,1)S(1)}, bf16[256,256]{1,0:T(8,128)(2,1)S(1)}, u32[]{:S(2)}, u32[]{:S(2)}) %collective-permute-start.1) | collective-permute-done | bytes 131104 | tf_op jit(solution)/shard_map/ppermute | solution.py:32
  12.4 0.0 collective-permute-done.2.kv3
  12.4 0.7 copy-done.3
  13.1 1.5 %slots.1 = (bf16[1024,128]{1,0:T(8,128)(2,1)S(1)}, bf16[256,256]{1,0:T(8,128)(2,1)S(1)}, s32[128]{0:T(128)S(1)}) custom-call(s32[5]{0:T(128)S(1)} %stack.23.place_ref, s32[4,64]{1,0:T(4,128)S(1)} %copy-done.3, s32[4,2]{1,0:T(4,128)S(1)} %copy.22.slash_ref, bf16[256,256]{1,0:T(8,128)(2,1)S(1)} %get-tuple-element.34.kv0, ...), custom_call_target="tpu_custom_call" | custom-call | flops 1000000 | bytes 1000000 | tf_op jit(solution)/shard_map/slots/pallas_call | solution.py:421
  14.7 1.7 %collective-permute-start.3 = (bf16[1024,128]{1,0:T(8,128)(2,1)S(1)}, bf16[1024,128]{1,0:T(8,128)(2,1)S(1)}, u32[]{:S(2)}, u32[]{:S(2)}) collective-permute-start(bf16[1024,128]{1,0:T(8,128)(2,1)S(1)} %get-tuple-element.39.a0), channel_id=1, source_target_pairs={{0,32},{1,9},{2,34},{3,11},{4,36},{5,13},{6,38},{7,15},{8,40},{9,1... | collective-permute-start | bytes 786440 | tf_op jit(solution)/shard_map/ppermute | solution.py:32
  16.4 1.2 %collective-permute-start.4 = (bf16[1024,128]{1,0:T(8,128)(2,1)S(1)}, bf16[1024,128]{1,0:T(8,128)(2,1)S(1)}, u32[]{:S(2)}, u32[]{:S(2)}) collective-permute-start(bf16[1024,128]{1,0:T(8,128)(2,1)S(1)} %get-tuple-element.39.a0), channel_id=1, source_target_pairs={{0,64},{1,17},{2,66},{3,19},{4,68},{5,21},{6,70},{7,23},{8,72},{9,... | collective-permute-start | bytes 786440 | tf_op jit(solution)/shard_map/ppermute | solution.py:32
  17.5 2.0 %collective-permute-start.5 = (bf16[1024,128]{1,0:T(8,128)(2,1)S(1)}, bf16[1024,128]{1,0:T(8,128)(2,1)S(1)}, u32[]{:S(2)}, u32[]{:S(2)}) collective-permute-start(bf16[1024,128]{1,0:T(8,128)(2,1)S(1)} %get-tuple-element.39.a0), channel_id=1, source_target_pairs={{0,96},{1,25},{2,98},{3,27},{4,100},{5,29},{6,102},{7,31},{8,104},... | collective-permute-start | bytes 786440 | tf_op jit(solution)/shard_map/ppermute | solution.py:32
  19.5 0.7 collective-permute-done.3.a1
  20.2 3.2 %collective-permute-done.4.a2 = bf16[1024,128]{1,0:T(8,128)(2,1)S(1)} collective-permute-done((bf16[1024,128]{1,0:T(8,128)(2,1)S(1)}, bf16[1024,128]{1,0:T(8,128)(2,1)S(1)}, u32[]{:S(2)}, u32[]{:S(2)}) %collective-permute-start.4) | collective-permute-done | bytes 262176 | tf_op jit(solution)/shard_map/ppermute | solution.py:32
  23.4 2.4 %collective-permute-done.5.a3 = bf16[1024,128]{1,0:T(8,128)(2,1)S(1)} collective-permute-done((bf16[1024,128]{1,0:T(8,128)(2,1)S(1)}, bf16[1024,128]{1,0:T(8,128)(2,1)S(1)}, u32[]{:S(2)}, u32[]{:S(2)}) %collective-permute-start.5) | collective-permute-done | bytes 262176 | tf_op jit(solution)/shard_map/ppermute | solution.py:32
  25.8 0.1 shard_map.65.refs_0_
  25.9 1.0 collective-permute-start.6
  26.9 0.5 collective-permute-start.8
  27.4 0.6 shard_map.66
  28.1 1.3 %collective-permute-start.10 = (bf16[256,512]{1,0:T(8,128)(2,1)S(1)}, bf16[256,512]{1,0:T(8,128)(2,1)S(1)}, u32[]{:S(2)}, u32[]{:S(2)}) collective-permute-start(bf16[256,512]{1,0:T(8,128)(2,1)S(1)} %get-tuple-element.41), channel_id=1, source_target_pairs={{0,2},{1,3},{2,4},{3,5},{4,6},{5,7},{6,0},{7,1},{8,10},{9,11},{10,... | collective-permute-start | bytes 786440 | tf_op jit(solution)/shard_map/ppermute | solution.py:32
  29.3 2.2 %collective-permute-start.11 = (bf16[256,512]{1,0:T(8,128)(2,1)S(1)}, bf16[256,512]{1,0:T(8,128)(2,1)S(1)}, u32[]{:S(2)}, u32[]{:S(2)}) collective-permute-start(bf16[256,512]{1,0:T(8,128)(2,1)S(1)} %get-tuple-element.42), channel_id=1, source_target_pairs={{0,4},{1,5},{2,6},{3,7},{4,0},{5,1},{6,2},{7,3},{8,12},{9,13},{10,... | collective-permute-start | bytes 786440 | tf_op jit(solution)/shard_map/ppermute | solution.py:32
  31.5 0.7 collective-permute-start.12
  32.3 2.7 %collective-permute-done.10.q1 = bf16[256,512]{1,0:T(8,128)(2,1)S(1)} collective-permute-done((bf16[256,512]{1,0:T(8,128)(2,1)S(1)}, bf16[256,512]{1,0:T(8,128)(2,1)S(1)}, u32[]{:S(2)}, u32[]{:S(2)}) %collective-permute-start.10) | collective-permute-done | bytes 262176 | tf_op jit(solution)/shard_map/ppermute | solution.py:32
  35.0 6.7 %collective-permute-done.11.q2 = bf16[256,512]{1,0:T(8,128)(2,1)S(1)} collective-permute-done((bf16[256,512]{1,0:T(8,128)(2,1)S(1)}, bf16[256,512]{1,0:T(8,128)(2,1)S(1)}, u32[]{:S(2)}, u32[]{:S(2)}) %collective-permute-start.11) | collective-permute-done | bytes 262176 | tf_op jit(solution)/shard_map/ppermute | solution.py:32
  41.6 0.2 collective-permute-done.12.q3
  41.8 3.3 %shard_map.67 = (bf16[16,256,128]{2,1,0:T(8,128)(2,1)S(1)}, f32[16,8,256]{2,1,0:T(8,128)S(1)}, f32[16,8,256]{2,1,0:T(8,128)S(1)}, f32[16,128,256]{2,1,0:T(8,128)S(1)}) custom-call(s32[128]{0:T(128)S(1)} %get-tuple-element.38.place_ref, bf16[256,512]{1,0:T(8,128)(2,1)S(1)} %get-tuple-element.40.q0, bf16[256,512]{1,0:T(8,128)(2,1)S(1)} %collective-permute-done.10.q1, ...), custom_call_target="tpu_custom_call" | custom-call | flops 3000000000 | bytes 1000000 | tf_op jit(solution)/shard_map/pallas_call | solution.py:402
  45.1 1.0 shard_map.68
  46.1 0.9 collective-permute-start.7
  47.1 3.8 %collective-permute-start.9 = (bf16[2048,128]{1,0:T(8,128)(2,1)S(1)}, bf16[2048,128]{1,0:T(8,128)(2,1)S(1)}, u32[]{:S(2)}, u32[]{:S(2)}) collective-permute-start(bf16[2048,128]{1,0:T(8,128)(2,1)S(1)} %slice.9), channel_id=1, source_target_pairs={{0,24},{1,97},{2,26},{3,99},{4,28},{5,101},{6,30},{7,103},{8,0},{9... | collective-permute-start | bytes 1572872 | tf_op jit(solution)/shard_map/ppermute | solution.py:32
  50.9 9.7 %shard_map.69 = (bf16[4096,128]{1,0:T(8,128)(2,1)S(1)}, bf16[4096,128]{1,0:T(8,128)(2,1)S(1)}, f32[16,8,256]{2,1,0:T(8,128)S(1)}, f32[16,8,256]{2,1,0:T(8,128)S(1)}, f32[16,128,256]{2,1,0:T(8,128)S(1)}) custom-call(s32[128]{0:T(128)S(1)} %get-tuple-element.38.place_ref, ...), custom_call_target="tpu_custom_call", output_to_operand_aliasing={{0}: (4, {}), {1}: (5, {}), {2}: (6, {}), {3}: (7, {}), {4}... | custom-call | flops 10000000000 | bytes 1000000 | tf_op jit(solution)/shard_map/pallas_call | solution.py:402
  60.6 4.4 %collective-permute-done.9.refs_1_ = bf16[2048,128]{1,0:T(8,128)(2,1)S(1)} collective-permute-done((bf16[2048,128]{1,0:T(8,128)(2,1)S(1)}, bf16[2048,128]{1,0:T(8,128)(2,1)S(1)}, u32[]{:S(2)}, u32[]{:S(2)}) %collective-permute-start.9) | collective-permute-done | bytes 524320 | tf_op jit(solution)/shard_map/ppermute | solution.py:32
  65.0 22.6 %shard_map.70 = (bf16[4096,128]{1,0:T(8,128)(2,1)S(1)}, bf16[4096,128]{1,0:T(8,128)(2,1)S(1)}, f32[16,8,256]{2,1,0:T(8,128)S(1)}, f32[16,8,256]{2,1,0:T(8,128)S(...) custom-call(s32[128]{0:T(128)S(1)} %get-tuple-element.38.place_ref, ...), custom_call_target="tpu_custom_call", output_to_operand_aliasing={{0}: (4, {}), {1}: (5, {}), {2}: (6, {}), {3}: (7, {}), {4}... | custom-call | flops 5000000000 | bytes 1000000 | tf_op jit(solution)/shard_map/pallas_call | solution.py:402
  87.6 3.5 %collective-permute-start.16 = (bf16[256,512]{1,0:T(8,128)(2,1)S(1)}, bf16[256,512]{1,0:T(8,128)(2,1)S(1)}, u32[]{:S(2)}, u32[]{:S(2)}) collective-permute-start(bf16[256,512]{1,0:T(8,128)(2,1)S(1)} %get-tuple-element.61), channel_id=1, source_target_pairs={{0,6},{1,7},{2,0},{3,1},{4,2},{5,3},{6,4},{7,5},{8,14},{9,15},{10,... | collective-permute-start | bytes 786440 | tf_op jit(solution)/shard_map/ppermute | solution.py:32
  91.1 1.3 %collective-permute-start.14 = (bf16[256,512]{1,0:T(8,128)(2,1)S(1)}, bf16[256,512]{1,0:T(8,128)(2,1)S(1)}, u32[]{:S(2)}, u32[]{:S(2)}) collective-permute-start(bf16[256,512]{1,0:T(8,128)(2,1)S(1)} %get-tuple-element.59), channel_id=1, source_target_pairs={{0,4},{1,5},{2,6},{3,7},{4,0},{5,1},{6,2},{7,3},{8,12},{9,13},{10,... | collective-permute-start | bytes 786440 | tf_op jit(solution)/shard_map/ppermute | solution.py:32
  92.4 1.8 %shard_map.71.total_in = f32[256,4096]{1,0:T(8,128)S(1)} custom-call(s32[5]{0:T(128)S(1)} %stack.23.place_ref, bf16[256,512]{1,0:T(8,128)(2,1)S(1)} %get-tuple-element.62.a, bf16[2048,4096]{1,0:T(8,128)(2,1)S(1)} %bitcast.6), custom_call_target="tpu_custom_call" | custom-call | flops 1000000000 | bytes 1000000 | tf_op jit(solution)/shard_map/pallas_call | solution.py:402
  94.2 5.4 %collective-permute-done.16.a = bf16[256,512]{1,0:T(8,128)(2,1)S(1)} collective-permute-done((bf16[256,512]{1,0:T(8,128)(2,1)S(1)}, bf16[256,512]{1,0:T(8,128)(2,1)S(1)}, u32[]{:S(2)}, u32[]{:S(2)}) %collective-permute-start.16) | collective-permute-done | bytes 262176 | tf_op jit(solution)/shard_map/ppermute | solution.py:32
  99.6 1.8 %shard_map.72.total_in = f32[256,4096]{1,0:T(8,128)S(1)} custom-call(s32[5]{0:T(128)S(1)} %stack.23.place_ref, bf16[256,512]{1,0:T(8,128)(2,1)S(1)} %collective-permute-done.16.a, bf16[2048,4096]{1,0:T(8,128)(2,1)S(1)} %bitcast.6, f32[256,4096]{1,0:T(8,128)S(1)} %shard_map.71.total_in), custom_call_target="tpu_custom_call", output_to_operand_aliasing={{}: (3, {})} | custom-call | flops 1000000000 | bytes 1000000 | tf_op jit(solution)/shard_map/pallas_call | solution.py:402
  101.4 0.4 collective-permute-done.15.a
  101.9 1.8 %shard_map.73.total_ref = f32[256,4096]{1,0:T(8,128)S(1)} custom-call(s32[5]{0:T(128)S(1)} %stack.23.place_ref, bf16[256,512]{1,0:T(8,128)(2,1)S(1)} %collective-permute-done.15.a, bf16[2048,4096]{1,0:T(8,128)(2,1)S(1)} %bitcast.6, f32[256,4096]{1,0:T(8,128)S(1)} %shard_map.72.total_in), custom_call_target="tpu_custom_call", output_to_operand_aliasing={{}: (3, {})} | custom-call | flops 1000000000 | bytes 1000000 | tf_op jit(solution)/shard_map/pallas_call | solution.py:402
  103.7 1.3 %shard_map.75 = bf16[128,4096]{1,0:T(8,128)(2,1)S(1)} custom-call(s32[5]{0:T(128)S(1)} %stack.23.place_ref, bf16[256,512]{1,0:T(8,128)(2,1)S(1)} %collective-permute-done.14.a, bf16[2048,4096]{1,0:T(8,128)(2,1)S(1)} %bitcast.6, f32[256,4096]{1,0:T(8,128)S(1)} %shard_map.73.total_ref), custom_call_target="tpu_custom_call" | custom-call | flops 1000000000 | bytes 1000000 | tf_op jit(solution)/shard_map/pallas_call | solution.py:402
  105.0 0.1 collective-permute-start.17
  105.1 1.3 %shard_map.74 = f32[128,4096]{1,0:T(8,128)S(1)} custom-call(s32[5]{0:T(128)S(1)} %stack.23.place_ref, bf16[256,512]{1,0:T(8,128)(2,1)S(1)} %collective-permute-done.14.a, bf16[2048,4096]{1,0:T(8,128)(2,1)S(1)} %bitcast.6, f32[256,4096]{1,0:T(8,128)S(1)} %shard_map.73.total_ref), custom_call_target="tpu_custom_call" | custom-call | flops 1000000000 | bytes 1000000 | tf_op jit(solution)/shard_map/pallas_call | solution.py:402
  106.4 1.4 %collective-permute-done.17 = bf16[128,4096]{1,0:T(8,128)(2,1)S(1)} collective-permute-done((bf16[128,4096]{1,0:T(8,128)(2,1)S(1)}, bf16[128,4096]{1,0:T(8,128)(2,1)S(1)}, u32[]{:S(2)}, u32[]{:S(2)}) %collective-permute-start.17) | collective-permute-done | bytes 1048608 | tf_op jit(solution)/shard_map/ppermute | solution.py:32
  107.7 1.2 %add_convert_fusion = bf16[128,4096]{1,0:T(8,128)(2,1)} fusion(f32[128,4096]{1,0:T(8,128)S(1)} %shard_map.74, bf16[128,4096]{1,0:T(8,128)(2,1)S(1)} %collective-permute-done.17), kind=kLoop, calls=%fused_computation | loop fusion | flops 1572864 | bytes 4194304 | tf_op jit(solution)/shard_map/convert_element_type | solution.py:467
  (23 shorter events, 0.1 us)
Async XLA Ops:
  0.0 27.4 %copy-start = (bf16[256,2048]{1,0:T(8,128)(2,1)S(1)}, bf16[256,2048]{1,0:T(8,128)(2,1)}, u32[]{:S(2)}) copy-start(bf16[256,2048]{1,0:T(8,128)(2,1)} %queries_ref.1) | copy-start | bytes 3145732
  0.1 1.0 copy-start.1
  1.1 0.9 copy-start.2
  2.7 5.8 %collective-permute-start = (bf16[256,256]{1,0:T(8,128)(2,1)S(1)}, bf16[256,256]{1,0:T(8,128)(2,1)S(1)}, u32[]{:S(2)}, u32[]{:S(2)}) collective-permute-start(bf16[256,256]{1,0:T(8,128)(2,1)S(1)} %get-tuple-element.35), channel_id=1, source_target_pairs={{0,2},{1,3},{2,4},{3,5},{4,6},{5,7},{6,0},{7,1},{8,10},{9,11},{10,... | collective-permute-start | bytes 393224 | tf_op jit(solution)/shard_map/ppermute | solution.py:32
  4.1 8.3 %collective-permute-start.1 = (bf16[256,256]{1,0:T(8,128)(2,1)S(1)}, bf16[256,256]{1,0:T(8,128)(2,1)S(1)}, u32[]{:S(2)}, u32[]{:S(2)}) collective-permute-start(bf16[256,256]{1,0:T(8,128)(2,1)S(1)} %get-tuple-element.36), channel_id=1, source_target_pairs={{0,4},{1,5},{2,6},{3,7},{4,0},{5,1},{6,2},{7,3},{8,12},{9,13},{10,... | collective-permute-start | bytes 393224 | tf_op jit(solution)/shard_map/ppermute | solution.py:32
  6.7 5.7 %collective-permute-start.2 = (bf16[256,256]{1,0:T(8,128)(2,1)S(1)}, bf16[256,256]{1,0:T(8,128)(2,1)S(1)}, u32[]{:S(2)}, u32[]{:S(2)}) collective-permute-start(bf16[256,256]{1,0:T(8,128)(2,1)S(1)} %get-tuple-element.37), channel_id=1, source_target_pairs={{0,6},{1,7},{2,0},{3,1},{4,2},{5,3},{6,4},{7,5},{8,14},{9,15},{10,... | collective-permute-start | bytes 393224 | tf_op jit(solution)/shard_map/ppermute | solution.py:32
  12.4 0.7 copy-start.3
  14.7 5.6 %collective-permute-start.3 = (bf16[1024,128]{1,0:T(8,128)(2,1)S(1)}, bf16[1024,128]{1,0:T(8,128)(2,1)S(1)}, u32[]{:S(2)}, u32[]{:S(2)}) collective-permute-start(bf16[1024,128]{1,0:T(8,128)(2,1)S(1)} %get-tuple-element.39.a0), channel_id=1, source_target_pairs={{0,32},{1,9},{2,34},{3,11},{4,36},{5,13},{6,38},{7,15},{8,40},{9,1... | collective-permute-start | bytes 786440 | tf_op jit(solution)/shard_map/ppermute | solution.py:32
  16.4 7.1 %collective-permute-start.4 = (bf16[1024,128]{1,0:T(8,128)(2,1)S(1)}, bf16[1024,128]{1,0:T(8,128)(2,1)S(1)}, u32[]{:S(2)}, u32[]{:S(2)}) collective-permute-start(bf16[1024,128]{1,0:T(8,128)(2,1)S(1)} %get-tuple-element.39.a0), channel_id=1, source_target_pairs={{0,64},{1,17},{2,66},{3,19},{4,68},{5,21},{6,70},{7,23},{8,72},{9,... | collective-permute-start | bytes 786440 | tf_op jit(solution)/shard_map/ppermute | solution.py:32
  17.5 8.3 %collective-permute-start.5 = (bf16[1024,128]{1,0:T(8,128)(2,1)S(1)}, bf16[1024,128]{1,0:T(8,128)(2,1)S(1)}, u32[]{:S(2)}, u32[]{:S(2)}) collective-permute-start(bf16[1024,128]{1,0:T(8,128)(2,1)S(1)} %get-tuple-element.39.a0), channel_id=1, source_target_pairs={{0,96},{1,25},{2,98},{3,27},{4,100},{5,29},{6,102},{7,31},{8,104},... | collective-permute-start | bytes 786440 | tf_op jit(solution)/shard_map/ppermute | solution.py:32
  19.5 12.1 %collective-permute-start.13 = (bf16[256,256]{1,0:T(8,128)(2,1)S(1)}, bf16[256,256]{1,0:T(8,128)(2,1)S(1)}, u32[]{:S(2)}, u32[]{:S(2)}) collective-permute-start(bf16[256,256]{1,0:T(8,128)(2,1)S(1)} %get-tuple-element.44), channel_id=1, source_target_pairs={{0,8},{1,9},{2,10},{3,11},{4,12},{5,13},{6,14},{7,15},{8,16},{9,17... | collective-permute-start | bytes 393224 | tf_op jit(solution)/shard_map/ppermute | solution.py:32
  25.9 20.2 %collective-permute-start.6 = (bf16[4096,128]{1,0:T(8,128)(2,1)S(1)}, bf16[4096,128]{1,0:T(8,128)(2,1)S(1)}, u32[]{:S(2)}, u32[]{:S(2)}) collective-permute-start(bf16[4096,128]{1,0:T(8,128)(2,1)S(1)} %shard_map.65.refs_0_), channel_id=1, source_target_pairs={{0,8},{1,33},{2,10},{3,35},{4,12},{5,37},{6,14},{7,39},{8,16},{9,4... | collective-permute-start | bytes 3145736 | tf_op jit(solution)/shard_map/ppermute | solution.py:32
  26.9 20.2 %collective-permute-start.8 = (bf16[4096,128]{1,0:T(8,128)(2,1)S(1)}, bf16[4096,128]{1,0:T(8,128)(2,1)S(1)}, u32[]{:S(2)}, u32[]{:S(2)}) collective-permute-start(bf16[4096,128]{1,0:T(8,128)(2,1)S(1)} %shard_map.65.refs_0_), channel_id=1, source_target_pairs={{0,24},{1,97},{2,26},{3,99},{4,28},{5,101},{6,30},{7,103},{8,0},{9... | collective-permute-start | bytes 3145736 | tf_op jit(solution)/shard_map/ppermute | solution.py:32
  28.1 6.9 %collective-permute-start.10 = (bf16[256,512]{1,0:T(8,128)(2,1)S(1)}, bf16[256,512]{1,0:T(8,128)(2,1)S(1)}, u32[]{:S(2)}, u32[]{:S(2)}) collective-permute-start(bf16[256,512]{1,0:T(8,128)(2,1)S(1)} %get-tuple-element.41), channel_id=1, source_target_pairs={{0,2},{1,3},{2,4},{3,5},{4,6},{5,7},{6,0},{7,1},{8,10},{9,11},{10,... | collective-permute-start | bytes 786440 | tf_op jit(solution)/shard_map/ppermute | solution.py:32
  29.3 12.3 %collective-permute-start.11 = (bf16[256,512]{1,0:T(8,128)(2,1)S(1)}, bf16[256,512]{1,0:T(8,128)(2,1)S(1)}, u32[]{:S(2)}, u32[]{:S(2)}) collective-permute-start(bf16[256,512]{1,0:T(8,128)(2,1)S(1)} %get-tuple-element.42), channel_id=1, source_target_pairs={{0,4},{1,5},{2,6},{3,7},{4,0},{5,1},{6,2},{7,3},{8,12},{9,13},{10,... | collective-permute-start | bytes 786440 | tf_op jit(solution)/shard_map/ppermute | solution.py:32
  31.5 10.3 %collective-permute-start.12 = (bf16[256,512]{1,0:T(8,128)(2,1)S(1)}, bf16[256,512]{1,0:T(8,128)(2,1)S(1)}, u32[]{:S(2)}, u32[]{:S(2)}) collective-permute-start(bf16[256,512]{1,0:T(8,128)(2,1)S(1)} %get-tuple-element.43), channel_id=1, source_target_pairs={{0,6},{1,7},{2,0},{3,1},{4,2},{5,3},{6,4},{7,5},{8,14},{9,15},{10,... | collective-permute-start | bytes 786440 | tf_op jit(solution)/shard_map/ppermute | solution.py:32
  46.1 14.4 %collective-permute-start.7 = (bf16[2048,128]{1,0:T(8,128)(2,1)S(1)}, bf16[2048,128]{1,0:T(8,128)(2,1)S(1)}, u32[]{:S(2)}, u32[]{:S(2)}) collective-permute-start(bf16[2048,128]{1,0:T(8,128)(2,1)S(1)} %slice.8), channel_id=1, source_target_pairs={{0,8},{1,33},{2,10},{3,35},{4,12},{5,37},{6,14},{7,39},{8,16},{9,4... | collective-permute-start | bytes 1572872 | tf_op jit(solution)/shard_map/ppermute | solution.py:32
  47.1 17.9 %collective-permute-start.9 = (bf16[2048,128]{1,0:T(8,128)(2,1)S(1)}, bf16[2048,128]{1,0:T(8,128)(2,1)S(1)}, u32[]{:S(2)}, u32[]{:S(2)}) collective-permute-start(bf16[2048,128]{1,0:T(8,128)(2,1)S(1)} %slice.9), channel_id=1, source_target_pairs={{0,24},{1,97},{2,26},{3,99},{4,28},{5,101},{6,30},{7,103},{8,0},{9... | collective-permute-start | bytes 1572872 | tf_op jit(solution)/shard_map/ppermute | solution.py:32
  50.9 41.5 %slice-start = ((s8[16777216]{0:T(1024)(128)(4,1)}), s8[4194304]{0:T(1024)(128)(4,1)S(1)}, s32[]{:S(2)}) async-start(s8[16777216]{0:T(1024)(128)(4,1)} %bitcast.5), calls=%async_computation | async-start | bytes 8388608
  50.9 41.5 %slice-start.1 = ((s8[16777216]{0:T(1024)(128)(4,1)}), s8[4194304]{0:T(1024)(128)(4,1)S(1)}, s32[]{:S(2)}) async-start(s8[16777216]{0:T(1024)(128)(4,1)} %bitcast.5), calls=%async_computation.1 | async-start | bytes 8388608
  50.9 41.5 %slice-start.2 = ((s8[16777216]{0:T(1024)(128)(4,1)}), s8[4194304]{0:T(1024)(128)(4,1)S(1)}, s32[]{:S(2)}) async-start(s8[16777216]{0:T(1024)(128)(4,1)} %bitcast.5), calls=%async_computation.2 | async-start | bytes 8388608
  65.0 27.4 %slice-start.3 = ((s8[16777216]{0:T(1024)(128)(4,1)}), s8[4194304]{0:T(1024)(128)(4,1)S(1)}, s32[]{:S(2)}) async-start(s8[16777216]{0:T(1024)(128)(4,1)} %bitcast.5), calls=%async_computation.3 | async-start | bytes 8388608
  87.6 12.0 %collective-permute-start.16 = (bf16[256,512]{1,0:T(8,128)(2,1)S(1)}, bf16[256,512]{1,0:T(8,128)(2,1)S(1)}, u32[]{:S(2)}, u32[]{:S(2)}) collective-permute-start(bf16[256,512]{1,0:T(8,128)(2,1)S(1)} %get-tuple-element.61), channel_id=1, source_target_pairs={{0,6},{1,7},{2,0},{3,1},{4,2},{5,3},{6,4},{7,5},{8,14},{9,15},{10,... | collective-permute-start | bytes 786440 | tf_op jit(solution)/shard_map/ppermute | solution.py:32
  91.1 10.8 %collective-permute-start.15 = (bf16[256,512]{1,0:T(8,128)(2,1)S(1)}, bf16[256,512]{1,0:T(8,128)(2,1)S(1)}, u32[]{:S(2)}, u32[]{:S(2)}) collective-permute-start(bf16[256,512]{1,0:T(8,128)(2,1)S(1)} %get-tuple-element.60), channel_id=1, source_target_pairs={{0,2},{1,3},{2,4},{3,5},{4,6},{5,7},{6,0},{7,1},{8,10},{9,11},{10,... | collective-permute-start | bytes 786440 | tf_op jit(solution)/shard_map/ppermute | solution.py:32
  91.1 12.6 %collective-permute-start.14 = (bf16[256,512]{1,0:T(8,128)(2,1)S(1)}, bf16[256,512]{1,0:T(8,128)(2,1)S(1)}, u32[]{:S(2)}, u32[]{:S(2)}) collective-permute-start(bf16[256,512]{1,0:T(8,128)(2,1)S(1)} %get-tuple-element.59), channel_id=1, source_target_pairs={{0,4},{1,5},{2,6},{3,7},{4,0},{5,1},{6,2},{7,3},{8,12},{9,13},{10,... | collective-permute-start | bytes 786440 | tf_op jit(solution)/shard_map/ppermute | solution.py:32
  105.0 2.7 %collective-permute-start.17 = (bf16[128,4096]{1,0:T(8,128)(2,1)S(1)}, bf16[128,4096]{1,0:T(8,128)(2,1)S(1)}, u32[]{:S(2)}, u32[]{:S(2)}) collective-permute-start(bf16[128,4096]{1,0:T(8,128)(2,1)S(1)} %shard_map.75), channel_id=1, source_target_pairs={{0,1},{1,0},{2,3},{3,2},{4,5},{5,4},{6,7},{7,6},{8,9},{9,8},{10,11... | collective-permute-start | bytes 3145736 | tf_op jit(solution)/shard_map/ppermute | solution.py:32

commit v3 on v2

--- a/solution.py
+++ b/solution.py
@@ -78,7 +78,7 @@
     for n in range(5):
         table_ref[n] = place_ref[n]
     for n in range(2):
-        table_ref[SLASH + n] = slash_ref[y, n]
+        table_ref[SLASH + n] = slash_ref[n, y]
     for n in range(NV):
         table_ref[VERT + n] = vert_ref[y, n]
     for by, kv in enumerate((kv0, kv1, kv2, kv3)):
@@ -106,6 +106,7 @@
 
 CHUNK = 1024
 HALF = 512
+EVERY = (0, 1, 2, 3)
 
 
 def scores_of(keys, q):
@@ -188,9 +189,16 @@
     return at
 
 
-def chunks(size, unroll, place_ref, order, begin, count, ql, kc, vc, top, tot, acc, vt_ref, sa_ref, sb_ref, ma, mb):
+def chunks(size, unroll, picks, place_ref, order, begin, count, ql, kc, vc, top, tot, acc, vt_ref, sa_ref, sb_ref, ma, mb):
     pieces = size // BLK
     vt, sa, sb = vt_ref.at[:, 0:size], sa_ref.at[0:size, :], sb_ref.at[0:size, :]
+
+    total = 4 * len(picks)
+
+    def query(m):
+        if len(picks) == 4:
+            return m
+        return jnp.where(m < 4, 4 * picks[0], 4 * picks[1]) + m % 4
 
     def one_chunk(n, carry):
         first = begin + n * pieces
@@ -220,20 +228,20 @@
                 else:
                     weigh(i, plain, pieces, eight[...], vt[...], top, tot, acc)
 
-            score(0, sa, ma)
-            score(1, sb, mb)
+            score(query(0), sa, ma)
+            score(query(1), sb, mb)
             each = 1 if masked else unroll
 
             def some(j, carry):
                 for u in range(each):
-                    i = 2 * (j * each + u)
-                    finish(i, sa, ma)
-                    score((i + 2) % 16, sa, ma)
-                    finish(i + 1, sb, mb)
-                    score((i + 3) % 16, sb, mb)
+                    m = 2 * (j * each + u)
+                    finish(query(m), sa, ma)
+                    score(query((m + 2) % total), sa, ma)
+                    finish(query(m + 1), sb, mb)
+                    score(query((m + 3) % total), sb, mb)
                 return carry
 
-            lax.fori_loop(0, 8 // each, some, 0)
+            lax.fori_loop(0, total // (2 * each), some, 0)
 
         free = last < place_ref[0] * 16
         pl.when(free)(lambda: run(False))
@@ -243,16 +251,16 @@
     lax.fori_loop(0, count, one_chunk, 0)
 
 
-def part_kernel(stage, place_ref, *refs):
-    splits = ((1,), (1, 1), (2,))[stage]
+def part_kernel(stage, picks, place_ref, *refs):
+    splits = ((1,), (1, 1), (2,), ())[stage]
     sources, refs = refs[: sum(splits)], refs[sum(splits) :]
     ql = refs[0]
     refs = refs[6:] if stage else refs[4:]
-    final = stage == 2
-    outs = refs[5:9] if final else None
-    bounds, order = refs[9:11] if final else refs[5:7]
-    work = (ql, *refs[:5], *(refs[11:] if final else refs[7:]))
-    kc, vc, _, tot, acc = refs[:5]
+    kc, vc, top, tot, acc = refs[:5]
+    final = stage >= 2
+    outs, refs = (refs[5 : 5 + len(picks)], refs[5 + len(picks) :]) if final else (None, refs[5:])
+    bounds, order = refs[:2]
+    work = (ql, kc, vc, top, tot, acc, *refs[2:])
     find_bounds(place_ref, bounds)
 
     def add(outer, at, fresh):
@@ -261,35 +269,34 @@
     near = add(0, jnp.int32(0), sources if stage == 0 else None)
     begin = near // 8 * 8
     if stage == 0:
-        chunks(HALF, 2, place_ref, order, jnp.int32(0), near // 8, *work)
-    else:
-        at = add(1, near, sources[:1] if stage == 1 else None)
-        at = add(3, at, sources[1:] if stage == 1 else None)
-        whole = (at - begin) // 16
-        if stage == 1:
-            chunks(CHUNK, 2, place_ref, order, begin, whole, *work)
-        else:
-            at = add(2, at, sources)
-            begin = begin + whole * 16
-            left = (at - begin) // 16
-            chunks(CHUNK, 2, place_ref, order, begin, left, *work)
-            begin = begin + left * 16
-            left = (at - begin + 7) // 8
-
-            def clear(n, carry):
-                order[n] = NEVER
-                vc[pl.ds(pl.multiple_of(n * BLK, BLK), BLK), :] = jnp.zeros((BLK, 128), jnp.bfloat16)
-                return carry
-
-            lax.fori_loop(at, begin + left * 8, clear, 0)
-            chunks(HALF, 1, place_ref, order, begin, left, *work)
-    if final:
-        for by in range(4):
-            for block in range(4):
-                i = by * 4 + block
-                o = (acc[i] / jnp.sum(tot[i], axis=0, keepdims=True)).T.astype(jnp.bfloat16)
-                for g in range(4):
-                    outs[by][block * BLK : (block + 1) * BLK, g * 128 : (g + 1) * 128] = o[g * BLK : (g + 1) * BLK, :]
+        chunks(HALF, 2, picks, place_ref, order, jnp.int32(0), near // 8, *work)
+        return
+    at = add(1, near, sources[:1] if stage == 1 else None)
+    at = add(3, at, sources[1:] if stage == 1 else None)
+    whole = (at - begin) // 16
+    if stage == 1:
+        chunks(CHUNK, 2, picks, place_ref, order, begin, whole, *work)
+        return
+    at = add(2, at, sources if stage == 2 else None)
+    begin = begin + whole * 16
+    whole = (at - begin) // 16
+    rest = begin + whole * 16
+    left = (at - rest + 7) // 8
+
+    def clear(n, carry):
+        order[n] = NEVER
+        vc[pl.ds(pl.multiple_of(n * BLK, BLK), BLK), :] = jnp.zeros((BLK, 128), jnp.bfloat16)
+        return carry
+
+    lax.fori_loop(at, rest + left * 8, clear, 0)
+    chunks(CHUNK, 2, picks, place_ref, order, begin, whole, *work)
+    chunks(HALF, 1, picks, place_ref, order, rest, left, *work)
+    for out, by in zip(outs, picks):
+        for block in range(4):
+            i = by * 4 + block
+            o = (acc[i] / jnp.sum(tot[i], axis=0, keepdims=True)).T.astype(jnp.bfloat16)
+            for g in range(4):
+                out[block * BLK : (block + 1) * BLK, g * 128 : (g + 1) * 128] = o[g * BLK : (g + 1) * BLK, :]
 
 
 def local_kernel(
@@ -339,38 +346,26 @@
     lax.fori_loop(0, 4, some, 0)
 
 
-def project(place_ref, a, weight_ref, by, rows, keep):
-    head = (place_ref[1] + by) % 4
-    depth = pl.ds(pl.multiple_of(head * 512, 512), 512)
-
+def early_kernel(place_ref, a0, a1, a2, weight_ref, total_ref):
     for n in range(8):
         columns = slice(n * 512, (n + 1) * 512)
-        keep(columns, jnp.dot(a[rows, :], weight_ref[depth, columns], preferred_element_type=jnp.float32))
-
-
-def first_piece_kernel(place_ref, a, weight_ref, total_ref):
-    def keep(columns, product):
-        total_ref[:, columns] = product
-
-    project(place_ref, a, weight_ref, 0, slice(None), keep)
-
-
-def next_piece_kernel(by, place_ref, a, weight_ref, total_in, total_ref):
-    def keep(columns, product):
-        total_ref[:, columns] = total_ref[:, columns] + product
-
-    project(place_ref, a, weight_ref, by, slice(None), keep)
-
-
-def last_piece_kernel(by, mine, place_ref, a, weight_ref, total_ref, out_ref):
+        total = None
+        for by, a in enumerate((a0, a1, a2)):
+            depth = pl.ds(pl.multiple_of((place_ref[1] + by) % 4 * 512, 512), 512)
+            part = jnp.dot(a[...], weight_ref[depth, columns], preferred_element_type=jnp.float32)
+            total = part if total is None else total + part
+        total_ref[:, columns] = total
+
+
+def last_kernel(mine, place_ref, a, weight_ref, total_ref, out_ref):
     core = place_ref[4]
     half = core if mine else 1 - core
     rows = pl.ds(pl.multiple_of(half * 128, 128), 128)
-
-    def keep(columns, product):
-        out_ref[:, columns] = (total_ref[rows, columns] + product).astype(out_ref.dtype)
-
-    project(place_ref, a, weight_ref, by, rows, keep)
+    depth = pl.ds(pl.multiple_of((place_ref[1] + 3) % 4 * 512, 512), 512)
+    for n in range(8):
+        columns = slice(n * 512, (n + 1) * 512)
+        part = jnp.dot(a[rows, :], weight_ref[depth, columns], preferred_element_type=jnp.float32)
+        out_ref[:, columns] = (total_ref[rows, columns] + part).astype(out_ref.dtype)
 
 
 SMEM = pl.BlockSpec(memory_space=pltpu.SMEM)
@@ -398,12 +393,12 @@
 ]
 
 
-def call(kernel, outs, scalars, arrays, flops, limit, scratch=(), aliases=None):
+def call(kernel, outs, scalars, arrays, flops, limit, scratch=(), aliases=None, places=None):
     return pl.pallas_call(
         kernel,
         out_shape=outs,
         in_specs=[SMEM] * len(scalars) + [VMEM] * len(arrays),
-        out_specs=[VMEM] * len(outs),
+        out_specs=places or [VMEM] * len(outs),
         scratch_shapes=list(scratch),
         input_output_aliases=aliases or {},
         compiler_params=pltpu.CompilerParams(vmem_limit_bytes=limit * MIB),
@@ -418,15 +413,10 @@
     kv = [kv[0]] + [along_y(kv[by], by) for by in (1, 2, 3)]
     q = call(q_kernel, [bf16(SLAB, 512)] * 4, [place], [queries], 1e6, 4)
     q = [q[0]] + [along_y(q[by], by) for by in (1, 2, 3)]
-    own, last, table = pl.pallas_call(
-        slots_kernel,
-        out_shape=[bf16(1024, 128), bf16(SLAB, 256), jax.ShapeDtypeStruct((128,), jnp.int32)],
-        in_specs=[SMEM] * 3 + [VMEM] * 4,
-        out_specs=[VMEM, VMEM, SMEM],
-        compiler_params=pltpu.CompilerParams(vmem_limit_bytes=4 * MIB),
-        cost_estimate=pl.CostEstimate(flops=10**6, bytes_accessed=10**6, transcendentals=0),
-        name="slots",
-    )(place, vertical, slash, *kv)
+    own, last, table = call(
+        slots_kernel, [bf16(1024, 128), bf16(SLAB, 256), jax.ShapeDtypeStruct((128,), jnp.int32)],
+        [place, vertical, slash.T], kv, 1e6, 4, (), None, [VMEM, VMEM, SMEM],
+    )
     hops = [first_hop(own, by) for by in (1, 2, 3)]
     prev = to_next_group(last)
     near = call(join_kernel, [bf16(4096, 128)], [], [own, *hops], 1e6, 4)[0]
@@ -437,30 +427,26 @@
         [pltpu.VMEM((5 * SLAB, 128), jnp.bfloat16)] * 2,
     )
     state = call(
-        functools.partial(part_kernel, 0), PACKED + STATE, [table],
+        functools.partial(part_kernel, 0, EVERY), PACKED + STATE, [table],
         [near, ql, *state], 5e9, 8, WORK, {3 + n: 2 + n for n in range(3)},
     )
     state = call(
-        functools.partial(part_kernel, 1), PACKED + STATE, [table],
+        functools.partial(part_kernel, 1, EVERY), PACKED + STATE, [table],
         [plus, minus, ql, *state], 1e10, 8, WORK, {4 + n: n for n in range(5)},
     )
-    state = call(
-        functools.partial(part_kernel, 2), PACKED + STATE + [bf16(SLAB, 512)] * 4,
-        [table], [*beyond, ql, *state], 5e9, 8, WORK, {4 + n: n for n in range(5)},
-    )
-    attention = state[5:]
-    back = [attention[0]] + [along_y(attention[by], -by) for by in (1, 2, 3)]
-    total = call(first_piece_kernel, [f32(SLAB, 4096)], [place], [back[0], out_weight], 1e9, 6)[0]
-    for by in (1, 3):
-        total = call(
-            functools.partial(next_piece_kernel, by), [f32(SLAB, 4096)], [place],
-            [back[by], out_weight, total], 1e9, 6, (), {3: 0},
-        )[0]
+    *state, a2, a1 = call(
+        functools.partial(part_kernel, 2, (2, 1)), PACKED + STATE + [bf16(SLAB, 512)] * 2, [table],
+        [*beyond, ql, *state], 3e9, 8, WORK, {4 + n: n for n in range(5)},
+    )
+    a2, a1 = along_y(a2, -2), along_y(a1, -1)
+    *state, a3, a0 = call(
+        functools.partial(part_kernel, 3, (3, 0)), PACKED + STATE + [bf16(SLAB, 512)] * 2, [table],
+        [ql, *state], 3e9, 8, WORK, {2 + n: n for n in range(5)},
+    )
+    a3 = along_y(a3, -3)
+    total = call(early_kernel, [f32(SLAB, 4096)], [place], [a0, a1, a2, out_weight], 3e9, 6)[0]
     theirs, mine = (
-        call(
-            functools.partial(last_piece_kernel, 2, own), [out], [place],
-            [back[2], out_weight, total], 1e9, 6,
-        )[0]
+        call(functools.partial(last_kernel, own), [out], [place], [a3, out_weight, total], 1e9, 6)[0]
         for own, out in ((False, bf16(128, 4096)), (True, f32(128, 4096)))
     )
     other = to_partner(theirs)

time: 109 us -> 111 us (1.018)
  the two profiles are of different devices: /device:TPU:37 before, /device:TPU:103 now
where the time goes in v3:
time: 111 us
  Pallas kernels  44 us (40%)
  starting transfers between devices  39.7 us (36%)
  waiting for transfers between devices  22.2 us (20%)
  local copies, waits for them, and re-layouts  3.52 us (3%)
  other arithmetic  1.22 us (1%)
    pallas_call x12, Pallas kernels, call(): pl.pallas_call(kernel, out_shape=outs, in_specs=[SMEM] * len(scalars) + [...  44 us
    ppermute x18, starting transfers between devices, moved(): return lax.ppermute(value, ALL, pairs)  39.7 us
    ppermute x18, waiting for transfers between devices, moved(): return lax.ppermute(value, ALL, pairs)  22.2 us
    unnamed x18, local copies, waits for them, and re-layouts  3.36 us
  transfers between devices with their start and end apart: 18, of which 10 were waited for; matrix products, arithmetic and copies ran while one was open for 0% of the time, Pallas kernels for 29%

profile of v3, /device:TPU:103, one launch (start us, length us, event | category | flops | bytes accessed | tf_op | source)
XLA Modules:
  0.0 110.9 jit_solution(9983653725883145300)
XLA Ops:
  0.0 0.1 stack.23.place_ref
  0.1 1.0 copy-done.1
  1.1 0.9 copy-done.2
  2.1 0.6 shard_map.64
  2.7 1.4 %collective-permute-start = (bf16[256,256]{1,0:T(8,128)(2,1)S(1)}, bf16[256,256]{1,0:T(8,128)(2,1)S(1)}, u32[]{:S(2)}, u32[]{:S(2)}) collective-permute-start(bf16[256,256]{1,0:T(8,128)(2,1)S(1)} %get-tuple-element.40), channel_id=1, source_target_pairs={{0,2},{1,3},{2,4},{3,5},{4,6},{5,7},{6,0},{7,1},{8,10},{9,11},{10,... | collective-permute-start | bytes 393224 | tf_op jit(solution)/shard_map/ppermute | solution.py:32
  4.1 2.6 %collective-permute-start.1 = (bf16[256,256]{1,0:T(8,128)(2,1)S(1)}, bf16[256,256]{1,0:T(8,128)(2,1)S(1)}, u32[]{:S(2)}, u32[]{:S(2)}) collective-permute-start(bf16[256,256]{1,0:T(8,128)(2,1)S(1)} %get-tuple-element.41), channel_id=1, source_target_pairs={{0,4},{1,5},{2,6},{3,7},{4,0},{5,1},{6,2},{7,3},{8,12},{9,13},{10,... | collective-permute-start | bytes 393224 | tf_op jit(solution)/shard_map/ppermute | solution.py:32
  6.7 1.1 collective-permute-start.2
  7.8 0.7 collective-permute-done.kv1
  8.5 3.9 %collective-permute-done.1.kv2 = bf16[256,256]{1,0:T(8,128)(2,1)S(1)} collective-permute-done((bf16[256,256]{1,0:T(8,128)(2,1)S(1)}, bf16[256,256]{1,0:T(8,128)(2,1)S(1)}, u32[]{:S(2)}, u32[]{:S(2)}) %collective-permute-start.1) | collective-permute-done | bytes 131104 | tf_op jit(solution)/shard_map/ppermute | solution.py:32
  12.4 0.7 copy-done.3
  13.1 0.7 copy-done.4
  13.8 1.5 %shard_map.65 = (bf16[1024,128]{1,0:T(8,128)(2,1)S(1)}, bf16[256,256]{1,0:T(8,128)(2,1)S(1)}, s32[128]{0:T(128)S(1)}) custom-call(s32[5]{0:T(128)S(1)} %stack.23.place_ref, s32[4,64]{1,0:T(4,128)S(1)} %copy-done.3, s32[2,4]{1,0:T(2,128)S(1)} %bitcast.8, bf16[256,256]{1,0:T(8,128)(2,1)S(1)} %get-tuple-element.39.kv0, ...), custom_call_target="tpu_custom_call" | custom-call | flops 1000000 | bytes 1000000 | tf_op jit(solution)/shard_map/pallas_call | solution.py:397
  15.3 0.1 collective-permute-start.7
  15.4 1.9 %collective-permute-start.8 = (bf16[1024,128]{1,0:T(8,128)(2,1)S(1)}, bf16[1024,128]{1,0:T(8,128)(2,1)S(1)}, u32[]{:S(2)}, u32[]{:S(2)}) collective-permute-start(bf16[1024,128]{1,0:T(8,128)(2,1)S(1)} %get-tuple-element.50.a0), channel_id=1, source_target_pairs={{0,64},{1,17},{2,66},{3,19},{4,68},{5,21},{6,70},{7,23},{8,72},{9,... | collective-permute-start | bytes 786440 | tf_op jit(solution)/shard_map/ppermute | solution.py:32
  17.3 2.6 %collective-permute-start.6 = (bf16[256,256]{1,0:T(8,128)(2,1)S(1)}, bf16[256,256]{1,0:T(8,128)(2,1)S(1)}, u32[]{:S(2)}, u32[]{:S(2)}) collective-permute-start(bf16[256,256]{1,0:T(8,128)(2,1)S(1)} %get-tuple-element.48), channel_id=1, source_target_pairs={{0,8},{1,9},{2,10},{3,11},{4,12},{5,13},{6,14},{7,15},{8,16},{9,17... | collective-permute-start | bytes 393224 | tf_op jit(solution)/shard_map/ppermute | solution.py:32
  19.9 1.0 collective-permute-done.7.a1
  20.9 1.6 %collective-permute-done.8.a2 = bf16[1024,128]{1,0:T(8,128)(2,1)S(1)} collective-permute-done((bf16[1024,128]{1,0:T(8,128)(2,1)S(1)}, bf16[1024,128]{1,0:T(8,128)(2,1)S(1)}, u32[]{:S(2)}, u32[]{:S(2)}) %collective-permute-start.8) | collective-permute-done | bytes 262176 | tf_op jit(solution)/shard_map/ppermute | solution.py:32
  22.5 2.8 %collective-permute-done.9.a3 = bf16[1024,128]{1,0:T(8,128)(2,1)S(1)} collective-permute-done((bf16[1024,128]{1,0:T(8,128)(2,1)S(1)}, bf16[1024,128]{1,0:T(8,128)(2,1)S(1)}, u32[]{:S(2)}, u32[]{:S(2)}) %collective-permute-start.9) | collective-permute-done | bytes 262176 | tf_op jit(solution)/shard_map/ppermute | solution.py:32
  25.3 0.1 shard_map.68.refs_0_
  25.4 0.1 collective-permute-start.10
  25.5 1.5 %collective-permute-start.12 = (bf16[4096,128]{1,0:T(8,128)(2,1)S(1)}, bf16[4096,128]{1,0:T(8,128)(2,1)S(1)}, u32[]{:S(2)}, u32[]{:S(2)}) collective-permute-start(bf16[4096,128]{1,0:T(8,128)(2,1)S(1)} %shard_map.68.refs_0_), channel_id=1, source_target_pairs={{0,24},{1,97},{2,26},{3,99},{4,28},{5,101},{6,30},{7,103},{8,0},{9... | collective-permute-start | bytes 3145736 | tf_op jit(solution)/shard_map/ppermute | solution.py:32
  26.9 0.6 shard_map.66
  27.5 1.3 %collective-permute-start.3 = (bf16[256,512]{1,0:T(8,128)(2,1)S(1)}, bf16[256,512]{1,0:T(8,128)(2,1)S(1)}, u32[]{:S(2)}, u32[]{:S(2)}) collective-permute-start(bf16[256,512]{1,0:T(8,128)(2,1)S(1)} %get-tuple-element.45), channel_id=1, source_target_pairs={{0,2},{1,3},{2,4},{3,5},{4,6},{5,7},{6,0},{7,1},{8,10},{9,11},{10,... | collective-permute-start | bytes 786440 | tf_op jit(solution)/shard_map/ppermute | solution.py:32
  28.8 2.2 %collective-permute-start.4 = (bf16[256,512]{1,0:T(8,128)(2,1)S(1)}, bf16[256,512]{1,0:T(8,128)(2,1)S(1)}, u32[]{:S(2)}, u32[]{:S(2)}) collective-permute-start(bf16[256,512]{1,0:T(8,128)(2,1)S(1)} %get-tuple-element.46), channel_id=1, source_target_pairs={{0,4},{1,5},{2,6},{3,7},{4,0},{5,1},{6,2},{7,3},{8,12},{9,13},{10,... | collective-permute-start | bytes 786440 | tf_op jit(solution)/shard_map/ppermute | solution.py:32
  31.0 0.7 collective-permute-start.5
  31.7 2.6 %collective-permute-done.3.q1 = bf16[256,512]{1,0:T(8,128)(2,1)S(1)} collective-permute-done((bf16[256,512]{1,0:T(8,128)(2,1)S(1)}, bf16[256,512]{1,0:T(8,128)(2,1)S(1)}, u32[]{:S(2)}, u32[]{:S(2)}) %collective-permute-start.3) | collective-permute-done | bytes 262176 | tf_op jit(solution)/shard_map/ppermute | solution.py:32
  34.3 5.4 %collective-permute-done.4.q2 = bf16[256,512]{1,0:T(8,128)(2,1)S(1)} collective-permute-done((bf16[256,512]{1,0:T(8,128)(2,1)S(1)}, bf16[256,512]{1,0:T(8,128)(2,1)S(1)}, u32[]{:S(2)}, u32[]{:S(2)}) %collective-permute-start.4) | collective-permute-done | bytes 262176 | tf_op jit(solution)/shard_map/ppermute | solution.py:32
  39.7 0.3 collective-permute-done.5.q3
  40.1 3.3 %shard_map.67 = (bf16[16,256,128]{2,1,0:T(8,128)(2,1)S(1)}, f32[16,8,256]{2,1,0:T(8,128)S(1)}, f32[16,8,256]{2,1,0:T(8,128)S(1)}, f32[16,128,256]{2,1,0:T(8,128)S(1)}) custom-call(s32[128]{0:T(128)S(1)} %get-tuple-element.43.place_ref, bf16[256,512]{1,0:T(8,128)(2,1)S(1)} %get-tuple-element.44.q0, bf16[256,512]{1,0:T(8,128)(2,1)S(1)} %collective-permute-done.3.q1, ...), custom_call_target="tpu_custom_call" | custom-call | flops 3000000000 | bytes 1000000 | tf_op jit(solution)/shard_map/pallas_call | solution.py:397
  43.4 0.8 shard_map.69
  44.2 17.0 %collective-permute-start.11 = (bf16[2048,128]{1,0:T(8,128)(2,1)S(1)}, bf16[2048,128]{1,0:T(8,128)(2,1)S(1)}, u32[]{:S(2)}, u32[]{:S(2)}) collective-permute-start(bf16[2048,128]{1,0:T(8,128)(2,1)S(1)} %slice.8), channel_id=1, source_target_pairs={{0,8},{1,33},{2,10},{3,35},{4,12},{5,37},{6,14},{7,39},{8,16},{9,4... | collective-permute-start | bytes 1572872 | tf_op jit(solution)/shard_map/ppermute | solution.py:32
  61.3 0.1 collective-permute-start.13
  61.4 0.0 slice-start
  61.4 0.0 slice-start.2
  61.4 13.9 %shard_map.70 = (bf16[4096,128]{1,0:T(8,128)(2,1)S(1)}, bf16[4096,128]{1,0:T(8,128)(2,1)S(1)}, f32[16,8,256]{2,1,0:T(8,128)S(1)}, f32[16,8,256]{2,1,0:T(8,128)S(1)}, f32[16,128,256]{2,1,0:T(8,128)S(1)}) custom-call(s32[128]{0:T(128)S(1)} %get-tuple-element.43.place_ref, ...), custom_call_target="tpu_custom_call", output_to_operand_aliasing={{0}: (4, {}), {1}: (5, {}), {2}: (6, {}), {3}: (7, {}), {4}... | custom-call | flops 10000000000 | bytes 1000000 | tf_op jit(solution)/shard_map/pallas_call | solution.py:397
  75.3 0.0 slice-start.3
  75.3 8.5 %shard_map.71 = (bf16[4096,128]{1,0:T(8,128)(2,1)S(1)}, bf16[4096,128]{1,0:T(8,128)(2,1)S(1)}, f32[16,8,256]{2,1,0:T(8,128)S(1)}, f32[16,8,256]{2,1,0:T(8,128)S(...) custom-call(s32[128]{0:T(128)S(1)} %get-tuple-element.43.place_ref, ...), custom_call_target="tpu_custom_call", output_to_operand_aliasing={{0}: (4, {}), {1}: (5, {}), {2}: (6, {}), {3}: (7, {}), {4}... | custom-call | flops 3000000000 | bytes 1000000 | tf_op jit(solution)/shard_map/pallas_call | solution.py:397
  83.9 1.9 %collective-permute-start.15 = (bf16[256,512]{1,0:T(8,128)(2,1)S(1)}, bf16[256,512]{1,0:T(8,128)(2,1)S(1)}, u32[]{:S(2)}, u32[]{:S(2)}) collective-permute-start(bf16[256,512]{1,0:T(8,128)(2,1)S(1)} %get-tuple-element.71), channel_id=1, source_target_pairs={{0,6},{1,7},{2,0},{3,1},{4,2},{5,3},{6,4},{7,5},{8,14},{9,15},{10,... | collective-permute-start | bytes 786440 | tf_op jit(solution)/shard_map/ppermute | solution.py:32
  85.7 5.3 %collective-permute-start.16 = (bf16[256,512]{1,0:T(8,128)(2,1)S(1)}, bf16[256,512]{1,0:T(8,128)(2,1)S(1)}, u32[]{:S(2)}, u32[]{:S(2)}) collective-permute-start(bf16[256,512]{1,0:T(8,128)(2,1)S(1)} %get-tuple-element.72), channel_id=1, source_target_pairs={{0,4},{1,5},{2,6},{3,7},{4,0},{5,1},{6,2},{7,3},{8,12},{9,13},{10,... | collective-permute-start | bytes 786440 | tf_op jit(solution)/shard_map/ppermute | solution.py:32
  91.0 8.2 %shard_map.72 = (bf16[4096,128]{1,0:T(8,128)(2,1)S(1)}, bf16[4096,128]{1,0:T(8,128)(2,1)S(1)}, f32[16,8,256]{2,1,0:T(8,128)S(1)}, f32[16,8,256]{2,1,0:T(8,128)S(...) custom-call(s32[128]{0:T(128)S(1)} %get-tuple-element.43.place_ref, ...), custom_call_target="tpu_custom_call", output_to_operand_aliasing={{0}: (2, {}), {1}: (3, {}), {2}: (4, {}), {3}: (5, {}), {4}... | custom-call | flops 3000000000 | bytes 1000000 | tf_op jit(solution)/shard_map/pallas_call | solution.py:397
  99.2 0.1 collective-permute-start.14
  99.4 4.0 %shard_map.73.total_ref = f32[256,4096]{1,0:T(8,128)S(1)} custom-call(s32[5]{0:T(128)S(1)} %stack.23.place_ref, bf16[256,512]{1,0:T(8,128)(2,1)S(1)} %get-tuple-element.70.a0, bf16[256,512]{1,0:T(8,128)(2,1)S(1)} %collective-permute-done.15.a1, bf16[256,512]{1,0:T(8,128)(2,1)S(1)} %collective-permute-done.16.a2, bf16[2048,4096]{1,0:T(8,128)(2,1)S(1)} %bitcast.7), custom_call_target="tpu_custom_call" | custom-call | flops 3000000000 | bytes 1000000 | tf_op jit(solution)/shard_map/pallas_call | solution.py:397
  103.3 2.4 %collective-permute-done.14.a = bf16[256,512]{1,0:T(8,128)(2,1)S(1)} collective-permute-done((bf16[256,512]{1,0:T(8,128)(2,1)S(1)}, bf16[256,512]{1,0:T(8,128)(2,1)S(1)}, u32[]{:S(2)}, u32[]{:S(2)}) %collective-permute-start.14) | collective-permute-done | bytes 262176 | tf_op jit(solution)/shard_map/ppermute | solution.py:32
  105.7 1.3 %shard_map.75 = bf16[128,4096]{1,0:T(8,128)(2,1)S(1)} custom-call(s32[5]{0:T(128)S(1)} %stack.23.place_ref, bf16[256,512]{1,0:T(8,128)(2,1)S(1)} %collective-permute-done.14.a, bf16[2048,4096]{1,0:T(8,128)(2,1)S(1)} %bitcast.7, f32[256,4096]{1,0:T(8,128)S(1)} %shard_map.73.total_ref), custom_call_target="tpu_custom_call" | custom-call | flops 1000000000 | bytes 1000000 | tf_op jit(solution)/shard_map/pallas_call | solution.py:397
  107.0 0.1 collective-permute-start.17
  107.1 1.3 %shard_map.74 = f32[128,4096]{1,0:T(8,128)S(1)} custom-call(s32[5]{0:T(128)S(1)} %stack.23.place_ref, bf16[256,512]{1,0:T(8,128)(2,1)S(1)} %collective-permute-done.14.a, bf16[2048,4096]{1,0:T(8,128)(2,1)S(1)} %bitcast.7, f32[256,4096]{1,0:T(8,128)S(1)} %shard_map.73.total_ref), custom_call_target="tpu_custom_call" | custom-call | flops 1000000000 | bytes 1000000 | tf_op jit(solution)/shard_map/pallas_call | solution.py:397
  108.4 1.4 %collective-permute-done.17 = bf16[128,4096]{1,0:T(8,128)(2,1)S(1)} collective-permute-done((bf16[128,4096]{1,0:T(8,128)(2,1)S(1)}, bf16[128,4096]{1,0:T(8,128)(2,1)S(1)}, u32[]{:S(2)}, u32[]{:S(2)}) %collective-permute-start.17) | collective-permute-done | bytes 1048608 | tf_op jit(solution)/shard_map/ppermute | solution.py:32
  109.7 1.2 %add_convert_fusion = bf16[128,4096]{1,0:T(8,128)(2,1)} fusion(f32[128,4096]{1,0:T(8,128)S(1)} %shard_map.74, bf16[128,4096]{1,0:T(8,128)(2,1)S(1)} %collective-permute-done.17), kind=kLoop, calls=%fused_computation | loop fusion | flops 1572864 | bytes 4194304 | tf_op jit(solution)/shard_map/convert_element_type | solution.py:453
  (23 shorter events, 0.1 us)
Async XLA Ops:
  0.0 26.9 %copy-start = (bf16[256,2048]{1,0:T(8,128)(2,1)S(1)}, bf16[256,2048]{1,0:T(8,128)(2,1)}, u32[]{:S(2)}) copy-start(bf16[256,2048]{1,0:T(8,128)(2,1)} %queries_ref.1) | copy-start | bytes 3145732
  0.1 1.0 copy-start.1
  1.1 0.9 copy-start.2
  2.7 5.8 %collective-permute-start = (bf16[256,256]{1,0:T(8,128)(2,1)S(1)}, bf16[256,256]{1,0:T(8,128)(2,1)S(1)}, u32[]{:S(2)}, u32[]{:S(2)}) collective-permute-start(bf16[256,256]{1,0:T(8,128)(2,1)S(1)} %get-tuple-element.40), channel_id=1, source_target_pairs={{0,2},{1,3},{2,4},{3,5},{4,6},{5,7},{6,0},{7,1},{8,10},{9,11},{10,... | collective-permute-start | bytes 393224 | tf_op jit(solution)/shard_map/ppermute | solution.py:32
  4.1 8.3 %collective-permute-start.1 = (bf16[256,256]{1,0:T(8,128)(2,1)S(1)}, bf16[256,256]{1,0:T(8,128)(2,1)S(1)}, u32[]{:S(2)}, u32[]{:S(2)}) collective-permute-start(bf16[256,256]{1,0:T(8,128)(2,1)S(1)} %get-tuple-element.41), channel_id=1, source_target_pairs={{0,4},{1,5},{2,6},{3,7},{4,0},{5,1},{6,2},{7,3},{8,12},{9,13},{10,... | collective-permute-start | bytes 393224 | tf_op jit(solution)/shard_map/ppermute | solution.py:32
  6.7 5.7 %collective-permute-start.2 = (bf16[256,256]{1,0:T(8,128)(2,1)S(1)}, bf16[256,256]{1,0:T(8,128)(2,1)S(1)}, u32[]{:S(2)}, u32[]{:S(2)}) collective-permute-start(bf16[256,256]{1,0:T(8,128)(2,1)S(1)} %get-tuple-element.42), channel_id=1, source_target_pairs={{0,6},{1,7},{2,0},{3,1},{4,2},{5,3},{6,4},{7,5},{8,14},{9,15},{10,... | collective-permute-start | bytes 393224 | tf_op jit(solution)/shard_map/ppermute | solution.py:32
  12.4 0.7 copy-start.3
  13.1 0.7 copy-start.4
  15.3 5.6 %collective-permute-start.7 = (bf16[1024,128]{1,0:T(8,128)(2,1)S(1)}, bf16[1024,128]{1,0:T(8,128)(2,1)S(1)}, u32[]{:S(2)}, u32[]{:S(2)}) collective-permute-start(bf16[1024,128]{1,0:T(8,128)(2,1)S(1)} %get-tuple-element.50.a0), channel_id=1, source_target_pairs={{0,32},{1,9},{2,34},{3,11},{4,36},{5,13},{6,38},{7,15},{8,40},{9,1... | collective-permute-start | bytes 786440 | tf_op jit(solution)/shard_map/ppermute | solution.py:32
  15.4 7.1 %collective-permute-start.8 = (bf16[1024,128]{1,0:T(8,128)(2,1)S(1)}, bf16[1024,128]{1,0:T(8,128)(2,1)S(1)}, u32[]{:S(2)}, u32[]{:S(2)}) collective-permute-start(bf16[1024,128]{1,0:T(8,128)(2,1)S(1)} %get-tuple-element.50.a0), channel_id=1, source_target_pairs={{0,64},{1,17},{2,66},{3,19},{4,68},{5,21},{6,70},{7,23},{8,72},{9,... | collective-permute-start | bytes 786440 | tf_op jit(solution)/shard_map/ppermute | solution.py:32
  17.3 8.0 %collective-permute-start.9 = (bf16[1024,128]{1,0:T(8,128)(2,1)S(1)}, bf16[1024,128]{1,0:T(8,128)(2,1)S(1)}, u32[]{:S(2)}, u32[]{:S(2)}) collective-permute-start(bf16[1024,128]{1,0:T(8,128)(2,1)S(1)} %get-tuple-element.50.a0), channel_id=1, source_target_pairs={{0,96},{1,25},{2,98},{3,27},{4,100},{5,29},{6,102},{7,31},{8,104},... | collective-permute-start | bytes 786440 | tf_op jit(solution)/shard_map/ppermute | solution.py:32
  17.3 13.7 %collective-permute-start.6 = (bf16[256,256]{1,0:T(8,128)(2,1)S(1)}, bf16[256,256]{1,0:T(8,128)(2,1)S(1)}, u32[]{:S(2)}, u32[]{:S(2)}) collective-permute-start(bf16[256,256]{1,0:T(8,128)(2,1)S(1)} %get-tuple-element.48), channel_id=1, source_target_pairs={{0,8},{1,9},{2,10},{3,11},{4,12},{5,13},{6,14},{7,15},{8,16},{9,17... | collective-permute-start | bytes 393224 | tf_op jit(solution)/shard_map/ppermute | solution.py:32
  25.4 18.8 %collective-permute-start.10 = (bf16[4096,128]{1,0:T(8,128)(2,1)S(1)}, bf16[4096,128]{1,0:T(8,128)(2,1)S(1)}, u32[]{:S(2)}, u32[]{:S(2)}) collective-permute-start(bf16[4096,128]{1,0:T(8,128)(2,1)S(1)} %shard_map.68.refs_0_), channel_id=1, source_target_pairs={{0,8},{1,33},{2,10},{3,35},{4,12},{5,37},{6,14},{7,39},{8,16},{9,4... | collective-permute-start | bytes 3145736 | tf_op jit(solution)/shard_map/ppermute | solution.py:32
  25.5 35.8 %collective-permute-start.12 = (bf16[4096,128]{1,0:T(8,128)(2,1)S(1)}, bf16[4096,128]{1,0:T(8,128)(2,1)S(1)}, u32[]{:S(2)}, u32[]{:S(2)}) collective-permute-start(bf16[4096,128]{1,0:T(8,128)(2,1)S(1)} %shard_map.68.refs_0_), channel_id=1, source_target_pairs={{0,24},{1,97},{2,26},{3,99},{4,28},{5,101},{6,30},{7,103},{8,0},{9... | collective-permute-start | bytes 3145736 | tf_op jit(solution)/shard_map/ppermute | solution.py:32
  27.5 6.8 %collective-permute-start.3 = (bf16[256,512]{1,0:T(8,128)(2,1)S(1)}, bf16[256,512]{1,0:T(8,128)(2,1)S(1)}, u32[]{:S(2)}, u32[]{:S(2)}) collective-permute-start(bf16[256,512]{1,0:T(8,128)(2,1)S(1)} %get-tuple-element.45), channel_id=1, source_target_pairs={{0,2},{1,3},{2,4},{3,5},{4,6},{5,7},{6,0},{7,1},{8,10},{9,11},{10,... | collective-permute-start | bytes 786440 | tf_op jit(solution)/shard_map/ppermute | solution.py:32
  28.8 10.9 %collective-permute-start.4 = (bf16[256,512]{1,0:T(8,128)(2,1)S(1)}, bf16[256,512]{1,0:T(8,128)(2,1)S(1)}, u32[]{:S(2)}, u32[]{:S(2)}) collective-permute-start(bf16[256,512]{1,0:T(8,128)(2,1)S(1)} %get-tuple-element.46), channel_id=1, source_target_pairs={{0,4},{1,5},{2,6},{3,7},{4,0},{5,1},{6,2},{7,3},{8,12},{9,13},{10,... | collective-permute-start | bytes 786440 | tf_op jit(solution)/shard_map/ppermute | solution.py:32
  31.0 9.1 %collective-permute-start.5 = (bf16[256,512]{1,0:T(8,128)(2,1)S(1)}, bf16[256,512]{1,0:T(8,128)(2,1)S(1)}, u32[]{:S(2)}, u32[]{:S(2)}) collective-permute-start(bf16[256,512]{1,0:T(8,128)(2,1)S(1)} %get-tuple-element.47), channel_id=1, source_target_pairs={{0,6},{1,7},{2,0},{3,1},{4,2},{5,3},{6,4},{7,5},{8,14},{9,15},{10,... | collective-permute-start | bytes 786440 | tf_op jit(solution)/shard_map/ppermute | solution.py:32
  44.2 31.1 %collective-permute-start.11 = (bf16[2048,128]{1,0:T(8,128)(2,1)S(1)}, bf16[2048,128]{1,0:T(8,128)(2,1)S(1)}, u32[]{:S(2)}, u32[]{:S(2)}) collective-permute-start(bf16[2048,128]{1,0:T(8,128)(2,1)S(1)} %slice.8), channel_id=1, source_target_pairs={{0,8},{1,33},{2,10},{3,35},{4,12},{5,37},{6,14},{7,39},{8,16},{9,4... | collective-permute-start | bytes 1572872 | tf_op jit(solution)/shard_map/ppermute | solution.py:32
  61.3 14.0 %collective-permute-start.13 = (bf16[2048,128]{1,0:T(8,128)(2,1)S(1)}, bf16[2048,128]{1,0:T(8,128)(2,1)S(1)}, u32[]{:S(2)}, u32[]{:S(2)}) collective-permute-start(bf16[2048,128]{1,0:T(8,128)(2,1)S(1)} %slice.9), channel_id=1, source_target_pairs={{0,24},{1,97},{2,26},{3,99},{4,28},{5,101},{6,30},{7,103},{8,0},{9... | collective-permute-start | bytes 1572872 | tf_op jit(solution)/shard_map/ppermute | solution.py:32
  61.4 37.9 %slice-start = ((s8[16777216]{0:T(1024)(128)(4,1)}), s8[4194304]{0:T(1024)(128)(4,1)S(1)}, s32[]{:S(2)}) async-start(s8[16777216]{0:T(1024)(128)(4,1)} %bitcast.6), calls=%async_computation | async-start | bytes 8388608
  61.4 37.9 %slice-start.1 = ((s8[16777216]{0:T(1024)(128)(4,1)}), s8[4194304]{0:T(1024)(128)(4,1)S(1)}, s32[]{:S(2)}) async-start(s8[16777216]{0:T(1024)(128)(4,1)} %bitcast.6), calls=%async_computation.1 | async-start | bytes 8388608
  61.4 37.9 %slice-start.2 = ((s8[16777216]{0:T(1024)(128)(4,1)}), s8[4194304]{0:T(1024)(128)(4,1)S(1)}, s32[]{:S(2)}) async-start(s8[16777216]{0:T(1024)(128)(4,1)} %bitcast.6), calls=%async_computation.2 | async-start | bytes 8388608
  75.3 24.0 %slice-start.3 = ((s8[16777216]{0:T(1024)(128)(4,1)}), s8[4194304]{0:T(1024)(128)(4,1)S(1)}, s32[]{:S(2)}) async-start(s8[16777216]{0:T(1024)(128)(4,1)} %bitcast.6), calls=%async_computation.3 | async-start | bytes 8388608
  83.9 15.4 %collective-permute-start.15 = (bf16[256,512]{1,0:T(8,128)(2,1)S(1)}, bf16[256,512]{1,0:T(8,128)(2,1)S(1)}, u32[]{:S(2)}, u32[]{:S(2)}) collective-permute-start(bf16[256,512]{1,0:T(8,128)(2,1)S(1)} %get-tuple-element.71), channel_id=1, source_target_pairs={{0,6},{1,7},{2,0},{3,1},{4,2},{5,3},{6,4},{7,5},{8,14},{9,15},{10,... | collective-permute-start | bytes 786440 | tf_op jit(solution)/shard_map/ppermute | solution.py:32
  85.7 13.6 %collective-permute-start.16 = (bf16[256,512]{1,0:T(8,128)(2,1)S(1)}, bf16[256,512]{1,0:T(8,128)(2,1)S(1)}, u32[]{:S(2)}, u32[]{:S(2)}) collective-permute-start(bf16[256,512]{1,0:T(8,128)(2,1)S(1)} %get-tuple-element.72), channel_id=1, source_target_pairs={{0,4},{1,5},{2,6},{3,7},{4,0},{5,1},{6,2},{7,3},{8,12},{9,13},{10,... | collective-permute-start | bytes 786440 | tf_op jit(solution)/shard_map/ppermute | solution.py:32
  99.2 6.5 %collective-permute-start.14 = (bf16[256,512]{1,0:T(8,128)(2,1)S(1)}, bf16[256,512]{1,0:T(8,128)(2,1)S(1)}, u32[]{:S(2)}, u32[]{:S(2)}) collective-permute-start(bf16[256,512]{1,0:T(8,128)(2,1)S(1)} %get-tuple-element.69), channel_id=1, source_target_pairs={{0,2},{1,3},{2,4},{3,5},{4,6},{5,7},{6,0},{7,1},{8,10},{9,11},{10,... | collective-permute-start | bytes 786440 | tf_op jit(solution)/shard_map/ppermute | solution.py:32
  107.0 2.7 %collective-permute-start.17 = (bf16[128,4096]{1,0:T(8,128)(2,1)S(1)}, bf16[128,4096]{1,0:T(8,128)(2,1)S(1)}, u32[]{:S(2)}, u32[]{:S(2)}) collective-permute-start(bf16[128,4096]{1,0:T(8,128)(2,1)S(1)} %shard_map.75), channel_id=1, source_target_pairs={{0,1},{1,0},{2,3},{3,2},{4,5},{5,4},{6,7},{7,6},{8,9},{9,8},{10,11... | collective-permute-start | bytes 3145736 | tf_op jit(solution)/shard_map/ppermute | solution.py:32

commit v4 on v3

--- a/solution.py
+++ b/solution.py
@@ -17,6 +17,7 @@
 SLASH = 8
 VERT = 16
 NEVER = 1 << 20
+BOUNDS = 96
 ALL = ("x", "z", "y", "c")
 MIB = 1 << 20
 
@@ -151,48 +152,51 @@
     return place_ref[0] * 16 + ((place_ref[1] - i // 4 + 4) % 4) * 4 + i % 4
 
 
-def find_bounds(place_ref, bounds):
-    bounds[0] = 0
-    for g in range(1, 16):
-        bounds[g] = row_rank(place_ref, 16 * g)
-    bounds[16] = NV
-
-
-def walk(place_ref, bounds, order, outer, at, sources, kc, vc):
-    group, y, mine1, mine2, core = (place_ref[i] for i in range(5))
-    second = (mine2 - outer + 4) % 4
+def count_of(table_ref, outer):
+    total = jnp.int32(0)
     for inner in range(4):
-        first = (mine1 - inner + 4) % 4
-        g = jnp.where(core == 0, first * 4 + second, second * 4 + first)
-        start = bounds[g]
-        end = jnp.where(g <= group, bounds[g + 1], start)
-        shift = at - start
-
-        def one(entry, carry):
-            block = place_ref[VERT + entry]
-            to = entry + shift
-            order[to] = block
-            if sources is not None:
-                source = sources[inner * len(sources) // 4]
-                skip = inner % (4 // len(sources))
-                slab = block // 4
-                before = place_ref[VERT + jnp.maximum(entry - 1, 0)] // 4
-                rank = jnp.where((entry > 0) & (before == slab), BLK, 0)
-                row = (skip * 4 + (y - slab % 4 + 4) % 4) * 256 + rank
-                rows = pl.ds(pl.multiple_of(to * BLK, BLK), BLK)
-                kc[rows, :] = source[pl.ds(pl.multiple_of(row, BLK), BLK), :]
-                vc[rows, :] = source[pl.ds(pl.multiple_of(row + 128, BLK), BLK), :]
-            return carry
-
-        lax.fori_loop(start, end, one, 0)
-        at = at + end - start
+        start, end = span_of(table_ref, outer, inner)
+        total = total + end - start
+    return total
+
+
+def span_of(table_ref, outer, inner):
+    group, core = table_ref[0], table_ref[4]
+    first = (table_ref[2] - inner + 4) % 4
+    second = (table_ref[3] - outer + 4) % 4
+    g = jnp.where(core == 0, first * 4 + second, second * 4 + first)
+    start = table_ref[BOUNDS + g]
+    return start, jnp.where(g < group, table_ref[BOUNDS + g + 1], start)
+
+
+def pack(table_ref, start, end, at, source, base, kc, vc):
+    y = table_ref[1]
+
+    def one(entry, carry):
+        slab = table_ref[VERT + entry] // 4
+        before = table_ref[VERT + jnp.maximum(entry - 1, 0)] // 4
+        rank = jnp.where((entry > 0) & (before == slab), BLK, 0)
+        row = (base * 4 + (y - slab % 4 + 4) % 4) * 256 + rank
+        rows = pl.ds(pl.multiple_of((at + entry - start) * BLK, BLK), BLK)
+        kc[rows, :] = source[pl.ds(pl.multiple_of(row, BLK), BLK), :]
+        vc[rows, :] = source[pl.ds(pl.multiple_of(row + 128, BLK), BLK), :]
+        return carry
+
+    lax.fori_loop(start, end, one, 0)
+    return at + end - start
+
+
+def pack_all(table_ref, outer, at, sources, kc, vc):
+    for inner in range(4):
+        start, end = span_of(table_ref, outer, inner)
+        part = 4 // len(sources)
+        at = pack(table_ref, start, end, at, sources[inner // part], inner % part, kc, vc)
     return at
 
 
-def chunks(size, unroll, picks, place_ref, order, begin, count, ql, kc, vc, top, tot, acc, vt_ref, sa_ref, sb_ref, ma, mb):
+def chunks(size, each, masked, picks, table_ref, order, begin, count, ql, kc, vc, top, tot, acc, vt_ref, sa_ref, sb_ref, ma, mb):
     pieces = size // BLK
     vt, sa, sb = vt_ref.at[:, 0:size], sa_ref.at[0:size, :], sb_ref.at[0:size, :]
-
     total = 4 * len(picks)
 
     def query(m):
@@ -203,55 +207,44 @@
     def one_chunk(n, carry):
         first = begin + n * pieces
         rows = pl.ds(pl.multiple_of(first * BLK, HALF), size)
-        last = order[first]
-        for j in range(1, pieces):
-            last = jnp.maximum(last, order[first + j])
         vt[...] = vc[rows, :].T
 
         def score(i, buffer, eight):
             scores = scores_of(kc[rows, :], ql[i])
+            if masked:
+                mine = block_of(table_ref, i)
+                scores = jnp.concatenate(
+                    [
+                        jnp.where(order[first + t] < mine, scores[BLK * t : BLK * (t + 1)], NEGATIVE)
+                        for t in range(pieces)
+                    ],
+                    axis=0,
+                )
             buffer[...] = scores
             eight[...] = top_of(lambda t: scores[BLK * t : BLK * (t + 1)], pieces)
 
-        def run(masked):
-            def finish(i, buffer, eight):
-                def plain(t):
-                    return buffer[BLK * t : BLK * (t + 1), :]
-
-                if masked:
-                    mine = block_of(place_ref, i)
-
-                    def load(t):
-                        return jnp.where(order[first + t] < mine, plain(t), NEGATIVE)
-
-                    weigh(i, load, pieces, top_of(load, pieces), vt[...], top, tot, acc)
-                else:
-                    weigh(i, plain, pieces, eight[...], vt[...], top, tot, acc)
-
-            score(query(0), sa, ma)
-            score(query(1), sb, mb)
-            each = 1 if masked else unroll
-
-            def some(j, carry):
-                for u in range(each):
-                    m = 2 * (j * each + u)
-                    finish(query(m), sa, ma)
-                    score(query((m + 2) % total), sa, ma)
-                    finish(query(m + 1), sb, mb)
-                    score(query((m + 3) % total), sb, mb)
-                return carry
-
-            lax.fori_loop(0, total // (2 * each), some, 0)
-
-        free = last < place_ref[0] * 16
-        pl.when(free)(lambda: run(False))
-        pl.when(jnp.logical_not(free))(lambda: run(True))
+        def finish(i, buffer, eight):
+            weigh(i, lambda t: buffer[BLK * t : BLK * (t + 1), :], pieces, eight[...], vt[...], top, tot, acc)
+
+        score(query(0), sa, ma)
+        score(query(1), sb, mb)
+
+        def some(j, carry):
+            for u in range(each):
+                m = 2 * (j * each + u)
+                finish(query(m), sa, ma)
+                score(query((m + 2) % total), sa, ma)
+                finish(query(m + 1), sb, mb)
+                score(query((m + 3) % total), sb, mb)
+            return carry
+
+        lax.fori_loop(0, total // (2 * each), some, 0)
         return carry
 
     lax.fori_loop(0, count, one_chunk, 0)
 
 
-def part_kernel(stage, picks, place_ref, *refs):
+def part_kernel(stage, picks, table_ref, *refs):
     splits = ((1,), (1, 1), (2,), ())[stage]
     sources, refs = refs[: sum(splits)], refs[sum(splits) :]
     ql = refs[0]
@@ -259,38 +252,45 @@
     kc, vc, top, tot, acc = refs[:5]
     final = stage >= 2
     outs, refs = (refs[5 : 5 + len(picks)], refs[5 + len(picks) :]) if final else (None, refs[5:])
-    bounds, order = refs[:2]
-    work = (ql, kc, vc, top, tot, acc, *refs[2:])
-    find_bounds(place_ref, bounds)
-
-    def add(outer, at, fresh):
-        return walk(place_ref, bounds, order, outer, at, fresh, kc, vc)
-
-    near = add(0, jnp.int32(0), sources if stage == 0 else None)
-    begin = near // 8 * 8
+    order = refs[0]
+    work = (ql, kc, vc, top, tot, acc, *refs[1:])
+    others, total = table_ref[BOUNDS + table_ref[0]], table_ref[BOUNDS + table_ref[0] + 1]
+    near = count_of(table_ref, 0)
+    begin = jnp.minimum(near // 8, 2) * 8
     if stage == 0:
-        chunks(HALF, 2, picks, place_ref, order, jnp.int32(0), near // 8, *work)
+        pack_all(table_ref, 0, jnp.int32(0), sources, kc, vc)
+        pack(table_ref, others, total, others, sources[0], 0, kc, vc)
+        chunks(HALF, 2, False, picks, table_ref, order, jnp.int32(0), begin // 8, *work)
         return
-    at = add(1, near, sources[:1] if stage == 1 else None)
-    at = add(3, at, sources[1:] if stage == 1 else None)
-    whole = (at - begin) // 16
     if stage == 1:
-        chunks(CHUNK, 2, picks, place_ref, order, begin, whole, *work)
+        at = pack_all(table_ref, 1, near, sources[:1], kc, vc)
+        at = pack_all(table_ref, 3, at, sources[1:], kc, vc)
+        chunks(CHUNK, 4, False, picks, table_ref, order, begin, (at - begin) // 16, *work)
         return
-    at = add(2, at, sources if stage == 2 else None)
-    begin = begin + whole * 16
-    whole = (at - begin) // 16
-    rest = begin + whole * 16
-    left = (at - rest + 7) // 8
-
-    def clear(n, carry):
-        order[n] = NEVER
-        vc[pl.ds(pl.multiple_of(n * BLK, BLK), BLK), :] = jnp.zeros((BLK, 128), jnp.bfloat16)
+    at = near + count_of(table_ref, 1) + count_of(table_ref, 3)
+    begin = begin + (at - begin) // 16 * 16
+    whole = (others - begin) // 16
+    half = begin + whole * 16
+    halves = (others - half) // 8
+    rest = half + halves * 8
+    left = (total - rest + 7) // 8
+    if stage == 2:
+        pack_all(table_ref, 2, at, sources, kc, vc)
+
+    def mark(n, carry):
+        own = table_ref[VERT + jnp.minimum(n, NV - 1)]
+        order[n] = jnp.where(n < others, -1, jnp.where(n < total, own, NEVER))
+
+        @pl.when(n >= total)
+        def _():
+            vc[pl.ds(pl.multiple_of(n * BLK, BLK), BLK), :] = jnp.zeros((BLK, 128), jnp.bfloat16)
+
         return carry
 
-    lax.fori_loop(at, rest + left * 8, clear, 0)
-    chunks(CHUNK, 2, picks, place_ref, order, begin, whole, *work)
-    chunks(HALF, 1, picks, place_ref, order, rest, left, *work)
+    lax.fori_loop(rest, rest + left * 8, mark, 0)
+    chunks(CHUNK, 4, False, picks, table_ref, order, begin, whole, *work)
+    chunks(HALF, 2, False, picks, table_ref, order, half, halves, *work)
+    chunks(HALF, 1, True, picks, table_ref, order, rest, left, *work)
     for out, by in zip(outs, picks):
         for block in range(4):
             i = by * 4 + block
@@ -300,9 +300,15 @@
 
 
 def local_kernel(
-    place_ref, q0, q1, q2, q3, kv0, kv1, kv2, kv3, prev_ref, ql, top, tot, acc, kl, vl
+    place_ref, q0, q1, q2, q3, kv0, kv1, kv2, kv3, prev_ref, ql, top, tot, acc, table_ref, kl, vl
 ):
     group, y = place_ref[0], place_ref[1]
+    for n in range(VERT + NV):
+        table_ref[n] = place_ref[n]
+    table_ref[BOUNDS] = 0
+    for g in range(1, 16):
+        table_ref[BOUNDS + g] = row_rank(place_ref, 16 * g)
+    table_ref[BOUNDS + 16] = NV
     kl[0:SLAB, :] = prev_ref[:, 0:128]
     vl[0:SLAB, :] = prev_ref[:, 128:256]
     for by, (q, kv) in enumerate(((q0, kv0), (q1, kv1), (q2, kv2), (q3, kv3))):
@@ -380,11 +386,11 @@
     return jax.ShapeDtypeStruct(shape, jnp.float32)
 
 
+TABLE = jax.ShapeDtypeStruct((128,), jnp.int32)
 STATE = [f32(16, 8, 256), f32(16, 8, 256), f32(16, 128, 256)]
 PACKED = [bf16(NV * BLK, 128)] * 2
 WORK = [
-    pltpu.SMEM((17,), jnp.int32),
-    pltpu.SMEM((NV,), jnp.int32),
+    pltpu.SMEM((NV + 8,), jnp.int32),
     pltpu.VMEM((128, CHUNK), jnp.bfloat16),
     pltpu.VMEM((CHUNK, 256), jnp.float32),
     pltpu.VMEM((CHUNK, 256), jnp.float32),
@@ -414,7 +420,7 @@
     q = call(q_kernel, [bf16(SLAB, 512)] * 4, [place], [queries], 1e6, 4)
     q = [q[0]] + [along_y(q[by], by) for by in (1, 2, 3)]
     own, last, table = call(
-        slots_kernel, [bf16(1024, 128), bf16(SLAB, 256), jax.ShapeDtypeStruct((128,), jnp.int32)],
+        slots_kernel, [bf16(1024, 128), bf16(SLAB, 256), TABLE],
         [place, vertical, slash.T], kv, 1e6, 4, (), None, [VMEM, VMEM, SMEM],
     )
     hops = [first_hop(own, by) for by in (1, 2, 3)]
@@ -422,9 +428,9 @@
     near = call(join_kernel, [bf16(4096, 128)], [], [own, *hops], 1e6, 4)[0]
     plus, minus = second_hop(near, 1), second_hop(near, 3)
     beyond = [second_hop(plus[:2048], 1), second_hop(minus[2048:], 3)]
-    ql, *state = call(
-        local_kernel, [bf16(16, 256, 128)] + STATE, [table], [*q, *kv, prev], 3e9, 6,
-        [pltpu.VMEM((5 * SLAB, 128), jnp.bfloat16)] * 2,
+    ql, *state, table = call(
+        local_kernel, [bf16(16, 256, 128)] + STATE + [TABLE], [table], [*q, *kv, prev], 3e9, 6,
+        [pltpu.VMEM((5 * SLAB, 128), jnp.bfloat16)] * 2, None, [VMEM] * 4 + [SMEM],
     )
     state = call(
         functools.partial(part_kernel, 0, EVERY), PACKED + STATE, [table],

time: 111 us -> 104 us (0.937)
  the two profiles are of different devices: /device:TPU:103 before, /device:TPU:37 now
where the time goes in v4:
time: 104 us; the launch traced here: 103 us
  Pallas kernels  44.3 us (43%)
  waiting for transfers between devices  29.9 us (29%)
  starting transfers between devices  24.2 us (23%)
  local copies, waits for them, and re-layouts  3.51 us (3%)
  other arithmetic  1.22 us (1%)
    pallas_call x12, Pallas kernels, call(): pl.pallas_call(kernel, out_shape=outs, in_specs=[SMEM] * len(scalars) + [...  44.3 us
    ppermute x18, waiting for transfers between devices, moved(): return lax.ppermute(value, ALL, pairs)  29.9 us
    ppermute x18, starting transfers between devices, moved(): return lax.ppermute(value, ALL, pairs)  24.2 us
    unnamed x18, local copies, waits for them, and re-layouts  3.35 us
  transfers between devices with their start and end apart: 18, of which 11 were waited for; matrix products, arithmetic and copies ran while one was open for 0% of the time, Pallas kernels for 28%

profile of v4, /device:TPU:37, one launch (start us, length us, event | category | flops | bytes accessed | tf_op | source)
XLA Modules:
  0.0 103.3 jit_solution(9972985621181490423)
XLA Ops:
  0.0 0.1 stack.23.place_ref
  0.1 1.0 copy-done.1
  1.1 0.9 copy-done.2
  2.1 0.6 shard_map.64
  2.7 1.4 %collective-permute-start = (bf16[256,256]{1,0:T(8,128)(2,1)S(1)}, bf16[256,256]{1,0:T(8,128)(2,1)S(1)}, u32[]{:S(2)}, u32[]{:S(2)}) collective-permute-start(bf16[256,256]{1,0:T(8,128)(2,1)S(1)} %get-tuple-element.41), channel_id=1, source_target_pairs={{0,2},{1,3},{2,4},{3,5},{4,6},{5,7},{6,0},{7,1},{8,10},{9,11},{10,... | collective-permute-start | bytes 393224 | tf_op jit(solution)/shard_map/ppermute | solution.py:33
  4.1 2.6 %collective-permute-start.1 = (bf16[256,256]{1,0:T(8,128)(2,1)S(1)}, bf16[256,256]{1,0:T(8,128)(2,1)S(1)}, u32[]{:S(2)}, u32[]{:S(2)}) collective-permute-start(bf16[256,256]{1,0:T(8,128)(2,1)S(1)} %get-tuple-element.42), channel_id=1, source_target_pairs={{0,4},{1,5},{2,6},{3,7},{4,0},{5,1},{6,2},{7,3},{8,12},{9,13},{10,... | collective-permute-start | bytes 393224 | tf_op jit(solution)/shard_map/ppermute | solution.py:33
  6.7 1.1 %collective-permute-start.2 = (bf16[256,256]{1,0:T(8,128)(2,1)S(1)}, bf16[256,256]{1,0:T(8,128)(2,1)S(1)}, u32[]{:S(2)}, u32[]{:S(2)}) collective-permute-start(bf16[256,256]{1,0:T(8,128)(2,1)S(1)} %get-tuple-element.43), channel_id=1, source_target_pairs={{0,6},{1,7},{2,0},{3,1},{4,2},{5,3},{6,4},{7,5},{8,14},{9,15},{10,... | collective-permute-start | bytes 393224 | tf_op jit(solution)/shard_map/ppermute | solution.py:33
  7.8 0.7 collective-permute-done.kv1
  8.5 3.9 %collective-permute-done.1.kv2 = bf16[256,256]{1,0:T(8,128)(2,1)S(1)} collective-permute-done((bf16[256,256]{1,0:T(8,128)(2,1)S(1)}, bf16[256,256]{1,0:T(8,128)(2,1)S(1)}, u32[]{:S(2)}, u32[]{:S(2)}) %collective-permute-start.1) | collective-permute-done | bytes 131104 | tf_op jit(solution)/shard_map/ppermute | solution.py:33
  12.4 0.0 collective-permute-done.2.kv3
  12.4 0.7 copy-done.3
  13.1 0.7 copy-done.4
  13.8 1.5 %shard_map.65 = (bf16[1024,128]{1,0:T(8,128)(2,1)S(1)}, bf16[256,256]{1,0:T(8,128)(2,1)S(1)}, s32[128]{0:T(128)S(1)}) custom-call(s32[5]{0:T(128)S(1)} %stack.23.place_ref, s32[4,64]{1,0:T(4,128)S(1)} %copy-done.3, s32[2,4]{1,0:T(2,128)S(1)} %bitcast.8, bf16[256,256]{1,0:T(8,128)(2,1)S(1)} %get-tuple-element.40.kv0, ...), custom_call_target="tpu_custom_call" | custom-call | flops 1000000 | bytes 1000000 | tf_op jit(solution)/shard_map/pallas_call | solution.py:403
  15.3 1.7 %collective-permute-start.7 = (bf16[1024,128]{1,0:T(8,128)(2,1)S(1)}, bf16[1024,128]{1,0:T(8,128)(2,1)S(1)}, u32[]{:S(2)}, u32[]{:S(2)}) collective-permute-start(bf16[1024,128]{1,0:T(8,128)(2,1)S(1)} %get-tuple-element.52.a0), channel_id=1, source_target_pairs={{0,32},{1,9},{2,34},{3,11},{4,36},{5,13},{6,38},{7,15},{8,40},{9,1... | collective-permute-start | bytes 786440 | tf_op jit(solution)/shard_map/ppermute | solution.py:33
  17.0 1.2 %collective-permute-start.8 = (bf16[1024,128]{1,0:T(8,128)(2,1)S(1)}, bf16[1024,128]{1,0:T(8,128)(2,1)S(1)}, u32[]{:S(2)}, u32[]{:S(2)}) collective-permute-start(bf16[1024,128]{1,0:T(8,128)(2,1)S(1)} %get-tuple-element.52.a0), channel_id=1, source_target_pairs={{0,64},{1,17},{2,66},{3,19},{4,68},{5,21},{6,70},{7,23},{8,72},{9,... | collective-permute-start | bytes 786440 | tf_op jit(solution)/shard_map/ppermute | solution.py:33
  18.2 2.0 %collective-permute-start.9 = (bf16[1024,128]{1,0:T(8,128)(2,1)S(1)}, bf16[1024,128]{1,0:T(8,128)(2,1)S(1)}, u32[]{:S(2)}, u32[]{:S(2)}) collective-permute-start(bf16[1024,128]{1,0:T(8,128)(2,1)S(1)} %get-tuple-element.52.a0), channel_id=1, source_target_pairs={{0,96},{1,25},{2,98},{3,27},{4,100},{5,29},{6,102},{7,31},{8,104},... | collective-permute-start | bytes 786440 | tf_op jit(solution)/shard_map/ppermute | solution.py:33
  20.2 0.0 collective-permute-start.6
  20.2 0.7 collective-permute-done.7.a1
  20.9 3.2 %collective-permute-done.8.a2 = bf16[1024,128]{1,0:T(8,128)(2,1)S(1)} collective-permute-done((bf16[1024,128]{1,0:T(8,128)(2,1)S(1)}, bf16[1024,128]{1,0:T(8,128)(2,1)S(1)}, u32[]{:S(2)}, u32[]{:S(2)}) %collective-permute-start.8) | collective-permute-done | bytes 262176 | tf_op jit(solution)/shard_map/ppermute | solution.py:33
  24.1 2.4 %collective-permute-done.9.a3 = bf16[1024,128]{1,0:T(8,128)(2,1)S(1)} collective-permute-done((bf16[1024,128]{1,0:T(8,128)(2,1)S(1)}, bf16[1024,128]{1,0:T(8,128)(2,1)S(1)}, u32[]{:S(2)}, u32[]{:S(2)}) %collective-permute-start.9) | collective-permute-done | bytes 262176 | tf_op jit(solution)/shard_map/ppermute | solution.py:33
  26.5 0.1 shard_map.68.refs_0_
  26.6 1.0 collective-permute-start.10
  27.6 0.5 collective-permute-start.12
  28.1 0.6 shard_map.66
  28.7 1.3 %collective-permute-start.3 = (bf16[256,512]{1,0:T(8,128)(2,1)S(1)}, bf16[256,512]{1,0:T(8,128)(2,1)S(1)}, u32[]{:S(2)}, u32[]{:S(2)}) collective-permute-start(bf16[256,512]{1,0:T(8,128)(2,1)S(1)} %get-tuple-element.46), channel_id=1, source_target_pairs={{0,2},{1,3},{2,4},{3,5},{4,6},{5,7},{6,0},{7,1},{8,10},{9,11},{10,... | collective-permute-start | bytes 786440 | tf_op jit(solution)/shard_map/ppermute | solution.py:33
  30.0 2.2 %collective-permute-start.4 = (bf16[256,512]{1,0:T(8,128)(2,1)S(1)}, bf16[256,512]{1,0:T(8,128)(2,1)S(1)}, u32[]{:S(2)}, u32[]{:S(2)}) collective-permute-start(bf16[256,512]{1,0:T(8,128)(2,1)S(1)} %get-tuple-element.47), channel_id=1, source_target_pairs={{0,4},{1,5},{2,6},{3,7},{4,0},{5,1},{6,2},{7,3},{8,12},{9,13},{10,... | collective-permute-start | bytes 786440 | tf_op jit(solution)/shard_map/ppermute | solution.py:33
  32.2 0.7 collective-permute-start.5
  32.9 2.7 %collective-permute-done.3.q1 = bf16[256,512]{1,0:T(8,128)(2,1)S(1)} collective-permute-done((bf16[256,512]{1,0:T(8,128)(2,1)S(1)}, bf16[256,512]{1,0:T(8,128)(2,1)S(1)}, u32[]{:S(2)}, u32[]{:S(2)}) %collective-permute-start.3) | collective-permute-done | bytes 262176 | tf_op jit(solution)/shard_map/ppermute | solution.py:33
  35.6 6.7 %collective-permute-done.4.q2 = bf16[256,512]{1,0:T(8,128)(2,1)S(1)} collective-permute-done((bf16[256,512]{1,0:T(8,128)(2,1)S(1)}, bf16[256,512]{1,0:T(8,128)(2,1)S(1)}, u32[]{:S(2)}, u32[]{:S(2)}) %collective-permute-start.4) | collective-permute-done | bytes 262176 | tf_op jit(solution)/shard_map/ppermute | solution.py:33
  42.3 0.2 collective-permute-done.5.q3
  42.5 3.8 %shard_map.67 = (bf16[16,256,128]{2,1,0:T(8,128)(2,1)S(1)}, f32[16,8,256]{2,1,0:T(8,128)S(1)}, f32[16,8,256]{2,1,0:T(8,128)S(1)}, f32[16,128,256]{2,1,0:T(8,128)S(1)}, s32[128]{0:T(128)S(1)}) custom-call(s32[128]{0:T(128)S(1)} %get-tuple-element.44.place_ref, bf16[256,512]{1,0:T(8,128)(2,1)S(1)} %get-tuple-element.45.q0, ...), custom_call_target="tpu_custom_call" | custom-call | flops 3000000000 | bytes 1000000 | tf_op jit(solution)/shard_map/pallas_call | solution.py:403
  46.3 0.9 shard_map.69
  47.2 0.9 collective-permute-start.11
  48.2 2.6 %collective-permute-start.13 = (bf16[2048,128]{1,0:T(8,128)(2,1)S(1)}, bf16[2048,128]{1,0:T(8,128)(2,1)S(1)}, u32[]{:S(2)}, u32[]{:S(2)}) collective-permute-start(bf16[2048,128]{1,0:T(8,128)(2,1)S(1)} %slice.9), channel_id=1, source_target_pairs={{0,24},{1,97},{2,26},{3,99},{4,28},{5,101},{6,30},{7,103},{8,0},{9... | collective-permute-start | bytes 1572872 | tf_op jit(solution)/shard_map/ppermute | solution.py:33
  50.8 7.0 %shard_map.70 = (bf16[4096,128]{1,0:T(8,128)(2,1)S(1)}, bf16[4096,128]{1,0:T(8,128)(2,1)S(1)}, f32[16,8,256]{2,1,0:T(8,128)S(1)}, f32[16,8,256]{2,1,0:T(8,128)S(1)}, f32[16,128,256]{2,1,0:T(8,128)S(1)}) custom-call(s32[128]{0:T(128)S(1)} %get-tuple-element.50.table_ref, ...), custom_call_target="tpu_custom_call", output_to_operand_aliasing={{0}: (4, {}), {1}: (5, {}), {2}: (6, {}), {3}: (7, {}), {4}... | custom-call | flops 10000000000 | bytes 1000000 | tf_op jit(solution)/shard_map/pallas_call | solution.py:403
  57.7 3.5 %collective-permute-done.13.refs_1_ = bf16[2048,128]{1,0:T(8,128)(2,1)S(1)} collective-permute-done((bf16[2048,128]{1,0:T(8,128)(2,1)S(1)}, bf16[2048,128]{1,0:T(8,128)(2,1)S(1)}, u32[]{:S(2)}, u32[]{:S(2)}) %collective-permute-start.13) | collective-permute-done | bytes 524320 | tf_op jit(solution)/shard_map/ppermute | solution.py:33
  61.3 12.2 %shard_map.71 = (bf16[4096,128]{1,0:T(8,128)(2,1)S(1)}, bf16[4096,128]{1,0:T(8,128)(2,1)S(1)}, f32[16,8,256]{2,1,0:T(8,128)S(1)}, f32[16,8,256]{2,1,0:T(8,128)S(...) custom-call(s32[128]{0:T(128)S(1)} %get-tuple-element.50.table_ref, ...), custom_call_target="tpu_custom_call", output_to_operand_aliasing={{0}: (4, {}), {1}: (5, {}), {2}: (6, {}), {3}: (7, {}), {4}... | custom-call | flops 3000000000 | bytes 1000000 | tf_op jit(solution)/shard_map/pallas_call | solution.py:403
  73.5 3.5 %collective-permute-start.15 = (bf16[256,512]{1,0:T(8,128)(2,1)S(1)}, bf16[256,512]{1,0:T(8,128)(2,1)S(1)}, u32[]{:S(2)}, u32[]{:S(2)}) collective-permute-start(bf16[256,512]{1,0:T(8,128)(2,1)S(1)} %get-tuple-element.73), channel_id=1, source_target_pairs={{0,6},{1,7},{2,0},{3,1},{4,2},{5,3},{6,4},{7,5},{8,14},{9,15},{10,... | collective-permute-start | bytes 786440 | tf_op jit(solution)/shard_map/ppermute | solution.py:33
  77.0 0.8 collective-permute-start.16
  77.8 11.1 %shard_map.72 = (bf16[4096,128]{1,0:T(8,128)(2,1)S(1)}, bf16[4096,128]{1,0:T(8,128)(2,1)S(1)}, f32[16,8,256]{2,1,0:T(8,128)S(1)}, f32[16,8,256]{2,1,0:T(8,128)S(...) custom-call(s32[128]{0:T(128)S(1)} %get-tuple-element.50.table_ref, ...), custom_call_target="tpu_custom_call", output_to_operand_aliasing={{0}: (2, {}), {1}: (3, {}), {2}: (4, {}), {3}: (5, {}), {4}... | custom-call | flops 3000000000 | bytes 1000000 | tf_op jit(solution)/shard_map/pallas_call | solution.py:403
  88.9 0.3 collective-permute-start.14
  89.3 4.0 %shard_map.73.total_ref = f32[256,4096]{1,0:T(8,128)S(1)} custom-call(s32[5]{0:T(128)S(1)} %stack.23.place_ref, bf16[256,512]{1,0:T(8,128)(2,1)S(1)} %get-tuple-element.72.a0, bf16[256,512]{1,0:T(8,128)(2,1)S(1)} %collective-permute-done.15.a1, bf16[256,512]{1,0:T(8,128)(2,1)S(1)} %collective-permute-done.16.a2, bf16[2048,4096]{1,0:T(8,128)(2,1)S(1)} %bitcast.7), custom_call_target="tpu_custom_call" | custom-call | flops 3000000000 | bytes 1000000 | tf_op jit(solution)/shard_map/pallas_call | solution.py:403
  93.3 4.8 %collective-permute-done.14.a = bf16[256,512]{1,0:T(8,128)(2,1)S(1)} collective-permute-done((bf16[256,512]{1,0:T(8,128)(2,1)S(1)}, bf16[256,512]{1,0:T(8,128)(2,1)S(1)}, u32[]{:S(2)}, u32[]{:S(2)}) %collective-permute-start.14) | collective-permute-done | bytes 262176 | tf_op jit(solution)/shard_map/ppermute | solution.py:33
  98.1 1.3 %shard_map.75 = bf16[128,4096]{1,0:T(8,128)(2,1)S(1)} custom-call(s32[5]{0:T(128)S(1)} %stack.23.place_ref, bf16[256,512]{1,0:T(8,128)(2,1)S(1)} %collective-permute-done.14.a, bf16[2048,4096]{1,0:T(8,128)(2,1)S(1)} %bitcast.7, f32[256,4096]{1,0:T(8,128)S(1)} %shard_map.73.total_ref), custom_call_target="tpu_custom_call" | custom-call | flops 1000000000 | bytes 1000000 | tf_op jit(solution)/shard_map/pallas_call | solution.py:403
  99.4 0.4 collective-permute-start.17
  99.8 1.3 %shard_map.74 = f32[128,4096]{1,0:T(8,128)S(1)} custom-call(s32[5]{0:T(128)S(1)} %stack.23.place_ref, bf16[256,512]{1,0:T(8,128)(2,1)S(1)} %collective-permute-done.14.a, bf16[2048,4096]{1,0:T(8,128)(2,1)S(1)} %bitcast.7, f32[256,4096]{1,0:T(8,128)S(1)} %shard_map.73.total_ref), custom_call_target="tpu_custom_call" | custom-call | flops 1000000000 | bytes 1000000 | tf_op jit(solution)/shard_map/pallas_call | solution.py:403
  101.1 1.1 %collective-permute-done.17 = bf16[128,4096]{1,0:T(8,128)(2,1)S(1)} collective-permute-done((bf16[128,4096]{1,0:T(8,128)(2,1)S(1)}, bf16[128,4096]{1,0:T(8,128)(2,1)S(1)}, u32[]{:S(2)}, u32[]{:S(2)}) %collective-permute-start.17) | collective-permute-done | bytes 1048608 | tf_op jit(solution)/shard_map/ppermute | solution.py:33
  102.1 1.2 %add_convert_fusion = bf16[128,4096]{1,0:T(8,128)(2,1)} fusion(f32[128,4096]{1,0:T(8,128)S(1)} %shard_map.74, bf16[128,4096]{1,0:T(8,128)(2,1)S(1)} %collective-permute-done.17), kind=kLoop, calls=%fused_computation | loop fusion | flops 1572864 | bytes 4194304 | tf_op jit(solution)/shard_map/convert_element_type | solution.py:459
  (23 shorter events, 0.1 us)
Async XLA Ops:
  0.0 28.1 %copy-start = (bf16[256,2048]{1,0:T(8,128)(2,1)S(1)}, bf16[256,2048]{1,0:T(8,128)(2,1)}, u32[]{:S(2)}) copy-start(bf16[256,2048]{1,0:T(8,128)(2,1)} %queries_ref.1) | copy-start | bytes 3145732
  0.1 1.0 copy-start.1
  1.1 0.9 copy-start.2
  2.7 5.8 %collective-permute-start = (bf16[256,256]{1,0:T(8,128)(2,1)S(1)}, bf16[256,256]{1,0:T(8,128)(2,1)S(1)}, u32[]{:S(2)}, u32[]{:S(2)}) collective-permute-start(bf16[256,256]{1,0:T(8,128)(2,1)S(1)} %get-tuple-element.41), channel_id=1, source_target_pairs={{0,2},{1,3},{2,4},{3,5},{4,6},{5,7},{6,0},{7,1},{8,10},{9,11},{10,... | collective-permute-start | bytes 393224 | tf_op jit(solution)/shard_map/ppermute | solution.py:33
  4.1 8.3 %collective-permute-start.1 = (bf16[256,256]{1,0:T(8,128)(2,1)S(1)}, bf16[256,256]{1,0:T(8,128)(2,1)S(1)}, u32[]{:S(2)}, u32[]{:S(2)}) collective-permute-start(bf16[256,256]{1,0:T(8,128)(2,1)S(1)} %get-tuple-element.42), channel_id=1, source_target_pairs={{0,4},{1,5},{2,6},{3,7},{4,0},{5,1},{6,2},{7,3},{8,12},{9,13},{10,... | collective-permute-start | bytes 393224 | tf_op jit(solution)/shard_map/ppermute | solution.py:33
  6.7 5.7 %collective-permute-start.2 = (bf16[256,256]{1,0:T(8,128)(2,1)S(1)}, bf16[256,256]{1,0:T(8,128)(2,1)S(1)}, u32[]{:S(2)}, u32[]{:S(2)}) collective-permute-start(bf16[256,256]{1,0:T(8,128)(2,1)S(1)} %get-tuple-element.43), channel_id=1, source_target_pairs={{0,6},{1,7},{2,0},{3,1},{4,2},{5,3},{6,4},{7,5},{8,14},{9,15},{10,... | collective-permute-start | bytes 393224 | tf_op jit(solution)/shard_map/ppermute | solution.py:33
  12.4 0.7 copy-start.3
  13.1 0.7 copy-start.4
  15.3 5.6 %collective-permute-start.7 = (bf16[1024,128]{1,0:T(8,128)(2,1)S(1)}, bf16[1024,128]{1,0:T(8,128)(2,1)S(1)}, u32[]{:S(2)}, u32[]{:S(2)}) collective-permute-start(bf16[1024,128]{1,0:T(8,128)(2,1)S(1)} %get-tuple-element.52.a0), channel_id=1, source_target_pairs={{0,32},{1,9},{2,34},{3,11},{4,36},{5,13},{6,38},{7,15},{8,40},{9,1... | collective-permute-start | bytes 786440 | tf_op jit(solution)/shard_map/ppermute | solution.py:33
  17.0 7.1 %collective-permute-start.8 = (bf16[1024,128]{1,0:T(8,128)(2,1)S(1)}, bf16[1024,128]{1,0:T(8,128)(2,1)S(1)}, u32[]{:S(2)}, u32[]{:S(2)}) collective-permute-start(bf16[1024,128]{1,0:T(8,128)(2,1)S(1)} %get-tuple-element.52.a0), channel_id=1, source_target_pairs={{0,64},{1,17},{2,66},{3,19},{4,68},{5,21},{6,70},{7,23},{8,72},{9,... | collective-permute-start | bytes 786440 | tf_op jit(solution)/shard_map/ppermute | solution.py:33
  18.2 8.3 %collective-permute-start.9 = (bf16[1024,128]{1,0:T(8,128)(2,1)S(1)}, bf16[1024,128]{1,0:T(8,128)(2,1)S(1)}, u32[]{:S(2)}, u32[]{:S(2)}) collective-permute-start(bf16[1024,128]{1,0:T(8,128)(2,1)S(1)} %get-tuple-element.52.a0), channel_id=1, source_target_pairs={{0,96},{1,25},{2,98},{3,27},{4,100},{5,29},{6,102},{7,31},{8,104},... | collective-permute-start | bytes 786440 | tf_op jit(solution)/shard_map/ppermute | solution.py:33
  20.2 12.1 %collective-permute-start.6 = (bf16[256,256]{1,0:T(8,128)(2,1)S(1)}, bf16[256,256]{1,0:T(8,128)(2,1)S(1)}, u32[]{:S(2)}, u32[]{:S(2)}) collective-permute-start(bf16[256,256]{1,0:T(8,128)(2,1)S(1)} %get-tuple-element.49), channel_id=1, source_target_pairs={{0,8},{1,9},{2,10},{3,11},{4,12},{5,13},{6,14},{7,15},{8,16},{9,17... | collective-permute-start | bytes 393224 | tf_op jit(solution)/shard_map/ppermute | solution.py:33
  26.6 20.6 %collective-permute-start.10 = (bf16[4096,128]{1,0:T(8,128)(2,1)S(1)}, bf16[4096,128]{1,0:T(8,128)(2,1)S(1)}, u32[]{:S(2)}, u32[]{:S(2)}) collective-permute-start(bf16[4096,128]{1,0:T(8,128)(2,1)S(1)} %shard_map.68.refs_0_), channel_id=1, source_target_pairs={{0,8},{1,33},{2,10},{3,35},{4,12},{5,37},{6,14},{7,39},{8,16},{9,4... | collective-permute-start | bytes 3145736 | tf_op jit(solution)/shard_map/ppermute | solution.py:33
  27.6 20.6 %collective-permute-start.12 = (bf16[4096,128]{1,0:T(8,128)(2,1)S(1)}, bf16[4096,128]{1,0:T(8,128)(2,1)S(1)}, u32[]{:S(2)}, u32[]{:S(2)}) collective-permute-start(bf16[4096,128]{1,0:T(8,128)(2,1)S(1)} %shard_map.68.refs_0_), channel_id=1, source_target_pairs={{0,24},{1,97},{2,26},{3,99},{4,28},{5,101},{6,30},{7,103},{8,0},{9... | collective-permute-start | bytes 3145736 | tf_op jit(solution)/shard_map/ppermute | solution.py:33
  28.7 6.9 %collective-permute-start.3 = (bf16[256,512]{1,0:T(8,128)(2,1)S(1)}, bf16[256,512]{1,0:T(8,128)(2,1)S(1)}, u32[]{:S(2)}, u32[]{:S(2)}) collective-permute-start(bf16[256,512]{1,0:T(8,128)(2,1)S(1)} %get-tuple-element.46), channel_id=1, source_target_pairs={{0,2},{1,3},{2,4},{3,5},{4,6},{5,7},{6,0},{7,1},{8,10},{9,11},{10,... | collective-permute-start | bytes 786440 | tf_op jit(solution)/shard_map/ppermute | solution.py:33
  30.0 12.3 %collective-permute-start.4 = (bf16[256,512]{1,0:T(8,128)(2,1)S(1)}, bf16[256,512]{1,0:T(8,128)(2,1)S(1)}, u32[]{:S(2)}, u32[]{:S(2)}) collective-permute-start(bf16[256,512]{1,0:T(8,128)(2,1)S(1)} %get-tuple-element.47), channel_id=1, source_target_pairs={{0,4},{1,5},{2,6},{3,7},{4,0},{5,1},{6,2},{7,3},{8,12},{9,13},{10,... | collective-permute-start | bytes 786440 | tf_op jit(solution)/shard_map/ppermute | solution.py:33
  32.2 10.3 %collective-permute-start.5 = (bf16[256,512]{1,0:T(8,128)(2,1)S(1)}, bf16[256,512]{1,0:T(8,128)(2,1)S(1)}, u32[]{:S(2)}, u32[]{:S(2)}) collective-permute-start(bf16[256,512]{1,0:T(8,128)(2,1)S(1)} %get-tuple-element.48), channel_id=1, source_target_pairs={{0,6},{1,7},{2,0},{3,1},{4,2},{5,3},{6,4},{7,5},{8,14},{9,15},{10,... | collective-permute-start | bytes 786440 | tf_op jit(solution)/shard_map/ppermute | solution.py:33
  47.2 10.6 %collective-permute-start.11 = (bf16[2048,128]{1,0:T(8,128)(2,1)S(1)}, bf16[2048,128]{1,0:T(8,128)(2,1)S(1)}, u32[]{:S(2)}, u32[]{:S(2)}) collective-permute-start(bf16[2048,128]{1,0:T(8,128)(2,1)S(1)} %slice.8), channel_id=1, source_target_pairs={{0,8},{1,33},{2,10},{3,35},{4,12},{5,37},{6,14},{7,39},{8,16},{9,4... | collective-permute-start | bytes 1572872 | tf_op jit(solution)/shard_map/ppermute | solution.py:33
  48.2 13.1 %collective-permute-start.13 = (bf16[2048,128]{1,0:T(8,128)(2,1)S(1)}, bf16[2048,128]{1,0:T(8,128)(2,1)S(1)}, u32[]{:S(2)}, u32[]{:S(2)}) collective-permute-start(bf16[2048,128]{1,0:T(8,128)(2,1)S(1)} %slice.9), channel_id=1, source_target_pairs={{0,24},{1,97},{2,26},{3,99},{4,28},{5,101},{6,30},{7,103},{8,0},{9... | collective-permute-start | bytes 1572872 | tf_op jit(solution)/shard_map/ppermute | solution.py:33
  50.8 38.5 %slice-start = ((s8[16777216]{0:T(1024)(128)(4,1)}), s8[4194304]{0:T(1024)(128)(4,1)S(1)}, s32[]{:S(2)}) async-start(s8[16777216]{0:T(1024)(128)(4,1)} %bitcast.6), calls=%async_computation | async-start | bytes 8388608
  50.8 38.5 %slice-start.1 = ((s8[16777216]{0:T(1024)(128)(4,1)}), s8[4194304]{0:T(1024)(128)(4,1)S(1)}, s32[]{:S(2)}) async-start(s8[16777216]{0:T(1024)(128)(4,1)} %bitcast.6), calls=%async_computation.1 | async-start | bytes 8388608
  50.8 38.5 %slice-start.2 = ((s8[16777216]{0:T(1024)(128)(4,1)}), s8[4194304]{0:T(1024)(128)(4,1)S(1)}, s32[]{:S(2)}) async-start(s8[16777216]{0:T(1024)(128)(4,1)} %bitcast.6), calls=%async_computation.2 | async-start | bytes 8388608
  61.3 28.0 %slice-start.3 = ((s8[16777216]{0:T(1024)(128)(4,1)}), s8[4194304]{0:T(1024)(128)(4,1)S(1)}, s32[]{:S(2)}) async-start(s8[16777216]{0:T(1024)(128)(4,1)} %bitcast.6), calls=%async_computation.3 | async-start | bytes 8388608
  73.5 15.7 %collective-permute-start.15 = (bf16[256,512]{1,0:T(8,128)(2,1)S(1)}, bf16[256,512]{1,0:T(8,128)(2,1)S(1)}, u32[]{:S(2)}, u32[]{:S(2)}) collective-permute-start(bf16[256,512]{1,0:T(8,128)(2,1)S(1)} %get-tuple-element.73), channel_id=1, source_target_pairs={{0,6},{1,7},{2,0},{3,1},{4,2},{5,3},{6,4},{7,5},{8,14},{9,15},{10,... | collective-permute-start | bytes 786440 | tf_op jit(solution)/shard_map/ppermute | solution.py:33
  77.0 12.3 %collective-permute-start.16 = (bf16[256,512]{1,0:T(8,128)(2,1)S(1)}, bf16[256,512]{1,0:T(8,128)(2,1)S(1)}, u32[]{:S(2)}, u32[]{:S(2)}) collective-permute-start(bf16[256,512]{1,0:T(8,128)(2,1)S(1)} %get-tuple-element.74), channel_id=1, source_target_pairs={{0,4},{1,5},{2,6},{3,7},{4,0},{5,1},{6,2},{7,3},{8,12},{9,13},{10,... | collective-permute-start | bytes 786440 | tf_op jit(solution)/shard_map/ppermute | solution.py:33
  88.9 9.2 %collective-permute-start.14 = (bf16[256,512]{1,0:T(8,128)(2,1)S(1)}, bf16[256,512]{1,0:T(8,128)(2,1)S(1)}, u32[]{:S(2)}, u32[]{:S(2)}) collective-permute-start(bf16[256,512]{1,0:T(8,128)(2,1)S(1)} %get-tuple-element.71), channel_id=1, source_target_pairs={{0,2},{1,3},{2,4},{3,5},{4,6},{5,7},{6,0},{7,1},{8,10},{9,11},{10,... | collective-permute-start | bytes 786440 | tf_op jit(solution)/shard_map/ppermute | solution.py:33
  99.4 2.7 %collective-permute-start.17 = (bf16[128,4096]{1,0:T(8,128)(2,1)S(1)}, bf16[128,4096]{1,0:T(8,128)(2,1)S(1)}, u32[]{:S(2)}, u32[]{:S(2)}) collective-permute-start(bf16[128,4096]{1,0:T(8,128)(2,1)S(1)} %shard_map.75), channel_id=1, source_target_pairs={{0,1},{1,0},{2,3},{3,2},{4,5},{5,4},{6,7},{7,6},{8,9},{9,8},{10,11... | collective-permute-start | bytes 3145736 | tf_op jit(solution)/shard_map/ppermute | solution.py:33

commit v5 on v4

--- a/solution.py
+++ b/solution.py
@@ -74,14 +74,18 @@
         out_refs[by][...] = queries_ref[:, pl.ds(pl.multiple_of((y + by) % 4 * 512, 512), 512)]
 
 
-def slots_kernel(place_ref, vert_ref, slash_ref, kv0, kv1, kv2, kv3, own_ref, last_ref, table_ref):
-    group, y = place_ref[0], place_ref[1]
+def table_kernel(place_ref, vert_ref, slash_ref, table_ref):
+    y = place_ref[1]
     for n in range(5):
         table_ref[n] = place_ref[n]
     for n in range(2):
         table_ref[SLASH + n] = slash_ref[n, y]
     for n in range(NV):
         table_ref[VERT + n] = vert_ref[y, n]
+
+
+def slots_kernel(table_ref, kv0, kv1, kv2, kv3, own_ref, last_ref):
+    group, y = table_ref[0], table_ref[1]
     for by, kv in enumerate((kv0, kv1, kv2, kv3)):
         slab = (y - by + 4) % 4
         first = (group * 4 + slab) * 4
@@ -198,10 +202,13 @@
     pieces = size // BLK
     vt, sa, sb = vt_ref.at[:, 0:size], sa_ref.at[0:size, :], sb_ref.at[0:size, :]
     total = 4 * len(picks)
+    steps = total // (2 * each)
 
     def query(m):
         if len(picks) == 4:
             return m
+        if len(picks) == 1:
+            return 4 * picks[0] + m
         return jnp.where(m < 4, 4 * picks[0], 4 * picks[1]) + m % 4
 
     def one_chunk(n, carry):
@@ -232,49 +239,45 @@
         def some(j, carry):
             for u in range(each):
                 m = 2 * (j * each + u)
+                more = steps > 1 or u < each - 1
                 finish(query(m), sa, ma)
-                score(query((m + 2) % total), sa, ma)
+                if more:
+                    score(query((m + 2) % total), sa, ma)
                 finish(query(m + 1), sb, mb)
-                score(query((m + 3) % total), sb, mb)
+                if more:
+                    score(query((m + 3) % total), sb, mb)
             return carry
 
-        lax.fori_loop(0, total // (2 * each), some, 0)
+        if steps == 1:
+            some(0, 0)
+        else:
+            lax.fori_loop(0, steps, some, 0)
         return carry
 
     lax.fori_loop(0, count, one_chunk, 0)
 
 
 def part_kernel(stage, picks, table_ref, *refs):
-    splits = ((1,), (1, 1), (2,), ())[stage]
+    splits = ((1, 1), (2,), ())[stage]
     sources, refs = refs[: sum(splits)], refs[sum(splits) :]
-    ql = refs[0]
-    refs = refs[6:] if stage else refs[4:]
+    ql, refs = refs[0], refs[6:]
     kc, vc, top, tot, acc = refs[:5]
-    final = stage >= 2
-    outs, refs = (refs[5 : 5 + len(picks)], refs[5 + len(picks) :]) if final else (None, refs[5:])
+    outs, refs = (refs[5 : 5 + len(picks)], refs[5 + len(picks) :]) if stage else (None, refs[5:])
     order = refs[0]
     work = (ql, kc, vc, top, tot, acc, *refs[1:])
     others, total = table_ref[BOUNDS + table_ref[0]], table_ref[BOUNDS + table_ref[0] + 1]
-    near = count_of(table_ref, 0)
-    begin = jnp.minimum(near // 8, 2) * 8
+    at = count_of(table_ref, 0)
     if stage == 0:
-        pack_all(table_ref, 0, jnp.int32(0), sources, kc, vc)
-        pack(table_ref, others, total, others, sources[0], 0, kc, vc)
-        chunks(HALF, 2, False, picks, table_ref, order, jnp.int32(0), begin // 8, *work)
+        at = pack_all(table_ref, 1, at, sources[:1], kc, vc)
+        at = pack_all(table_ref, 3, at, sources[1:], kc, vc)
+        chunks(CHUNK, 4, False, picks, table_ref, order, jnp.int32(0), at // 16, *work)
         return
+    at = at + count_of(table_ref, 1) + count_of(table_ref, 3)
+    begin = at // 16 * 16
+    whole = (others - begin) // 16
+    rest = begin + whole * 16
+    left = (total - rest + 7) // 8
     if stage == 1:
-        at = pack_all(table_ref, 1, near, sources[:1], kc, vc)
-        at = pack_all(table_ref, 3, at, sources[1:], kc, vc)
-        chunks(CHUNK, 4, False, picks, table_ref, order, begin, (at - begin) // 16, *work)
-        return
-    at = near + count_of(table_ref, 1) + count_of(table_ref, 3)
-    begin = begin + (at - begin) // 16 * 16
-    whole = (others - begin) // 16
-    half = begin + whole * 16
-    halves = (others - half) // 8
-    rest = half + halves * 8
-    left = (total - rest + 7) // 8
-    if stage == 2:
         pack_all(table_ref, 2, at, sources, kc, vc)
 
     def mark(n, carry):
@@ -288,9 +291,8 @@
         return carry
 
     lax.fori_loop(rest, rest + left * 8, mark, 0)
-    chunks(CHUNK, 4, False, picks, table_ref, order, begin, whole, *work)
-    chunks(HALF, 2, False, picks, table_ref, order, half, halves, *work)
-    chunks(HALF, 1, True, picks, table_ref, order, rest, left, *work)
+    chunks(CHUNK, 2 * len(picks), False, picks, table_ref, order, begin, whole, *work)
+    chunks(HALF, 2 * len(picks), True, picks, table_ref, order, rest, left, *work)
     for out, by in zip(outs, picks):
         for block in range(4):
             i = by * 4 + block
@@ -300,7 +302,8 @@
 
 
 def local_kernel(
-    place_ref, q0, q1, q2, q3, kv0, kv1, kv2, kv3, prev_ref, ql, top, tot, acc, table_ref, kl, vl
+    place_ref, q0, q1, q2, q3, kv0, kv1, kv2, kv3, prev_ref, near,
+    ql, kc, vc, top, tot, acc, table_ref, kl, vl
 ):
     group, y = place_ref[0], place_ref[1]
     for n in range(VERT + NV):
@@ -350,6 +353,9 @@
         return carry
 
     lax.fori_loop(0, 4, some, 0)
+    pack_all(table_ref, 0, jnp.int32(0), [near], kc, vc)
+    others, total = table_ref[BOUNDS + group], table_ref[BOUNDS + group + 1]
+    pack(table_ref, others, total, others, near, 0, kc, vc)
 
 
 def early_kernel(place_ref, a0, a1, a2, weight_ref, total_ref):
@@ -419,37 +425,35 @@
     kv = [kv[0]] + [along_y(kv[by], by) for by in (1, 2, 3)]
     q = call(q_kernel, [bf16(SLAB, 512)] * 4, [place], [queries], 1e6, 4)
     q = [q[0]] + [along_y(q[by], by) for by in (1, 2, 3)]
-    own, last, table = call(
-        slots_kernel, [bf16(1024, 128), bf16(SLAB, 256), TABLE],
-        [place, vertical, slash.T], kv, 1e6, 4, (), None, [VMEM, VMEM, SMEM],
-    )
+    table = call(table_kernel, [TABLE], [place, vertical, slash.T], [], 1e6, 4, (), None, [SMEM])[0]
+    own, last = call(slots_kernel, [bf16(1024, 128), bf16(SLAB, 256)], [table], kv, 1e6, 4)
     hops = [first_hop(own, by) for by in (1, 2, 3)]
     prev = to_next_group(last)
     near = call(join_kernel, [bf16(4096, 128)], [], [own, *hops], 1e6, 4)[0]
     plus, minus = second_hop(near, 1), second_hop(near, 3)
     beyond = [second_hop(plus[:2048], 1), second_hop(minus[2048:], 3)]
     ql, *state, table = call(
-        local_kernel, [bf16(16, 256, 128)] + STATE + [TABLE], [table], [*q, *kv, prev], 3e9, 6,
-        [pltpu.VMEM((5 * SLAB, 128), jnp.bfloat16)] * 2, None, [VMEM] * 4 + [SMEM],
+        local_kernel, [bf16(16, 256, 128)] + PACKED + STATE + [TABLE], [table], [*q, *kv, prev, near], 3e9, 6,
+        [pltpu.VMEM((5 * SLAB, 128), jnp.bfloat16)] * 2, None, [VMEM] * 6 + [SMEM],
     )
     state = call(
         functools.partial(part_kernel, 0, EVERY), PACKED + STATE, [table],
-        [near, ql, *state], 5e9, 8, WORK, {3 + n: 2 + n for n in range(3)},
-    )
-    state = call(
-        functools.partial(part_kernel, 1, EVERY), PACKED + STATE, [table],
-        [plus, minus, ql, *state], 1e10, 8, WORK, {4 + n: n for n in range(5)},
+        [plus, minus, ql, *state], 1.5e10, 8, WORK, {4 + n: n for n in range(5)},
     )
     *state, a2, a1 = call(
-        functools.partial(part_kernel, 2, (2, 1)), PACKED + STATE + [bf16(SLAB, 512)] * 2, [table],
+        functools.partial(part_kernel, 1, (2, 1)), PACKED + STATE + [bf16(SLAB, 512)] * 2, [table],
         [*beyond, ql, *state], 3e9, 8, WORK, {4 + n: n for n in range(5)},
     )
     a2, a1 = along_y(a2, -2), along_y(a1, -1)
-    *state, a3, a0 = call(
-        functools.partial(part_kernel, 3, (3, 0)), PACKED + STATE + [bf16(SLAB, 512)] * 2, [table],
-        [ql, *state], 3e9, 8, WORK, {2 + n: n for n in range(5)},
+    *state, a3 = call(
+        functools.partial(part_kernel, 2, (3,)), PACKED + STATE + [bf16(SLAB, 512)], [table],
+        [ql, *state], 2e9, 8, WORK, {2 + n: n for n in range(5)},
     )
     a3 = along_y(a3, -3)
+    *state, a0 = call(
+        functools.partial(part_kernel, 2, (0,)), PACKED + STATE + [bf16(SLAB, 512)], [table],
+        [ql, *state], 2e9, 8, WORK, {2 + n: n for n in range(5)},
+    )
     total = call(early_kernel, [f32(SLAB, 4096)], [place], [a0, a1, a2, out_weight], 3e9, 6)[0]
     theirs, mine = (
         call(functools.partial(last_kernel, own), [out], [place], [a3, out_weight, total], 1e9, 6)[0]

time: 104 us -> 105 us (level)
  the two profiles are of different devices: /device:TPU:37 before, /device:TPU:13 now
where the time goes in v5:
time: 105 us
  Pallas kernels  45.7 us (44%)
  waiting for transfers between devices  30.5 us (29%)
  starting transfers between devices  24 us (23%)
  local copies, waits for them, and re-layouts  3.5 us (3%)
  other arithmetic  1.22 us (1%)
    pallas_call x13, Pallas kernels, call(): pl.pallas_call(kernel, out_shape=outs, in_specs=[SMEM] * len(scalars) + [...  45.7 us
    ppermute x18, waiting for transfers between devices, moved(): return lax.ppermute(value, ALL, pairs)  30.5 us
    ppermute x18, starting transfers between devices, moved(): return lax.ppermute(value, ALL, pairs)  24 us
    unnamed x18, local copies, waits for them, and re-layouts  3.35 us
  transfers between devices with their start and end apart: 18, of which 8 were waited for; matrix products, arithmetic and copies ran while one was open for 0% of the time, Pallas kernels for 30%

profile of v5, /device:TPU:13, one launch (start us, length us, event | category | flops | bytes accessed | tf_op | source)
XLA Modules:
  0.0 105.2 jit_solution(3668870873101694615)
XLA Ops:
  0.0 0.1 stack.23.place_ref
  0.1 1.0 copy-done.1
  1.1 0.9 copy-done.2
  2.1 0.6 shard_map.66
  2.7 1.4 %collective-permute-start.3 = (bf16[256,256]{1,0:T(8,128)(2,1)S(1)}, bf16[256,256]{1,0:T(8,128)(2,1)S(1)}, u32[]{:S(2)}, u32[]{:S(2)}) collective-permute-start(bf16[256,256]{1,0:T(8,128)(2,1)S(1)} %get-tuple-element.46), channel_id=1, source_target_pairs={{0,2},{1,3},{2,4},{3,5},{4,6},{5,7},{6,0},{7,1},{8,10},{9,11},{10,... | collective-permute-start | bytes 393224 | tf_op jit(solution)/shard_map/ppermute | solution.py:33
  4.1 0.8 collective-permute-start.4
  4.9 2.0 %collective-permute-start.5 = (bf16[256,256]{1,0:T(8,128)(2,1)S(1)}, bf16[256,256]{1,0:T(8,128)(2,1)S(1)}, u32[]{:S(2)}, u32[]{:S(2)}) collective-permute-start(bf16[256,256]{1,0:T(8,128)(2,1)S(1)} %get-tuple-element.48), channel_id=1, source_target_pairs={{0,6},{1,7},{2,0},{3,1},{4,2},{5,3},{6,4},{7,5},{8,14},{9,15},{10,... | collective-permute-start | bytes 393224 | tf_op jit(solution)/shard_map/ppermute | solution.py:33
  6.9 0.7 copy-done.3
  7.6 0.7 copy-done.4
  8.2 1.3 %shard_map.64.table_ref.place_ref = s32[128]{0:T(128)S(1)} custom-call(s32[5]{0:T(128)S(1)} %stack.23.place_ref, s32[4,64]{1,0:T(4,128)S(1)} %copy-done.3, s32[2,4]{1,0:T(2,128)S(1)} %bitcast.8), custom_call_target="tpu_custom_call" | custom-call | flops 1000000 | bytes 1000000 | tf_op jit(solution)/shard_map/pallas_call | solution.py:409
  9.5 0.3 collective-permute-done.4.kv2
  9.8 2.5 %collective-permute-done.5.kv3 = bf16[256,256]{1,0:T(8,128)(2,1)S(1)} collective-permute-done((bf16[256,256]{1,0:T(8,128)(2,1)S(1)}, bf16[256,256]{1,0:T(8,128)(2,1)S(1)}, u32[]{:S(2)}, u32[]{:S(2)}) %collective-permute-start.5) | collective-permute-done | bytes 131104 | tf_op jit(solution)/shard_map/ppermute | solution.py:33
  12.3 0.8 shard_map.67
  13.1 1.7 %collective-permute-start.7 = (bf16[1024,128]{1,0:T(8,128)(2,1)S(1)}, bf16[1024,128]{1,0:T(8,128)(2,1)S(1)}, u32[]{:S(2)}, u32[]{:S(2)}) collective-permute-start(bf16[1024,128]{1,0:T(8,128)(2,1)S(1)} %get-tuple-element.50.a0), channel_id=1, source_target_pairs={{0,32},{1,9},{2,34},{3,11},{4,36},{5,13},{6,38},{7,15},{8,40},{9,1... | collective-permute-start | bytes 786440 | tf_op jit(solution)/shard_map/ppermute | solution.py:33
  14.9 3.3 %collective-permute-start.8 = (bf16[1024,128]{1,0:T(8,128)(2,1)S(1)}, bf16[1024,128]{1,0:T(8,128)(2,1)S(1)}, u32[]{:S(2)}, u32[]{:S(2)}) collective-permute-start(bf16[1024,128]{1,0:T(8,128)(2,1)S(1)} %get-tuple-element.50.a0), channel_id=1, source_target_pairs={{0,64},{1,17},{2,66},{3,19},{4,68},{5,21},{6,70},{7,23},{8,72},{9,... | collective-permute-start | bytes 786440 | tf_op jit(solution)/shard_map/ppermute | solution.py:33
  18.2 0.7 collective-permute-start.9
  18.9 2.0 %collective-permute-done.7.a1 = bf16[1024,128]{1,0:T(8,128)(2,1)S(1)} collective-permute-done((bf16[1024,128]{1,0:T(8,128)(2,1)S(1)}, bf16[1024,128]{1,0:T(8,128)(2,1)S(1)}, u32[]{:S(2)}, u32[]{:S(2)}) %collective-permute-start.7) | collective-permute-done | bytes 262176 | tf_op jit(solution)/shard_map/ppermute | solution.py:33
  20.9 3.8 %collective-permute-done.8.a2 = bf16[1024,128]{1,0:T(8,128)(2,1)S(1)} collective-permute-done((bf16[1024,128]{1,0:T(8,128)(2,1)S(1)}, bf16[1024,128]{1,0:T(8,128)(2,1)S(1)}, u32[]{:S(2)}, u32[]{:S(2)}) %collective-permute-start.8) | collective-permute-done | bytes 262176 | tf_op jit(solution)/shard_map/ppermute | solution.py:33
  24.7 0.0 collective-permute-done.9.a3
  24.7 0.1 shard_map.68.near
  24.8 1.0 collective-permute-start.10
  25.8 0.5 collective-permute-start.12
  26.3 1.2 %collective-permute-start.6 = (bf16[256,256]{1,0:T(8,128)(2,1)S(1)}, bf16[256,256]{1,0:T(8,128)(2,1)S(1)}, u32[]{:S(2)}, u32[]{:S(2)}) collective-permute-start(bf16[256,256]{1,0:T(8,128)(2,1)S(1)} %get-tuple-element.49), channel_id=1, source_target_pairs={{0,8},{1,9},{2,10},{3,11},{4,12},{5,13},{6,14},{7,15},{8,16},{9,17... | collective-permute-start | bytes 393224 | tf_op jit(solution)/shard_map/ppermute | solution.py:33
  27.6 0.6 shard_map.65
  28.2 0.6 collective-permute-start
  28.8 1.5 %collective-permute-start.1 = (bf16[256,512]{1,0:T(8,128)(2,1)S(1)}, bf16[256,512]{1,0:T(8,128)(2,1)S(1)}, u32[]{:S(2)}, u32[]{:S(2)}) collective-permute-start(bf16[256,512]{1,0:T(8,128)(2,1)S(1)} %get-tuple-element.43), channel_id=1, source_target_pairs={{0,4},{1,5},{2,6},{3,7},{4,0},{5,1},{6,2},{7,3},{8,12},{9,13},{10,... | collective-permute-start | bytes 786440 | tf_op jit(solution)/shard_map/ppermute | solution.py:33
  30.3 12.8 %collective-permute-done.6.prev_ref = bf16[256,256]{1,0:T(8,128)(2,1)S(1)} collective-permute-done((bf16[256,256]{1,0:T(8,128)(2,1)S(1)}, bf16[256,256]{1,0:T(8,128)(2,1)S(1)}, u32[]{:S(2)}, u32[]{:S(2)}) %collective-permute-start.6) | collective-permute-done | bytes 131104 | tf_op jit(solution)/shard_map/ppermute | solution.py:33
  43.2 0.5 collective-permute-start.2
  43.7 7.5 %collective-permute-done.2.q3 = bf16[256,512]{1,0:T(8,128)(2,1)S(1)} collective-permute-done((bf16[256,512]{1,0:T(8,128)(2,1)S(1)}, bf16[256,512]{1,0:T(8,128)(2,1)S(1)}, u32[]{:S(2)}, u32[]{:S(2)}) %collective-permute-start.2) | collective-permute-done | bytes 262176 | tf_op jit(solution)/shard_map/ppermute | solution.py:33
  51.1 4.2 %shard_map.69 = (bf16[16,256,128]{2,1,0:T(8,128)(2,1)S(1)}, bf16[4096,128]{1,0:T(8,128)(2,1)S(1)}, bf16[4096,128]{1,0:T(8,128)(2,1)S(1)}, f32[16,8,256]{2,1,0:T(...) custom-call(s32[128]{0:T(128)S(1)} %shard_map.64.table_ref.place_ref, ...), custom_call_target="tpu_custom_call" | custom-call | flops 3000000000 | bytes 1000000 | tf_op jit(solution)/shard_map/pallas_call | solution.py:409
  55.4 0.0 collective-permute-done.10.refs_0_
  55.4 0.8 collective-permute-start.11
  56.2 0.8 collective-permute-start.13
  57.1 6.9 %shard_map.70 = (bf16[4096,128]{1,0:T(8,128)(2,1)S(1)}, bf16[4096,128]{1,0:T(8,128)(2,1)S(1)}, f32[16,8,256]{2,1,0:T(8,128)S(1)}, f32[16,8,256]{2,1,0:T(8,128)S(1)}, f32[16,128,256]{2,1,0:T(8,128)S(1)}) custom-call(s32[128]{0:T(128)S(1)} %get-tuple-element.51.table_ref, ...), custom_call_target="tpu_custom_call", output_to_operand_aliasing={{0}: (4, {}), {1}: (5, {}), {2}: (6, {}), {3}: (7, {}), {4}... | custom-call | flops 15000000512 | bytes 1000000 | tf_op jit(solution)/shard_map/pallas_call | solution.py:409
  64.0 0.0 collective-permute-done.11.refs_0_
  64.1 0.6 collective-permute-done.13.refs_1_
  64.6 11.8 %shard_map.71 = (bf16[4096,128]{1,0:T(8,128)(2,1)S(1)}, bf16[4096,128]{1,0:T(8,128)(2,1)S(1)}, f32[16,8,256]{2,1,0:T(8,128)S(1)}, f32[16,8,256]{2,1,0:T(8,128)S(...) custom-call(s32[128]{0:T(128)S(1)} %get-tuple-element.51.table_ref, ...), custom_call_target="tpu_custom_call", output_to_operand_aliasing={{0}: (4, {}), {1}: (5, {}), {2}: (6, {}), {3}: (7, {}), {4}... | custom-call | flops 3000000000 | bytes 1000000 | tf_op jit(solution)/shard_map/pallas_call | solution.py:409
  76.4 0.7 collective-permute-start.15
  77.1 2.3 %collective-permute-start.16 = (bf16[256,512]{1,0:T(8,128)(2,1)S(1)}, bf16[256,512]{1,0:T(8,128)(2,1)S(1)}, u32[]{:S(2)}, u32[]{:S(2)}) collective-permute-start(bf16[256,512]{1,0:T(8,128)(2,1)S(1)} %get-tuple-element.76), channel_id=1, source_target_pairs={{0,4},{1,5},{2,6},{3,7},{4,0},{5,1},{6,2},{7,3},{8,12},{9,13},{10,... | collective-permute-start | bytes 786440 | tf_op jit(solution)/shard_map/ppermute | solution.py:33
  79.4 6.3 %shard_map.72 = (bf16[4096,128]{1,0:T(8,128)(2,1)S(1)}, bf16[4096,128]{1,0:T(8,128)(2,1)S(1)}, f32[16,8,256]{2,1,0:T(8,128)S(1)}, f32[16,8,256]{2,1,0:T(8,128)S(...) custom-call(s32[128]{0:T(128)S(1)} %get-tuple-element.51.table_ref, ...), custom_call_target="tpu_custom_call", output_to_operand_aliasing={{0}: (2, {}), {1}: (3, {}), {2}: (4, {}), {3}: (5, {}), {4}... | custom-call | flops 2000000000 | bytes 1000000 | tf_op jit(solution)/shard_map/pallas_call | solution.py:409
  85.7 0.9 collective-permute-start.14
  86.6 6.5 %shard_map.73 = (bf16[4096,128]{1,0:T(8,128)(2,1)S(1)}, bf16[4096,128]{1,0:T(8,128)(2,1)S(1)}, f32[16,8,256]{2,1,0:T(8,128)S(1)}, f32[16,8,256]{2,1,0:T(8,128)S(...) custom-call(s32[128]{0:T(128)S(1)} %get-tuple-element.51.table_ref, ...), custom_call_target="tpu_custom_call", output_to_operand_aliasing={{0}: (2, {}), {1}: (3, {}), {2}: (4, {}), {3}: (5, {}), {4}... | custom-call | flops 2000000000 | bytes 1000000 | tf_op jit(solution)/shard_map/pallas_call | solution.py:409
  93.2 4.0 %shard_map.74.total_ref = f32[256,4096]{1,0:T(8,128)S(1)} custom-call(s32[5]{0:T(128)S(1)} %stack.23.place_ref, bf16[256,512]{1,0:T(8,128)(2,1)S(1)} %get-tuple-element.74.a0, bf16[256,512]{1,0:T(8,128)(2,1)S(1)} %collective-permute-done.15.a1, bf16[256,512]{1,0:T(8,128)(2,1)S(1)} %collective-permute-done.16.a2, bf16[2048,4096]{1,0:T(8,128)(2,1)S(1)} %bitcast.7), custom_call_target="tpu_custom_call" | custom-call | flops 3000000000 | bytes 1000000 | tf_op jit(solution)/shard_map/pallas_call | solution.py:409
  97.1 1.3 %shard_map.76 = bf16[128,4096]{1,0:T(8,128)(2,1)S(1)} custom-call(s32[5]{0:T(128)S(1)} %stack.23.place_ref, bf16[256,512]{1,0:T(8,128)(2,1)S(1)} %collective-permute-done.14.a, bf16[2048,4096]{1,0:T(8,128)(2,1)S(1)} %bitcast.7, f32[256,4096]{1,0:T(8,128)S(1)} %shard_map.74.total_ref), custom_call_target="tpu_custom_call" | custom-call | flops 1000000000 | bytes 1000000 | tf_op jit(solution)/shard_map/pallas_call | solution.py:409
  98.4 3.3 %collective-permute-start.17 = (bf16[128,4096]{1,0:T(8,128)(2,1)S(1)}, bf16[128,4096]{1,0:T(8,128)(2,1)S(1)}, u32[]{:S(2)}, u32[]{:S(2)}) collective-permute-start(bf16[128,4096]{1,0:T(8,128)(2,1)S(1)} %shard_map.76), channel_id=1, source_target_pairs={{0,1},{1,0},{2,3},{3,2},{4,5},{5,4},{6,7},{7,6},{8,9},{9,8},{10,11... | collective-permute-start | bytes 3145736 | tf_op jit(solution)/shard_map/ppermute | solution.py:33
  101.7 1.3 %shard_map.75 = f32[128,4096]{1,0:T(8,128)S(1)} custom-call(s32[5]{0:T(128)S(1)} %stack.23.place_ref, bf16[256,512]{1,0:T(8,128)(2,1)S(1)} %collective-permute-done.14.a, bf16[2048,4096]{1,0:T(8,128)(2,1)S(1)} %bitcast.7, f32[256,4096]{1,0:T(8,128)S(1)} %shard_map.74.total_ref), custom_call_target="tpu_custom_call" | custom-call | flops 1000000000 | bytes 1000000 | tf_op jit(solution)/shard_map/pallas_call | solution.py:409
  103.0 1.0 collective-permute-done.17
  104.0 1.2 %add_convert_fusion = bf16[128,4096]{1,0:T(8,128)(2,1)} fusion(f32[128,4096]{1,0:T(8,128)S(1)} %shard_map.75, bf16[128,4096]{1,0:T(8,128)(2,1)S(1)} %collective-permute-done.17), kind=kLoop, calls=%fused_computation | loop fusion | flops 1572864 | bytes 4194304 | tf_op jit(solution)/shard_map/convert_element_type | solution.py:463
  (24 shorter events, 0.1 us)
Async XLA Ops:
  0.0 27.6 %copy-start = (bf16[256,2048]{1,0:T(8,128)(2,1)S(1)}, bf16[256,2048]{1,0:T(8,128)(2,1)}, u32[]{:S(2)}) copy-start(bf16[256,2048]{1,0:T(8,128)(2,1)} %queries_ref.1) | copy-start | bytes 3145732
  0.1 1.0 copy-start.1
  1.1 0.9 copy-start.2
  2.7 6.8 %collective-permute-start.3 = (bf16[256,256]{1,0:T(8,128)(2,1)S(1)}, bf16[256,256]{1,0:T(8,128)(2,1)S(1)}, u32[]{:S(2)}, u32[]{:S(2)}) collective-permute-start(bf16[256,256]{1,0:T(8,128)(2,1)S(1)} %get-tuple-element.46), channel_id=1, source_target_pairs={{0,2},{1,3},{2,4},{3,5},{4,6},{5,7},{6,0},{7,1},{8,10},{9,11},{10,... | collective-permute-start | bytes 393224 | tf_op jit(solution)/shard_map/ppermute | solution.py:33
  4.1 5.7 %collective-permute-start.4 = (bf16[256,256]{1,0:T(8,128)(2,1)S(1)}, bf16[256,256]{1,0:T(8,128)(2,1)S(1)}, u32[]{:S(2)}, u32[]{:S(2)}) collective-permute-start(bf16[256,256]{1,0:T(8,128)(2,1)S(1)} %get-tuple-element.47), channel_id=1, source_target_pairs={{0,4},{1,5},{2,6},{3,7},{4,0},{5,1},{6,2},{7,3},{8,12},{9,13},{10,... | collective-permute-start | bytes 393224 | tf_op jit(solution)/shard_map/ppermute | solution.py:33
  4.9 7.4 %collective-permute-start.5 = (bf16[256,256]{1,0:T(8,128)(2,1)S(1)}, bf16[256,256]{1,0:T(8,128)(2,1)S(1)}, u32[]{:S(2)}, u32[]{:S(2)}) collective-permute-start(bf16[256,256]{1,0:T(8,128)(2,1)S(1)} %get-tuple-element.48), channel_id=1, source_target_pairs={{0,6},{1,7},{2,0},{3,1},{4,2},{5,3},{6,4},{7,5},{8,14},{9,15},{10,... | collective-permute-start | bytes 393224 | tf_op jit(solution)/shard_map/ppermute | solution.py:33
  6.9 0.7 copy-start.3
  7.6 0.7 copy-start.4
  13.1 7.7 %collective-permute-start.7 = (bf16[1024,128]{1,0:T(8,128)(2,1)S(1)}, bf16[1024,128]{1,0:T(8,128)(2,1)S(1)}, u32[]{:S(2)}, u32[]{:S(2)}) collective-permute-start(bf16[1024,128]{1,0:T(8,128)(2,1)S(1)} %get-tuple-element.50.a0), channel_id=1, source_target_pairs={{0,32},{1,9},{2,34},{3,11},{4,36},{5,13},{6,38},{7,15},{8,40},{9,1... | collective-permute-start | bytes 786440 | tf_op jit(solution)/shard_map/ppermute | solution.py:33
  14.9 9.9 %collective-permute-start.8 = (bf16[1024,128]{1,0:T(8,128)(2,1)S(1)}, bf16[1024,128]{1,0:T(8,128)(2,1)S(1)}, u32[]{:S(2)}, u32[]{:S(2)}) collective-permute-start(bf16[1024,128]{1,0:T(8,128)(2,1)S(1)} %get-tuple-element.50.a0), channel_id=1, source_target_pairs={{0,64},{1,17},{2,66},{3,19},{4,68},{5,21},{6,70},{7,23},{8,72},{9,... | collective-permute-start | bytes 786440 | tf_op jit(solution)/shard_map/ppermute | solution.py:33
  18.2 6.6 %collective-permute-start.9 = (bf16[1024,128]{1,0:T(8,128)(2,1)S(1)}, bf16[1024,128]{1,0:T(8,128)(2,1)S(1)}, u32[]{:S(2)}, u32[]{:S(2)}) collective-permute-start(bf16[1024,128]{1,0:T(8,128)(2,1)S(1)} %get-tuple-element.50.a0), channel_id=1, source_target_pairs={{0,96},{1,25},{2,98},{3,27},{4,100},{5,29},{6,102},{7,31},{8,104},... | collective-permute-start | bytes 786440 | tf_op jit(solution)/shard_map/ppermute | solution.py:33
  24.8 30.6 %collective-permute-start.10 = (bf16[4096,128]{1,0:T(8,128)(2,1)S(1)}, bf16[4096,128]{1,0:T(8,128)(2,1)S(1)}, u32[]{:S(2)}, u32[]{:S(2)}) collective-permute-start(bf16[4096,128]{1,0:T(8,128)(2,1)S(1)} %shard_map.68.near), channel_id=1, source_target_pairs={{0,8},{1,33},{2,10},{3,35},{4,12},{5,37},{6,14},{7,39},{8,16},{9,4... | collective-permute-start | bytes 3145736 | tf_op jit(solution)/shard_map/ppermute | solution.py:33
  25.8 30.4 %collective-permute-start.12 = (bf16[4096,128]{1,0:T(8,128)(2,1)S(1)}, bf16[4096,128]{1,0:T(8,128)(2,1)S(1)}, u32[]{:S(2)}, u32[]{:S(2)}) collective-permute-start(bf16[4096,128]{1,0:T(8,128)(2,1)S(1)} %shard_map.68.near), channel_id=1, source_target_pairs={{0,24},{1,97},{2,26},{3,99},{4,28},{5,101},{6,30},{7,103},{8,0},{9... | collective-permute-start | bytes 3145736 | tf_op jit(solution)/shard_map/ppermute | solution.py:33
  26.3 16.8 %collective-permute-start.6 = (bf16[256,256]{1,0:T(8,128)(2,1)S(1)}, bf16[256,256]{1,0:T(8,128)(2,1)S(1)}, u32[]{:S(2)}, u32[]{:S(2)}) collective-permute-start(bf16[256,256]{1,0:T(8,128)(2,1)S(1)} %get-tuple-element.49), channel_id=1, source_target_pairs={{0,8},{1,9},{2,10},{3,11},{4,12},{5,13},{6,14},{7,15},{8,16},{9,17... | collective-permute-start | bytes 393224 | tf_op jit(solution)/shard_map/ppermute | solution.py:33
  28.2 15.5 %collective-permute-start = (bf16[256,512]{1,0:T(8,128)(2,1)S(1)}, bf16[256,512]{1,0:T(8,128)(2,1)S(1)}, u32[]{:S(2)}, u32[]{:S(2)}) collective-permute-start(bf16[256,512]{1,0:T(8,128)(2,1)S(1)} %get-tuple-element.42), channel_id=1, source_target_pairs={{0,2},{1,3},{2,4},{3,5},{4,6},{5,7},{6,0},{7,1},{8,10},{9,11},{10,... | collective-permute-start | bytes 786440 | tf_op jit(solution)/shard_map/ppermute | solution.py:33
  28.8 14.9 %collective-permute-start.1 = (bf16[256,512]{1,0:T(8,128)(2,1)S(1)}, bf16[256,512]{1,0:T(8,128)(2,1)S(1)}, u32[]{:S(2)}, u32[]{:S(2)}) collective-permute-start(bf16[256,512]{1,0:T(8,128)(2,1)S(1)} %get-tuple-element.43), channel_id=1, source_target_pairs={{0,4},{1,5},{2,6},{3,7},{4,0},{5,1},{6,2},{7,3},{8,12},{9,13},{10,... | collective-permute-start | bytes 786440 | tf_op jit(solution)/shard_map/ppermute | solution.py:33
  43.2 8.0 %collective-permute-start.2 = (bf16[256,512]{1,0:T(8,128)(2,1)S(1)}, bf16[256,512]{1,0:T(8,128)(2,1)S(1)}, u32[]{:S(2)}, u32[]{:S(2)}) collective-permute-start(bf16[256,512]{1,0:T(8,128)(2,1)S(1)} %get-tuple-element.44), channel_id=1, source_target_pairs={{0,6},{1,7},{2,0},{3,1},{4,2},{5,3},{6,4},{7,5},{8,14},{9,15},{10,... | collective-permute-start | bytes 786440 | tf_op jit(solution)/shard_map/ppermute | solution.py:33
  55.4 8.6 %collective-permute-start.11 = (bf16[2048,128]{1,0:T(8,128)(2,1)S(1)}, bf16[2048,128]{1,0:T(8,128)(2,1)S(1)}, u32[]{:S(2)}, u32[]{:S(2)}) collective-permute-start(bf16[2048,128]{1,0:T(8,128)(2,1)S(1)} %slice.8), channel_id=1, source_target_pairs={{0,8},{1,33},{2,10},{3,35},{4,12},{5,37},{6,14},{7,39},{8,16},{9,4... | collective-permute-start | bytes 1572872 | tf_op jit(solution)/shard_map/ppermute | solution.py:33
  56.2 8.4 %collective-permute-start.13 = (bf16[2048,128]{1,0:T(8,128)(2,1)S(1)}, bf16[2048,128]{1,0:T(8,128)(2,1)S(1)}, u32[]{:S(2)}, u32[]{:S(2)}) collective-permute-start(bf16[2048,128]{1,0:T(8,128)(2,1)S(1)} %slice.9), channel_id=1, source_target_pairs={{0,24},{1,97},{2,26},{3,99},{4,28},{5,101},{6,30},{7,103},{8,0},{9... | collective-permute-start | bytes 1572872 | tf_op jit(solution)/shard_map/ppermute | solution.py:33
  57.1 36.0 %slice-start = ((s8[16777216]{0:T(1024)(128)(4,1)}), s8[4194304]{0:T(1024)(128)(4,1)S(1)}, s32[]{:S(2)}) async-start(s8[16777216]{0:T(1024)(128)(4,1)} %bitcast.6), calls=%async_computation | async-start | bytes 8388608
  57.1 36.0 %slice-start.1 = ((s8[16777216]{0:T(1024)(128)(4,1)}), s8[4194304]{0:T(1024)(128)(4,1)S(1)}, s32[]{:S(2)}) async-start(s8[16777216]{0:T(1024)(128)(4,1)} %bitcast.6), calls=%async_computation.1 | async-start | bytes 8388608
  57.1 36.0 %slice-start.2 = ((s8[16777216]{0:T(1024)(128)(4,1)}), s8[4194304]{0:T(1024)(128)(4,1)S(1)}, s32[]{:S(2)}) async-start(s8[16777216]{0:T(1024)(128)(4,1)} %bitcast.6), calls=%async_computation.2 | async-start | bytes 8388608
  64.6 28.5 %slice-start.3 = ((s8[16777216]{0:T(1024)(128)(4,1)}), s8[4194304]{0:T(1024)(128)(4,1)S(1)}, s32[]{:S(2)}) async-start(s8[16777216]{0:T(1024)(128)(4,1)} %bitcast.6), calls=%async_computation.3 | async-start | bytes 8388608
  76.4 16.6 %collective-permute-start.15 = (bf16[256,512]{1,0:T(8,128)(2,1)S(1)}, bf16[256,512]{1,0:T(8,128)(2,1)S(1)}, u32[]{:S(2)}, u32[]{:S(2)}) collective-permute-start(bf16[256,512]{1,0:T(8,128)(2,1)S(1)} %get-tuple-element.75), channel_id=1, source_target_pairs={{0,6},{1,7},{2,0},{3,1},{4,2},{5,3},{6,4},{7,5},{8,14},{9,15},{10,... | collective-permute-start | bytes 786440 | tf_op jit(solution)/shard_map/ppermute | solution.py:33
  77.1 16.0 %collective-permute-start.16 = (bf16[256,512]{1,0:T(8,128)(2,1)S(1)}, bf16[256,512]{1,0:T(8,128)(2,1)S(1)}, u32[]{:S(2)}, u32[]{:S(2)}) collective-permute-start(bf16[256,512]{1,0:T(8,128)(2,1)S(1)} %get-tuple-element.76), channel_id=1, source_target_pairs={{0,4},{1,5},{2,6},{3,7},{4,0},{5,1},{6,2},{7,3},{8,12},{9,13},{10,... | collective-permute-start | bytes 786440 | tf_op jit(solution)/shard_map/ppermute | solution.py:33
  85.7 11.4 %collective-permute-start.14 = (bf16[256,512]{1,0:T(8,128)(2,1)S(1)}, bf16[256,512]{1,0:T(8,128)(2,1)S(1)}, u32[]{:S(2)}, u32[]{:S(2)}) collective-permute-start(bf16[256,512]{1,0:T(8,128)(2,1)S(1)} %get-tuple-element.68), channel_id=1, source_target_pairs={{0,2},{1,3},{2,4},{3,5},{4,6},{5,7},{6,0},{7,1},{8,10},{9,11},{10,... | collective-permute-start | bytes 786440 | tf_op jit(solution)/shard_map/ppermute | solution.py:33
  98.4 5.6 %collective-permute-start.17 = (bf16[128,4096]{1,0:T(8,128)(2,1)S(1)}, bf16[128,4096]{1,0:T(8,128)(2,1)S(1)}, u32[]{:S(2)}, u32[]{:S(2)}) collective-permute-start(bf16[128,4096]{1,0:T(8,128)(2,1)S(1)} %shard_map.76), channel_id=1, source_target_pairs={{0,1},{1,0},{2,3},{3,2},{4,5},{5,4},{6,7},{7,6},{8,9},{9,8},{10,11... | collective-permute-start | bytes 3145736 | tf_op jit(solution)/shard_map/ppermute | solution.py:33

commit v6 on v5

--- a/solution.py
+++ b/solution.py
@@ -18,6 +18,7 @@
 VERT = 16
 NEVER = 1 << 20
 BOUNDS = 96
+COUNTS = 128
 ALL = ("x", "z", "y", "c")
 MIB = 1 << 20
 
@@ -80,8 +81,23 @@
         table_ref[n] = place_ref[n]
     for n in range(2):
         table_ref[SLASH + n] = slash_ref[n, y]
-    for n in range(NV):
-        table_ref[VERT + n] = vert_ref[y, n]
+    for n in range(64):
+        table_ref[COUNTS + n] = 0
+
+    def one(n, carry):
+        block = vert_ref[y, n]
+        table_ref[VERT + n] = block
+        slab = COUNTS + block // 4
+        table_ref[slab] = table_ref[slab] + 1
+        return carry
+
+    lax.fori_loop(0, NV, one, 0)
+    total = jnp.int32(0)
+    for g in range(16):
+        table_ref[BOUNDS + g] = total
+        for n in range(4):
+            total = total + table_ref[COUNTS + 4 * g + n]
+    table_ref[BOUNDS + 16] = total
 
 
 def slots_kernel(table_ref, kv0, kv1, kv2, kv3, own_ref, last_ref):
@@ -111,6 +127,7 @@
 
 CHUNK = 1024
 HALF = 512
+BIG = 2048
 EVERY = (0, 1, 2, 3)
 
 
@@ -156,45 +173,35 @@
     return place_ref[0] * 16 + ((place_ref[1] - i // 4 + 4) % 4) * 4 + i % 4
 
 
+def group_at(table_ref, outer, inner):
+    first = (table_ref[2] - inner + 4) % 4
+    second = (table_ref[3] - outer + 4) % 4
+    return jnp.where(table_ref[4] == 0, first * 4 + second, second * 4 + first)
+
+
 def count_of(table_ref, outer):
     total = jnp.int32(0)
     for inner in range(4):
-        start, end = span_of(table_ref, outer, inner)
-        total = total + end - start
+        g = group_at(table_ref, outer, inner)
+        total = total + jnp.where(g < table_ref[0], table_ref[BOUNDS + g + 1] - table_ref[BOUNDS + g], 0)
     return total
 
 
-def span_of(table_ref, outer, inner):
-    group, core = table_ref[0], table_ref[4]
-    first = (table_ref[2] - inner + 4) % 4
-    second = (table_ref[3] - outer + 4) % 4
-    g = jnp.where(core == 0, first * 4 + second, second * 4 + first)
-    start = table_ref[BOUNDS + g]
-    return start, jnp.where(g < group, table_ref[BOUNDS + g + 1], start)
-
-
-def pack(table_ref, start, end, at, source, base, kc, vc):
-    y = table_ref[1]
-
-    def one(entry, carry):
-        slab = table_ref[VERT + entry] // 4
-        before = table_ref[VERT + jnp.maximum(entry - 1, 0)] // 4
-        rank = jnp.where((entry > 0) & (before == slab), BLK, 0)
-        row = (base * 4 + (y - slab % 4 + 4) % 4) * 256 + rank
-        rows = pl.ds(pl.multiple_of((at + entry - start) * BLK, BLK), BLK)
-        kc[rows, :] = source[pl.ds(pl.multiple_of(row, BLK), BLK), :]
-        vc[rows, :] = source[pl.ds(pl.multiple_of(row + 128, BLK), BLK), :]
-        return carry
-
-    lax.fori_loop(start, end, one, 0)
-    return at + end - start
+def pack(table_ref, g, some, at, source, base, kc, vc):
+    for n in range(4):
+        row = pl.multiple_of((base * 4 + (table_ref[1] - n + 4) % 4) * 256, 256)
+        rows = pl.ds(pl.multiple_of(at * BLK, BLK), 2 * BLK)
+        kc[rows, :] = source[pl.ds(row, 128), :]
+        vc[rows, :] = source[pl.ds(row + 128, 128), :]
+        at = at + jnp.where(some, table_ref[COUNTS + 4 * g + n], 0)
+    return at
 
 
 def pack_all(table_ref, outer, at, sources, kc, vc):
     for inner in range(4):
-        start, end = span_of(table_ref, outer, inner)
+        g = group_at(table_ref, outer, inner)
         part = 4 // len(sources)
-        at = pack(table_ref, start, end, at, sources[inner // part], inner % part, kc, vc)
+        at = pack(table_ref, g, g < table_ref[0], at, sources[inner // part], inner % part, kc, vc)
     return at
 
 
@@ -258,7 +265,7 @@
 
 
 def part_kernel(stage, picks, table_ref, *refs):
-    splits = ((1, 1), (2,), ())[stage]
+    splits = ((1, 1), (2, 1), ())[stage]
     sources, refs = refs[: sum(splits)], refs[sum(splits) :]
     ql, refs = refs[0], refs[6:]
     kc, vc, top, tot, acc = refs[:5]
@@ -270,15 +277,19 @@
     if stage == 0:
         at = pack_all(table_ref, 1, at, sources[:1], kc, vc)
         at = pack_all(table_ref, 3, at, sources[1:], kc, vc)
-        chunks(CHUNK, 4, False, picks, table_ref, order, jnp.int32(0), at // 16, *work)
+        chunks(BIG, 2, False, picks, table_ref, order, jnp.int32(0), at // 32, *work)
+        chunks(CHUNK, 4, False, picks, table_ref, order, at // 32 * 32, at // 16 % 2, *work)
         return
     at = at + count_of(table_ref, 1) + count_of(table_ref, 3)
     begin = at // 16 * 16
     whole = (others - begin) // 16
     rest = begin + whole * 16
-    left = (total - rest + 7) // 8
+    long = (total - rest + 7) // 16
+    short = (jnp.maximum(total - rest - 16 * long, 0) + 7) // 8
+    end = rest + 16 * long + 8 * short
     if stage == 1:
-        pack_all(table_ref, 2, at, sources, kc, vc)
+        pack_all(table_ref, 2, at, sources[:2], kc, vc)
+        pack(table_ref, table_ref[0], True, others, sources[2], 0, kc, vc)
 
     def mark(n, carry):
         own = table_ref[VERT + jnp.minimum(n, NV - 1)]
@@ -290,9 +301,10 @@
 
         return carry
 
-    lax.fori_loop(rest, rest + left * 8, mark, 0)
+    lax.fori_loop(rest, end, mark, 0)
     chunks(CHUNK, 2 * len(picks), False, picks, table_ref, order, begin, whole, *work)
-    chunks(HALF, 2 * len(picks), True, picks, table_ref, order, rest, left, *work)
+    chunks(CHUNK, 2 * len(picks), True, picks, table_ref, order, rest, long, *work)
+    chunks(HALF, 2 * len(picks), True, picks, table_ref, order, rest + 16 * long, short, *work)
     for out, by in zip(outs, picks):
         for block in range(4):
             i = by * 4 + block
@@ -303,15 +315,9 @@
 
 def local_kernel(
     place_ref, q0, q1, q2, q3, kv0, kv1, kv2, kv3, prev_ref, near,
-    ql, kc, vc, top, tot, acc, table_ref, kl, vl
+    ql, kc, vc, top, tot, acc, kl, vl
 ):
     group, y = place_ref[0], place_ref[1]
-    for n in range(VERT + NV):
-        table_ref[n] = place_ref[n]
-    table_ref[BOUNDS] = 0
-    for g in range(1, 16):
-        table_ref[BOUNDS + g] = row_rank(place_ref, 16 * g)
-    table_ref[BOUNDS + 16] = NV
     kl[0:SLAB, :] = prev_ref[:, 0:128]
     vl[0:SLAB, :] = prev_ref[:, 128:256]
     for by, (q, kv) in enumerate(((q0, kv0), (q1, kv1), (q2, kv2), (q3, kv3))):
@@ -353,9 +359,7 @@
         return carry
 
     lax.fori_loop(0, 4, some, 0)
-    pack_all(table_ref, 0, jnp.int32(0), [near], kc, vc)
-    others, total = table_ref[BOUNDS + group], table_ref[BOUNDS + group + 1]
-    pack(table_ref, others, total, others, near, 0, kc, vc)
+    pack_all(place_ref, 0, jnp.int32(0), [near], kc, vc)
 
 
 def early_kernel(place_ref, a0, a1, a2, weight_ref, total_ref):
@@ -392,17 +396,23 @@
     return jax.ShapeDtypeStruct(shape, jnp.float32)
 
 
-TABLE = jax.ShapeDtypeStruct((128,), jnp.int32)
+TABLE = jax.ShapeDtypeStruct((192,), jnp.int32)
 STATE = [f32(16, 8, 256), f32(16, 8, 256), f32(16, 128, 256)]
-PACKED = [bf16(NV * BLK, 128)] * 2
-WORK = [
-    pltpu.SMEM((NV + 8,), jnp.int32),
-    pltpu.VMEM((128, CHUNK), jnp.bfloat16),
-    pltpu.VMEM((CHUNK, 256), jnp.float32),
-    pltpu.VMEM((CHUNK, 256), jnp.float32),
-    pltpu.VMEM((8, 256), jnp.float32),
-    pltpu.VMEM((8, 256), jnp.float32),
-]
+PACKED = [bf16((NV + 2) * BLK, 128)] * 2
+
+
+def work(size):
+    return [
+        pltpu.SMEM((NV + 16,), jnp.int32),
+        pltpu.VMEM((128, size), jnp.bfloat16),
+        pltpu.VMEM((size, 256), jnp.float32),
+        pltpu.VMEM((size, 256), jnp.float32),
+        pltpu.VMEM((8, 256), jnp.float32),
+        pltpu.VMEM((8, 256), jnp.float32),
+    ]
+
+
+WORK, LONG = work(CHUNK), work(BIG)
 
 
 def call(kernel, outs, scalars, arrays, flops, limit, scratch=(), aliases=None, places=None):
@@ -432,17 +442,17 @@
     near = call(join_kernel, [bf16(4096, 128)], [], [own, *hops], 1e6, 4)[0]
     plus, minus = second_hop(near, 1), second_hop(near, 3)
     beyond = [second_hop(plus[:2048], 1), second_hop(minus[2048:], 3)]
-    ql, *state, table = call(
-        local_kernel, [bf16(16, 256, 128)] + PACKED + STATE + [TABLE], [table], [*q, *kv, prev, near], 3e9, 6,
-        [pltpu.VMEM((5 * SLAB, 128), jnp.bfloat16)] * 2, None, [VMEM] * 6 + [SMEM],
+    ql, *state = call(
+        local_kernel, [bf16(16, 256, 128)] + PACKED + STATE, [table], [*q, *kv, prev, near], 3e9, 6,
+        [pltpu.VMEM((5 * SLAB, 128), jnp.bfloat16)] * 2,
     )
     state = call(
         functools.partial(part_kernel, 0, EVERY), PACKED + STATE, [table],
-        [plus, minus, ql, *state], 1.5e10, 8, WORK, {4 + n: n for n in range(5)},
+        [plus, minus, ql, *state], 1.5e10, 10, LONG, {4 + n: n for n in range(5)},
     )
     *state, a2, a1 = call(
         functools.partial(part_kernel, 1, (2, 1)), PACKED + STATE + [bf16(SLAB, 512)] * 2, [table],
-        [*beyond, ql, *state], 3e9, 8, WORK, {4 + n: n for n in range(5)},
+        [*beyond, near, ql, *state], 3e9, 8, WORK, {5 + n: n for n in range(5)},
     )
     a2, a1 = along_y(a2, -2), along_y(a1, -1)
     *state, a3 = call(

time: 105 us -> 101 us (0.962)
  the two profiles are of different devices: /device:TPU:13 before, /device:TPU:7 now
where the time goes in v6:
time: 101 us
  Pallas kernels  40.5 us (40%)
  starting transfers between devices  30.3 us (30%)
  waiting for transfers between devices  25.5 us (25%)
  local copies, waits for them, and re-layouts  3.51 us (3%)
  other arithmetic  1.22 us (1%)
    pallas_call x13, Pallas kernels, call(): pl.pallas_call(kernel, out_shape=outs, in_specs=[SMEM] * len(scalars) + [...  40.5 us
    ppermute x18, starting transfers between devices, moved(): return lax.ppermute(value, ALL, pairs)  30.3 us
    ppermute x18, waiting for transfers between devices, moved(): return lax.ppermute(value, ALL, pairs)  25.5 us
    unnamed x18, local copies, waits for them, and re-layouts  3.35 us
  transfers between devices with their start and end apart: 18, of which 6 were waited for; matrix products, arithmetic and copies ran while one was open for 0% of the time, Pallas kernels for 30%

profile of v6, /device:TPU:7, one launch (start us, length us, event | category | flops | bytes accessed | tf_op | source)
XLA Modules:
  0.0 101.3 jit_solution(3299347881679575974)
XLA Ops:
  0.0 0.1 stack.23.place_ref
  0.1 1.0 %copy-done.1 = bf16[256,512]{1,0:T(8,128)(2,1)S(1)} copy-done((bf16[256,512]{1,0:T(8,128)(2,1)S(1)}, bf16[256,512]{1,0:T(8,128)(2,1)}, u32[]{:S(2)}) %copy-start.1) | copy-done | bytes 262168
  1.1 0.9 copy-done.2
  2.1 0.6 shard_map.66
  2.7 1.4 %collective-permute-start.3 = (bf16[256,256]{1,0:T(8,128)(2,1)S(1)}, bf16[256,256]{1,0:T(8,128)(2,1)S(1)}, u32[]{:S(2)}, u32[]{:S(2)}) collective-permute-start(bf16[256,256]{1,0:T(8,128)(2,1)S(1)} %get-tuple-element.45), channel_id=1, source_target_pairs={{0,2},{1,3},{2,4},{3,5},{4,6},{5,7},{6,0},{7,1},{8,10},{9,11},{10,... | collective-permute-start | bytes 393224 | tf_op jit(solution)/shard_map/ppermute | solution.py:34
  4.1 2.6 %collective-permute-start.4 = (bf16[256,256]{1,0:T(8,128)(2,1)S(1)}, bf16[256,256]{1,0:T(8,128)(2,1)S(1)}, u32[]{:S(2)}, u32[]{:S(2)}) collective-permute-start(bf16[256,256]{1,0:T(8,128)(2,1)S(1)} %get-tuple-element.46), channel_id=1, source_target_pairs={{0,4},{1,5},{2,6},{3,7},{4,0},{5,1},{6,2},{7,3},{8,12},{9,13},{10,... | collective-permute-start | bytes 393224 | tf_op jit(solution)/shard_map/ppermute | solution.py:34
  6.7 1.1 %collective-permute-start.5 = (bf16[256,256]{1,0:T(8,128)(2,1)S(1)}, bf16[256,256]{1,0:T(8,128)(2,1)S(1)}, u32[]{:S(2)}, u32[]{:S(2)}) collective-permute-start(bf16[256,256]{1,0:T(8,128)(2,1)S(1)} %get-tuple-element.47), channel_id=1, source_target_pairs={{0,6},{1,7},{2,0},{3,1},{4,2},{5,3},{6,4},{7,5},{8,14},{9,15},{10,... | collective-permute-start | bytes 393224 | tf_op jit(solution)/shard_map/ppermute | solution.py:34
  7.8 0.7 copy-done.3
  8.5 0.7 copy-done.4
  9.1 2.3 %shard_map.64.table_ref.place_ref = s32[192]{0:T(256)S(1)} custom-call(s32[5]{0:T(128)S(1)} %stack.23.place_ref, s32[4,64]{1,0:T(4,128)S(1)} %copy-done.3, s32[2,4]{1,0:T(2,128)S(1)} %bitcast.8), custom_call_target="tpu_custom_call" | custom-call | flops 1000000 | bytes 1000000 | tf_op jit(solution)/shard_map/pallas_call | solution.py:419
  11.4 0.0 collective-permute-done.3.kv1
  11.4 1.0 collective-permute-done.4.kv2
  12.4 0.8 shard_map.67
  13.3 1.7 %collective-permute-start.7 = (bf16[1024,128]{1,0:T(8,128)(2,1)S(1)}, bf16[1024,128]{1,0:T(8,128)(2,1)S(1)}, u32[]{:S(2)}, u32[]{:S(2)}) collective-permute-start(bf16[1024,128]{1,0:T(8,128)(2,1)S(1)} %get-tuple-element.49.a0), channel_id=1, source_target_pairs={{0,32},{1,9},{2,34},{3,11},{4,36},{5,13},{6,38},{7,15},{8,40},{9,1... | collective-permute-start | bytes 786440 | tf_op jit(solution)/shard_map/ppermute | solution.py:34
  15.0 3.3 %collective-permute-start.8 = (bf16[1024,128]{1,0:T(8,128)(2,1)S(1)}, bf16[1024,128]{1,0:T(8,128)(2,1)S(1)}, u32[]{:S(2)}, u32[]{:S(2)}) collective-permute-start(bf16[1024,128]{1,0:T(8,128)(2,1)S(1)} %get-tuple-element.49.a0), channel_id=1, source_target_pairs={{0,64},{1,17},{2,66},{3,19},{4,68},{5,21},{6,70},{7,23},{8,72},{9,... | collective-permute-start | bytes 786440 | tf_op jit(solution)/shard_map/ppermute | solution.py:34
  18.3 0.7 collective-permute-start.9
  19.0 2.1 %collective-permute-done.7.a1 = bf16[1024,128]{1,0:T(8,128)(2,1)S(1)} collective-permute-done((bf16[1024,128]{1,0:T(8,128)(2,1)S(1)}, bf16[1024,128]{1,0:T(8,128)(2,1)S(1)}, u32[]{:S(2)}, u32[]{:S(2)}) %collective-permute-start.7) | collective-permute-done | bytes 262176 | tf_op jit(solution)/shard_map/ppermute | solution.py:34
  21.1 3.7 %collective-permute-done.8.a2 = bf16[1024,128]{1,0:T(8,128)(2,1)S(1)} collective-permute-done((bf16[1024,128]{1,0:T(8,128)(2,1)S(1)}, bf16[1024,128]{1,0:T(8,128)(2,1)S(1)}, u32[]{:S(2)}, u32[]{:S(2)}) %collective-permute-start.8) | collective-permute-done | bytes 262176 | tf_op jit(solution)/shard_map/ppermute | solution.py:34
  24.8 0.1 shard_map.68.near.refs_2_
  24.9 0.6 collective-permute-start.10
  25.5 1.0 collective-permute-start.12
  26.4 1.2 %collective-permute-start.6 = (bf16[256,256]{1,0:T(8,128)(2,1)S(1)}, bf16[256,256]{1,0:T(8,128)(2,1)S(1)}, u32[]{:S(2)}, u32[]{:S(2)}) collective-permute-start(bf16[256,256]{1,0:T(8,128)(2,1)S(1)} %get-tuple-element.48), channel_id=1, source_target_pairs={{0,8},{1,9},{2,10},{3,11},{4,12},{5,13},{6,14},{7,15},{8,16},{9,17... | collective-permute-start | bytes 393224 | tf_op jit(solution)/shard_map/ppermute | solution.py:34
  27.7 0.6 shard_map.65
  28.3 1.3 %collective-permute-start = (bf16[256,512]{1,0:T(8,128)(2,1)S(1)}, bf16[256,512]{1,0:T(8,128)(2,1)S(1)}, u32[]{:S(2)}, u32[]{:S(2)}) collective-permute-start(bf16[256,512]{1,0:T(8,128)(2,1)S(1)} %get-tuple-element.41), channel_id=1, source_target_pairs={{0,2},{1,3},{2,4},{3,5},{4,6},{5,7},{6,0},{7,1},{8,10},{9,11},{10,... | collective-permute-start | bytes 786440 | tf_op jit(solution)/shard_map/ppermute | solution.py:34
  29.6 2.2 %collective-permute-start.1 = (bf16[256,512]{1,0:T(8,128)(2,1)S(1)}, bf16[256,512]{1,0:T(8,128)(2,1)S(1)}, u32[]{:S(2)}, u32[]{:S(2)}) collective-permute-start(bf16[256,512]{1,0:T(8,128)(2,1)S(1)} %get-tuple-element.42), channel_id=1, source_target_pairs={{0,4},{1,5},{2,6},{3,7},{4,0},{5,1},{6,2},{7,3},{8,12},{9,13},{10,... | collective-permute-start | bytes 786440 | tf_op jit(solution)/shard_map/ppermute | solution.py:34
  31.8 11.9 %collective-permute-done.6.prev_ref = bf16[256,256]{1,0:T(8,128)(2,1)S(1)} collective-permute-done((bf16[256,256]{1,0:T(8,128)(2,1)S(1)}, bf16[256,256]{1,0:T(8,128)(2,1)S(1)}, u32[]{:S(2)}, u32[]{:S(2)}) %collective-permute-start.6) | collective-permute-done | bytes 131104 | tf_op jit(solution)/shard_map/ppermute | solution.py:34
  43.7 2.0 %collective-permute-start.2 = (bf16[256,512]{1,0:T(8,128)(2,1)S(1)}, bf16[256,512]{1,0:T(8,128)(2,1)S(1)}, u32[]{:S(2)}, u32[]{:S(2)}) collective-permute-start(bf16[256,512]{1,0:T(8,128)(2,1)S(1)} %get-tuple-element.43), channel_id=1, source_target_pairs={{0,6},{1,7},{2,0},{3,1},{4,2},{5,3},{6,4},{7,5},{8,14},{9,15},{10,... | collective-permute-start | bytes 786440 | tf_op jit(solution)/shard_map/ppermute | solution.py:34
  45.6 5.8 %collective-permute-done.2.q3 = bf16[256,512]{1,0:T(8,128)(2,1)S(1)} collective-permute-done((bf16[256,512]{1,0:T(8,128)(2,1)S(1)}, bf16[256,512]{1,0:T(8,128)(2,1)S(1)}, u32[]{:S(2)}, u32[]{:S(2)}) %collective-permute-start.2) | collective-permute-done | bytes 262176 | tf_op jit(solution)/shard_map/ppermute | solution.py:34
  51.4 3.4 %shard_map.69 = (bf16[16,256,128]{2,1,0:T(8,128)(2,1)S(1)}, bf16[4224,128]{1,0:T(8,128)(2,1)S(1)}, bf16[4224,128]{1,0:T(8,128)(2,1)S(1)}, f32[16,8,256]{2,1,0:T(...) custom-call(s32[192]{0:T(256)S(1)} %shard_map.64.table_ref.place_ref, ...), custom_call_target="tpu_custom_call" | custom-call | flops 3000000000 | bytes 1000000 | tf_op jit(solution)/shard_map/pallas_call | solution.py:419
  54.9 0.0 collective-permute-done.10.refs_0_
  54.9 0.7 collective-permute-start.11
  55.7 0.9 collective-permute-start.13
  56.6 11.1 %shard_map.70 = (bf16[4224,128]{1,0:T(8,128)(2,1)S(1)}, bf16[4224,128]{1,0:T(8,128)(2,1)S(1)}, f32[16,8,256]{2,1,0:T(8,128)S(1)}, f32[16,8,256]{2,1,0:T(8,128)S(1)}, f32[16,128,256]{2,1,0:T(8,128)S(1)}) custom-call(s32[192]{0:T(256)S(1)} %shard_map.64.table_ref.place_ref, ...), custom_call_target="tpu_custom_call", output_to_operand_aliasing={{0}: (4, {}), {1}: (5, {}), {2}: (6, {}), {3}: (7, {}), {4}... | custom-call | flops 15000000512 | bytes 1000000 | tf_op jit(solution)/shard_map/pallas_call | solution.py:419
  67.7 0.0 collective-permute-done.11.refs_0_
  67.7 0.0 slice-start.3
  67.8 6.9 %shard_map.71 = (bf16[4224,128]{1,0:T(8,128)(2,1)S(1)}, bf16[4224,128]{1,0:T(8,128)(2,1)S(1)}, f32[16,8,256]{2,1,0:T(8,128)S(1)}, f32[16,8,256]{2,1,0:T(8,128)S(...) custom-call(s32[192]{0:T(256)S(1)} %shard_map.64.table_ref.place_ref, ...), custom_call_target="tpu_custom_call", output_to_operand_aliasing={{0}: (5, {}), {1}: (6, {}), {2}: (7, {}), {3}: (8, {}), {4}... | custom-call | flops 3000000000 | bytes 1000000 | tf_op jit(solution)/shard_map/pallas_call | solution.py:419
  74.6 3.2 %collective-permute-start.15 = (bf16[256,512]{1,0:T(8,128)(2,1)S(1)}, bf16[256,512]{1,0:T(8,128)(2,1)S(1)}, u32[]{:S(2)}, u32[]{:S(2)}) collective-permute-start(bf16[256,512]{1,0:T(8,128)(2,1)S(1)} %get-tuple-element.73), channel_id=1, source_target_pairs={{0,6},{1,7},{2,0},{3,1},{4,2},{5,3},{6,4},{7,5},{8,14},{9,15},{10,... | collective-permute-start | bytes 786440 | tf_op jit(solution)/shard_map/ppermute | solution.py:34
  77.8 0.0 collective-permute-start.16
  77.8 4.2 %shard_map.72 = (bf16[4224,128]{1,0:T(8,128)(2,1)S(1)}, bf16[4224,128]{1,0:T(8,128)(2,1)S(1)}, f32[16,8,256]{2,1,0:T(8,128)S(1)}, f32[16,8,256]{2,1,0:T(8,128)S(...) custom-call(s32[192]{0:T(256)S(1)} %shard_map.64.table_ref.place_ref, ...), custom_call_target="tpu_custom_call", output_to_operand_aliasing={{0}: (2, {}), {1}: (3, {}), {2}: (4, {}), {3}: (5, {}), {4}... | custom-call | flops 2000000000 | bytes 1000000 | tf_op jit(solution)/shard_map/pallas_call | solution.py:419
  82.0 1.0 collective-permute-start.14
  83.0 4.0 %shard_map.73 = (bf16[4224,128]{1,0:T(8,128)(2,1)S(1)}, bf16[4224,128]{1,0:T(8,128)(2,1)S(1)}, f32[16,8,256]{2,1,0:T(8,128)S(1)}, f32[16,8,256]{2,1,0:T(8,128)S(...) custom-call(s32[192]{0:T(256)S(1)} %shard_map.64.table_ref.place_ref, ...), custom_call_target="tpu_custom_call", output_to_operand_aliasing={{0}: (2, {}), {1}: (3, {}), {2}: (4, {}), {3}: (5, {}), {4}... | custom-call | flops 2000000000 | bytes 1000000 | tf_op jit(solution)/shard_map/pallas_call | solution.py:419
  87.0 0.0 collective-permute-done.16.a2
  87.1 4.0 %shard_map.74.total_ref = f32[256,4096]{1,0:T(8,128)S(1)} custom-call(s32[5]{0:T(128)S(1)} %stack.23.place_ref, bf16[256,512]{1,0:T(8,128)(2,1)S(1)} %get-tuple-element.72.a0, bf16[256,512]{1,0:T(8,128)(2,1)S(1)} %collective-permute-done.15.a1, bf16[256,512]{1,0:T(8,128)(2,1)S(1)} %collective-permute-done.16.a2, bf16[2048,4096]{1,0:T(8,128)(2,1)S(1)} %bitcast.7), custom_call_target="tpu_custom_call" | custom-call | flops 3000000000 | bytes 1000000 | tf_op jit(solution)/shard_map/pallas_call | solution.py:419
  91.0 1.3 %shard_map.76 = bf16[128,4096]{1,0:T(8,128)(2,1)S(1)} custom-call(s32[5]{0:T(128)S(1)} %stack.23.place_ref, bf16[256,512]{1,0:T(8,128)(2,1)S(1)} %collective-permute-done.14.a, bf16[2048,4096]{1,0:T(8,128)(2,1)S(1)} %bitcast.7, f32[256,4096]{1,0:T(8,128)S(1)} %shard_map.74.total_ref), custom_call_target="tpu_custom_call" | custom-call | flops 1000000000 | bytes 1000000 | tf_op jit(solution)/shard_map/pallas_call | solution.py:419
  92.3 5.5 %collective-permute-start.17 = (bf16[128,4096]{1,0:T(8,128)(2,1)S(1)}, bf16[128,4096]{1,0:T(8,128)(2,1)S(1)}, u32[]{:S(2)}, u32[]{:S(2)}) collective-permute-start(bf16[128,4096]{1,0:T(8,128)(2,1)S(1)} %shard_map.76), channel_id=1, source_target_pairs={{0,1},{1,0},{2,3},{3,2},{4,5},{5,4},{6,7},{7,6},{8,9},{9,8},{10,11... | collective-permute-start | bytes 3145736 | tf_op jit(solution)/shard_map/ppermute | solution.py:34
  97.8 1.3 %shard_map.75 = f32[128,4096]{1,0:T(8,128)S(1)} custom-call(s32[5]{0:T(128)S(1)} %stack.23.place_ref, bf16[256,512]{1,0:T(8,128)(2,1)S(1)} %collective-permute-done.14.a, bf16[2048,4096]{1,0:T(8,128)(2,1)S(1)} %bitcast.7, f32[256,4096]{1,0:T(8,128)S(1)} %shard_map.74.total_ref), custom_call_target="tpu_custom_call" | custom-call | flops 1000000000 | bytes 1000000 | tf_op jit(solution)/shard_map/pallas_call | solution.py:419
  99.1 1.0 collective-permute-done.17
  100.1 1.2 %add_convert_fusion = bf16[128,4096]{1,0:T(8,128)(2,1)} fusion(f32[128,4096]{1,0:T(8,128)S(1)} %shard_map.75, bf16[128,4096]{1,0:T(8,128)(2,1)S(1)} %collective-permute-done.17), kind=kLoop, calls=%fused_computation | loop fusion | flops 1572864 | bytes 4194304 | tf_op jit(solution)/shard_map/convert_element_type | solution.py:473
  (24 shorter events, 0.1 us)
Async XLA Ops:
  0.0 27.7 %copy-start = (bf16[256,2048]{1,0:T(8,128)(2,1)S(1)}, bf16[256,2048]{1,0:T(8,128)(2,1)}, u32[]{:S(2)}) copy-start(bf16[256,2048]{1,0:T(8,128)(2,1)} %queries_ref.1) | copy-start | bytes 3145732
  0.1 1.0 %copy-start.1 = (bf16[256,512]{1,0:T(8,128)(2,1)S(1)}, bf16[256,512]{1,0:T(8,128)(2,1)}, u32[]{:S(2)}) copy-start(bf16[256,512]{1,0:T(8,128)(2,1)} %keys_ref.1) | copy-start | bytes 786436
  1.1 0.9 copy-start.2
  2.7 8.7 %collective-permute-start.3 = (bf16[256,256]{1,0:T(8,128)(2,1)S(1)}, bf16[256,256]{1,0:T(8,128)(2,1)S(1)}, u32[]{:S(2)}, u32[]{:S(2)}) collective-permute-start(bf16[256,256]{1,0:T(8,128)(2,1)S(1)} %get-tuple-element.45), channel_id=1, source_target_pairs={{0,2},{1,3},{2,4},{3,5},{4,6},{5,7},{6,0},{7,1},{8,10},{9,11},{10,... | collective-permute-start | bytes 393224 | tf_op jit(solution)/shard_map/ppermute | solution.py:34
  4.1 8.3 %collective-permute-start.4 = (bf16[256,256]{1,0:T(8,128)(2,1)S(1)}, bf16[256,256]{1,0:T(8,128)(2,1)S(1)}, u32[]{:S(2)}, u32[]{:S(2)}) collective-permute-start(bf16[256,256]{1,0:T(8,128)(2,1)S(1)} %get-tuple-element.46), channel_id=1, source_target_pairs={{0,4},{1,5},{2,6},{3,7},{4,0},{5,1},{6,2},{7,3},{8,12},{9,13},{10,... | collective-permute-start | bytes 393224 | tf_op jit(solution)/shard_map/ppermute | solution.py:34
  6.7 5.7 %collective-permute-start.5 = (bf16[256,256]{1,0:T(8,128)(2,1)S(1)}, bf16[256,256]{1,0:T(8,128)(2,1)S(1)}, u32[]{:S(2)}, u32[]{:S(2)}) collective-permute-start(bf16[256,256]{1,0:T(8,128)(2,1)S(1)} %get-tuple-element.47), channel_id=1, source_target_pairs={{0,6},{1,7},{2,0},{3,1},{4,2},{5,3},{6,4},{7,5},{8,14},{9,15},{10,... | collective-permute-start | bytes 393224 | tf_op jit(solution)/shard_map/ppermute | solution.py:34
  7.8 0.7 copy-start.3
  8.5 0.7 copy-start.4
  13.3 7.9 %collective-permute-start.7 = (bf16[1024,128]{1,0:T(8,128)(2,1)S(1)}, bf16[1024,128]{1,0:T(8,128)(2,1)S(1)}, u32[]{:S(2)}, u32[]{:S(2)}) collective-permute-start(bf16[1024,128]{1,0:T(8,128)(2,1)S(1)} %get-tuple-element.49.a0), channel_id=1, source_target_pairs={{0,32},{1,9},{2,34},{3,11},{4,36},{5,13},{6,38},{7,15},{8,40},{9,1... | collective-permute-start | bytes 786440 | tf_op jit(solution)/shard_map/ppermute | solution.py:34
  15.0 9.9 %collective-permute-start.8 = (bf16[1024,128]{1,0:T(8,128)(2,1)S(1)}, bf16[1024,128]{1,0:T(8,128)(2,1)S(1)}, u32[]{:S(2)}, u32[]{:S(2)}) collective-permute-start(bf16[1024,128]{1,0:T(8,128)(2,1)S(1)} %get-tuple-element.49.a0), channel_id=1, source_target_pairs={{0,64},{1,17},{2,66},{3,19},{4,68},{5,21},{6,70},{7,23},{8,72},{9,... | collective-permute-start | bytes 786440 | tf_op jit(solution)/shard_map/ppermute | solution.py:34
  18.3 6.6 %collective-permute-start.9 = (bf16[1024,128]{1,0:T(8,128)(2,1)S(1)}, bf16[1024,128]{1,0:T(8,128)(2,1)S(1)}, u32[]{:S(2)}, u32[]{:S(2)}) collective-permute-start(bf16[1024,128]{1,0:T(8,128)(2,1)S(1)} %get-tuple-element.49.a0), channel_id=1, source_target_pairs={{0,96},{1,25},{2,98},{3,27},{4,100},{5,29},{6,102},{7,31},{8,104},... | collective-permute-start | bytes 786440 | tf_op jit(solution)/shard_map/ppermute | solution.py:34
  24.9 30.0 %collective-permute-start.10 = (bf16[4096,128]{1,0:T(8,128)(2,1)S(1)}, bf16[4096,128]{1,0:T(8,128)(2,1)S(1)}, u32[]{:S(2)}, u32[]{:S(2)}) collective-permute-start(bf16[4096,128]{1,0:T(8,128)(2,1)S(1)} %shard_map.68.near.refs_2_), channel_id=1, source_target_pairs={{0,8},{1,33},{2,10},{3,35},{4,12},{5,37},{6,14},{7,39},{8,16},{9,4... | collective-permute-start | bytes 3145736 | tf_op jit(solution)/shard_map/ppermute | solution.py:34
  25.5 30.2 %collective-permute-start.12 = (bf16[4096,128]{1,0:T(8,128)(2,1)S(1)}, bf16[4096,128]{1,0:T(8,128)(2,1)S(1)}, u32[]{:S(2)}, u32[]{:S(2)}) collective-permute-start(bf16[4096,128]{1,0:T(8,128)(2,1)S(1)} %shard_map.68.near.refs_2_), channel_id=1, source_target_pairs={{0,24},{1,97},{2,26},{3,99},{4,28},{5,101},{6,30},{7,103},{8,0},{9... | collective-permute-start | bytes 3145736 | tf_op jit(solution)/shard_map/ppermute | solution.py:34
  26.4 17.2 %collective-permute-start.6 = (bf16[256,256]{1,0:T(8,128)(2,1)S(1)}, bf16[256,256]{1,0:T(8,128)(2,1)S(1)}, u32[]{:S(2)}, u32[]{:S(2)}) collective-permute-start(bf16[256,256]{1,0:T(8,128)(2,1)S(1)} %get-tuple-element.48), channel_id=1, source_target_pairs={{0,8},{1,9},{2,10},{3,11},{4,12},{5,13},{6,14},{7,15},{8,16},{9,17... | collective-permute-start | bytes 393224 | tf_op jit(solution)/shard_map/ppermute | solution.py:34
  28.3 17.3 %collective-permute-start = (bf16[256,512]{1,0:T(8,128)(2,1)S(1)}, bf16[256,512]{1,0:T(8,128)(2,1)S(1)}, u32[]{:S(2)}, u32[]{:S(2)}) collective-permute-start(bf16[256,512]{1,0:T(8,128)(2,1)S(1)} %get-tuple-element.41), channel_id=1, source_target_pairs={{0,2},{1,3},{2,4},{3,5},{4,6},{5,7},{6,0},{7,1},{8,10},{9,11},{10,... | collective-permute-start | bytes 786440 | tf_op jit(solution)/shard_map/ppermute | solution.py:34
  29.6 16.1 %collective-permute-start.1 = (bf16[256,512]{1,0:T(8,128)(2,1)S(1)}, bf16[256,512]{1,0:T(8,128)(2,1)S(1)}, u32[]{:S(2)}, u32[]{:S(2)}) collective-permute-start(bf16[256,512]{1,0:T(8,128)(2,1)S(1)} %get-tuple-element.42), channel_id=1, source_target_pairs={{0,4},{1,5},{2,6},{3,7},{4,0},{5,1},{6,2},{7,3},{8,12},{9,13},{10,... | collective-permute-start | bytes 786440 | tf_op jit(solution)/shard_map/ppermute | solution.py:34
  43.7 7.8 %collective-permute-start.2 = (bf16[256,512]{1,0:T(8,128)(2,1)S(1)}, bf16[256,512]{1,0:T(8,128)(2,1)S(1)}, u32[]{:S(2)}, u32[]{:S(2)}) collective-permute-start(bf16[256,512]{1,0:T(8,128)(2,1)S(1)} %get-tuple-element.43), channel_id=1, source_target_pairs={{0,6},{1,7},{2,0},{3,1},{4,2},{5,3},{6,4},{7,5},{8,14},{9,15},{10,... | collective-permute-start | bytes 786440 | tf_op jit(solution)/shard_map/ppermute | solution.py:34
  54.9 12.8 %collective-permute-start.11 = (bf16[2048,128]{1,0:T(8,128)(2,1)S(1)}, bf16[2048,128]{1,0:T(8,128)(2,1)S(1)}, u32[]{:S(2)}, u32[]{:S(2)}) collective-permute-start(bf16[2048,128]{1,0:T(8,128)(2,1)S(1)} %slice.8), channel_id=1, source_target_pairs={{0,8},{1,33},{2,10},{3,35},{4,12},{5,37},{6,14},{7,39},{8,16},{9,4... | collective-permute-start | bytes 1572872 | tf_op jit(solution)/shard_map/ppermute | solution.py:34
  55.7 12.0 %collective-permute-start.13 = (bf16[2048,128]{1,0:T(8,128)(2,1)S(1)}, bf16[2048,128]{1,0:T(8,128)(2,1)S(1)}, u32[]{:S(2)}, u32[]{:S(2)}) collective-permute-start(bf16[2048,128]{1,0:T(8,128)(2,1)S(1)} %slice.9), channel_id=1, source_target_pairs={{0,24},{1,97},{2,26},{3,99},{4,28},{5,101},{6,30},{7,103},{8,0},{9... | collective-permute-start | bytes 1572872 | tf_op jit(solution)/shard_map/ppermute | solution.py:34
  56.6 30.4 %slice-start = ((s8[16777216]{0:T(1024)(128)(4,1)}), s8[4194304]{0:T(1024)(128)(4,1)S(1)}, s32[]{:S(2)}) async-start(s8[16777216]{0:T(1024)(128)(4,1)} %bitcast.6), calls=%async_computation | async-start | bytes 8388608
  56.6 30.5 %slice-start.1 = ((s8[16777216]{0:T(1024)(128)(4,1)}), s8[4194304]{0:T(1024)(128)(4,1)S(1)}, s32[]{:S(2)}) async-start(s8[16777216]{0:T(1024)(128)(4,1)} %bitcast.6), calls=%async_computation.1 | async-start | bytes 8388608
  56.6 30.5 %slice-start.2 = ((s8[16777216]{0:T(1024)(128)(4,1)}), s8[4194304]{0:T(1024)(128)(4,1)S(1)}, s32[]{:S(2)}) async-start(s8[16777216]{0:T(1024)(128)(4,1)} %bitcast.6), calls=%async_computation.2 | async-start | bytes 8388608
  67.7 19.3 %slice-start.3 = ((s8[16777216]{0:T(1024)(128)(4,1)}), s8[4194304]{0:T(1024)(128)(4,1)S(1)}, s32[]{:S(2)}) async-start(s8[16777216]{0:T(1024)(128)(4,1)} %bitcast.6), calls=%async_computation.3 | async-start | bytes 8388608
  74.6 12.4 %collective-permute-start.15 = (bf16[256,512]{1,0:T(8,128)(2,1)S(1)}, bf16[256,512]{1,0:T(8,128)(2,1)S(1)}, u32[]{:S(2)}, u32[]{:S(2)}) collective-permute-start(bf16[256,512]{1,0:T(8,128)(2,1)S(1)} %get-tuple-element.73), channel_id=1, source_target_pairs={{0,6},{1,7},{2,0},{3,1},{4,2},{5,3},{6,4},{7,5},{8,14},{9,15},{10,... | collective-permute-start | bytes 786440 | tf_op jit(solution)/shard_map/ppermute | solution.py:34
  77.8 9.2 %collective-permute-start.16 = (bf16[256,512]{1,0:T(8,128)(2,1)S(1)}, bf16[256,512]{1,0:T(8,128)(2,1)S(1)}, u32[]{:S(2)}, u32[]{:S(2)}) collective-permute-start(bf16[256,512]{1,0:T(8,128)(2,1)S(1)} %get-tuple-element.74), channel_id=1, source_target_pairs={{0,4},{1,5},{2,6},{3,7},{4,0},{5,1},{6,2},{7,3},{8,12},{9,13},{10,... | collective-permute-start | bytes 786440 | tf_op jit(solution)/shard_map/ppermute | solution.py:34
  82.0 9.0 %collective-permute-start.14 = (bf16[256,512]{1,0:T(8,128)(2,1)S(1)}, bf16[256,512]{1,0:T(8,128)(2,1)S(1)}, u32[]{:S(2)}, u32[]{:S(2)}) collective-permute-start(bf16[256,512]{1,0:T(8,128)(2,1)S(1)} %get-tuple-element.66), channel_id=1, source_target_pairs={{0,2},{1,3},{2,4},{3,5},{4,6},{5,7},{6,0},{7,1},{8,10},{9,11},{10,... | collective-permute-start | bytes 786440 | tf_op jit(solution)/shard_map/ppermute | solution.py:34
  92.3 7.8 %collective-permute-start.17 = (bf16[128,4096]{1,0:T(8,128)(2,1)S(1)}, bf16[128,4096]{1,0:T(8,128)(2,1)S(1)}, u32[]{:S(2)}, u32[]{:S(2)}) collective-permute-start(bf16[128,4096]{1,0:T(8,128)(2,1)S(1)} %shard_map.76), channel_id=1, source_target_pairs={{0,1},{1,0},{2,3},{3,2},{4,5},{5,4},{6,7},{7,6},{8,9},{9,8},{10,11... | collective-permute-start | bytes 3145736 | tf_op jit(solution)/shard_map/ppermute | solution.py:34

commit v7 on v6

--- a/solution.py
+++ b/solution.py
@@ -61,12 +61,16 @@
     return at - VERT + jnp.where(table_ref[at] < block, 1, 0)
 
 
-def kv_kernel(place_ref, keys_ref, values_ref, *out_refs):
-    y = place_ref[1]
-    for by in range(4):
-        lanes = pl.ds(pl.multiple_of((y + by) % 4 * HEAD_DIM, HEAD_DIM), HEAD_DIM)
-        out_refs[by][:, 0:128] = keys_ref[:, lanes]
-        out_refs[by][:, 128:256] = values_ref[:, lanes]
+def kv_kernel(place_ref, keys, values, o0, o1, o2, o3, sems):
+    moves = []
+    for by, out in enumerate((o0, o1, o2, o3)):
+        lanes = pl.ds(pl.multiple_of((place_ref[1] + by) % 4 * HEAD_DIM, HEAD_DIM), HEAD_DIM)
+        moves.append(pltpu.make_async_copy(keys.at[:, lanes], out.at[:, 0:128], sems.at[2 * by]))
+        moves.append(pltpu.make_async_copy(values.at[:, lanes], out.at[:, 128:256], sems.at[2 * by + 1]))
+    for move in moves:
+        move.start()
+    for move in moves:
+        move.wait()
 
 
 def q_kernel(place_ref, queries_ref, *out_refs):
@@ -386,6 +390,8 @@
 
 SMEM = pl.BlockSpec(memory_space=pltpu.SMEM)
 VMEM = pl.BlockSpec(memory_space=pltpu.VMEM)
+HBM = pl.BlockSpec(memory_space=pltpu.HBM)
+LIMIT = 54900
 
 
 def bf16(*shape):
@@ -431,7 +437,15 @@
 def layer(queries, keys, values, vertical, slash, out_weight):
     x, z, y, c = (lax.axis_index(a) for a in ALL)
     place = jnp.stack([x * 4 + z, y, jnp.where(c == 0, x, z), jnp.where(c == 0, z, x), c]).astype(jnp.int32)
-    kv = call(kv_kernel, [bf16(SLAB, 256)] * 4, [place], [keys, values], 1e6, 4)
+    kv = pl.pallas_call(
+        kv_kernel,
+        out_shape=[bf16(SLAB, 256)] * 4,
+        in_specs=[SMEM, HBM, HBM],
+        out_specs=[VMEM] * 4,
+        scratch_shapes=[pltpu.SemaphoreType.DMA((8,))],
+        compiler_params=pltpu.CompilerParams(vmem_limit_bytes=LIMIT * 1024),
+        name="kv",
+    )(place, keys, values)
     kv = [kv[0]] + [along_y(kv[by], by) for by in (1, 2, 3)]
     q = call(q_kernel, [bf16(SLAB, 512)] * 4, [place], [queries], 1e6, 4)
     q = [q[0]] + [along_y(q[by], by) for by in (1, 2, 3)]

time: 101 us -> 102 us (level)
  local copies, waits for them, and re-layouts: 3.51 us -> 1.54 us
  Pallas kernels: 40.5 us -> 42.4 us
    pallas_call x0 -> x1, Pallas kernels: none -> 2.39 us  [layer(): pl.pallas_call(kv_kernel, out_shape=[bf16(SLAB, 256)] * 4, in_specs=[SMEM...]
    unnamed x18 -> x14, local copies, waits for them, and re-layouts: 3.35 us -> 1.38 us
    pallas_call x13 -> x12, Pallas kernels: 40.5 us -> 40 us  [call(): pl.pallas_call(kernel, out_shape=outs, in_specs=[SMEM] * len(scalars) + [...]
where the time goes in v7:
time: 102 us; the launch traced here: 101 us
  Pallas kernels  42.4 us (42%)
  starting transfers between devices  30.7 us (30%)
  waiting for transfers between devices  25.3 us (25%)
  local copies, waits for them, and re-layouts  1.54 us (2%)
  other arithmetic  1.22 us (1%)
    pallas_call x12, Pallas kernels, call(): pl.pallas_call(kernel, out_shape=outs, in_specs=[SMEM] * len(scalars) + [...  40 us
    ppermute x18, starting transfers between devices, moved(): return lax.ppermute(value, ALL, pairs)  30.7 us
    ppermute x18, waiting for transfers between devices, moved(): return lax.ppermute(value, ALL, pairs)  25.3 us
    pallas_call x1, Pallas kernels, layer(): pl.pallas_call(kv_kernel, out_shape=[bf16(SLAB, 256)] * 4, in_specs=[SMEM...  2.39 us
  transfers between devices with their start and end apart: 18, of which 6 were waited for; matrix products, arithmetic and copies ran while one was open for 0% of the time, Pallas kernels for 30%

profile of v7, /device:TPU:7, one launch (start us, length us, event | category | flops | bytes accessed | tf_op | source)
XLA Modules:
  0.0 101.4 jit_solution(9766094208398140180)
XLA Ops:
  0.0 0.1 stack.23.place_ref
  0.1 2.4 %kv.1 = (bf16[256,256]{1,0:T(8,128)(2,1)S(1)}, bf16[256,256]{1,0:T(8,128)(2,1)S(1)}, bf16[256,256]{1,0:T(8,128)(2,1)}, bf16[256,256]{1,0:T(8,128)(2,1)}) custom-call(s32[5]{0:T(128)S(1)} %stack.23.place_ref, bf16[256,512]{1,0:T(8,128)(2,1)} %keys.1, bf16[256,512]{1,0:T(8,128)(2,1)} %values.1), custom_call_target="tpu_custom_call" | custom-call | tf_op jit(solution)/shard_map/kv/pallas_call | solution.py:440
  2.5 1.4 %collective-permute-start.3 = (bf16[256,256]{1,0:T(8,128)(2,1)S(1)}, bf16[256,256]{1,0:T(8,128)(2,1)S(1)}, u32[]{:S(2)}, u32[]{:S(2)}) collective-permute-start(bf16[256,256]{1,0:T(8,128)(2,1)S(1)} %get-tuple-element.45), channel_id=1, source_target_pairs={{0,2},{1,3},{2,4},{3,5},{4,6},{5,7},{6,0},{7,1},{8,10},{9,11},{10,... | collective-permute-start | bytes 393224 | tf_op jit(solution)/shard_map/ppermute | solution.py:34
  3.8 2.6 %collective-permute-start.4 = (bf16[256,256]{1,0:T(8,128)(2,1)}, bf16[256,256]{1,0:T(8,128)(2,1)S(1)}, u32[]{:S(2)}, u32[]{:S(2)}) collective-permute-start(bf16[256,256]{1,0:T(8,128)(2,1)} %get-tuple-element.46), channel_id=1, source_target_pairs={{0,4},{1,5},{2,6},{3,7},{4,0},{5,1},{6,2},{7,3},{8,12},{9,13},{10,... | collective-permute-start | bytes 393224 | tf_op jit(solution)/shard_map/ppermute | solution.py:34
  6.5 1.1 %collective-permute-start.5 = (bf16[256,256]{1,0:T(8,128)(2,1)}, bf16[256,256]{1,0:T(8,128)(2,1)S(1)}, u32[]{:S(2)}, u32[]{:S(2)}) collective-permute-start(bf16[256,256]{1,0:T(8,128)(2,1)} %get-tuple-element.47), channel_id=1, source_target_pairs={{0,6},{1,7},{2,0},{3,1},{4,2},{5,3},{6,4},{7,5},{8,14},{9,15},{10,... | collective-permute-start | bytes 393224 | tf_op jit(solution)/shard_map/ppermute | solution.py:34
  7.5 0.7 copy-done.1
  8.2 0.7 copy-done.2
  8.9 2.3 %shard_map.64.table_ref.place_ref = s32[192]{0:T(256)S(1)} custom-call(s32[5]{0:T(128)S(1)} %stack.23.place_ref, s32[4,64]{1,0:T(4,128)S(1)} %copy-done.1, s32[2,4]{1,0:T(2,128)S(1)} %bitcast.8), custom_call_target="tpu_custom_call" | custom-call | flops 1000000 | bytes 1000000 | tf_op jit(solution)/shard_map/pallas_call | solution.py:425
  11.2 0.0 collective-permute-done.3.kv1
  11.2 1.0 collective-permute-done.4.kv2
  12.2 0.0 collective-permute-done.5.kv3
  12.2 0.8 shard_map.66
  13.0 1.7 %collective-permute-start.7 = (bf16[1024,128]{1,0:T(8,128)(2,1)S(1)}, bf16[1024,128]{1,0:T(8,128)(2,1)S(1)}, u32[]{:S(2)}, u32[]{:S(2)}) collective-permute-start(bf16[1024,128]{1,0:T(8,128)(2,1)S(1)} %get-tuple-element.49.a0), channel_id=1, source_target_pairs={{0,32},{1,9},{2,34},{3,11},{4,36},{5,13},{6,38},{7,15},{8,40},{9,1... | collective-permute-start | bytes 786440 | tf_op jit(solution)/shard_map/ppermute | solution.py:34
  14.7 3.3 %collective-permute-start.8 = (bf16[1024,128]{1,0:T(8,128)(2,1)S(1)}, bf16[1024,128]{1,0:T(8,128)(2,1)S(1)}, u32[]{:S(2)}, u32[]{:S(2)}) collective-permute-start(bf16[1024,128]{1,0:T(8,128)(2,1)S(1)} %get-tuple-element.49.a0), channel_id=1, source_target_pairs={{0,64},{1,17},{2,66},{3,19},{4,68},{5,21},{6,70},{7,23},{8,72},{9,... | collective-permute-start | bytes 786440 | tf_op jit(solution)/shard_map/ppermute | solution.py:34
  18.0 0.7 collective-permute-start.9
  18.8 2.1 %collective-permute-done.7.a1 = bf16[1024,128]{1,0:T(8,128)(2,1)S(1)} collective-permute-done((bf16[1024,128]{1,0:T(8,128)(2,1)S(1)}, bf16[1024,128]{1,0:T(8,128)(2,1)S(1)}, u32[]{:S(2)}, u32[]{:S(2)}) %collective-permute-start.7) | collective-permute-done | bytes 262176 | tf_op jit(solution)/shard_map/ppermute | solution.py:34
  20.9 3.7 %collective-permute-done.8.a2 = bf16[1024,128]{1,0:T(8,128)(2,1)S(1)} collective-permute-done((bf16[1024,128]{1,0:T(8,128)(2,1)S(1)}, bf16[1024,128]{1,0:T(8,128)(2,1)S(1)}, u32[]{:S(2)}, u32[]{:S(2)}) %collective-permute-start.8) | collective-permute-done | bytes 262176 | tf_op jit(solution)/shard_map/ppermute | solution.py:34
  24.6 0.0 collective-permute-done.9.a3
  24.6 0.1 shard_map.67.near.refs_2_
  24.7 0.6 collective-permute-start.10
  25.2 1.0 collective-permute-start.12
  26.2 1.2 %collective-permute-start.6 = (bf16[256,256]{1,0:T(8,128)(2,1)S(1)}, bf16[256,256]{1,0:T(8,128)(2,1)S(1)}, u32[]{:S(2)}, u32[]{:S(2)}) collective-permute-start(bf16[256,256]{1,0:T(8,128)(2,1)S(1)} %get-tuple-element.48), channel_id=1, source_target_pairs={{0,8},{1,9},{2,10},{3,11},{4,12},{5,13},{6,14},{7,15},{8,16},{9,17... | collective-permute-start | bytes 393224 | tf_op jit(solution)/shard_map/ppermute | solution.py:34
  27.5 0.6 shard_map.65
  28.1 1.5 %collective-permute-start = (bf16[256,512]{1,0:T(8,128)(2,1)S(1)}, bf16[256,512]{1,0:T(8,128)(2,1)S(1)}, u32[]{:S(2)}, u32[]{:S(2)}) collective-permute-start(bf16[256,512]{1,0:T(8,128)(2,1)S(1)} %get-tuple-element.41), channel_id=1, source_target_pairs={{0,2},{1,3},{2,4},{3,5},{4,6},{5,7},{6,0},{7,1},{8,10},{9,11},{10,... | collective-permute-start | bytes 786440 | tf_op jit(solution)/shard_map/ppermute | solution.py:34
  29.6 2.2 %collective-permute-start.1 = (bf16[256,512]{1,0:T(8,128)(2,1)S(1)}, bf16[256,512]{1,0:T(8,128)(2,1)S(1)}, u32[]{:S(2)}, u32[]{:S(2)}) collective-permute-start(bf16[256,512]{1,0:T(8,128)(2,1)S(1)} %get-tuple-element.42), channel_id=1, source_target_pairs={{0,4},{1,5},{2,6},{3,7},{4,0},{5,1},{6,2},{7,3},{8,12},{9,13},{10,... | collective-permute-start | bytes 786440 | tf_op jit(solution)/shard_map/ppermute | solution.py:34
  31.8 11.7 %collective-permute-done.6.prev_ref = bf16[256,256]{1,0:T(8,128)(2,1)S(1)} collective-permute-done((bf16[256,256]{1,0:T(8,128)(2,1)S(1)}, bf16[256,256]{1,0:T(8,128)(2,1)S(1)}, u32[]{:S(2)}, u32[]{:S(2)}) %collective-permute-start.6) | collective-permute-done | bytes 131104 | tf_op jit(solution)/shard_map/ppermute | solution.py:34
  43.4 2.2 %collective-permute-start.2 = (bf16[256,512]{1,0:T(8,128)(2,1)S(1)}, bf16[256,512]{1,0:T(8,128)(2,1)S(1)}, u32[]{:S(2)}, u32[]{:S(2)}) collective-permute-start(bf16[256,512]{1,0:T(8,128)(2,1)S(1)} %get-tuple-element.43), channel_id=1, source_target_pairs={{0,6},{1,7},{2,0},{3,1},{4,2},{5,3},{6,4},{7,5},{8,14},{9,15},{10,... | collective-permute-start | bytes 786440 | tf_op jit(solution)/shard_map/ppermute | solution.py:34
  45.6 0.0 collective-permute-done.1.q2
  45.6 5.8 %collective-permute-done.2.q3 = bf16[256,512]{1,0:T(8,128)(2,1)S(1)} collective-permute-done((bf16[256,512]{1,0:T(8,128)(2,1)S(1)}, bf16[256,512]{1,0:T(8,128)(2,1)S(1)}, u32[]{:S(2)}, u32[]{:S(2)}) %collective-permute-start.2) | collective-permute-done | bytes 262176 | tf_op jit(solution)/shard_map/ppermute | solution.py:34
  51.4 3.4 %shard_map.68 = (bf16[16,256,128]{2,1,0:T(8,128)(2,1)S(1)}, bf16[4224,128]{1,0:T(8,128)(2,1)S(1)}, bf16[4224,128]{1,0:T(8,128)(2,1)S(1)}, f32[16,8,256]{2,1,0:T(...) custom-call(s32[192]{0:T(256)S(1)} %shard_map.64.table_ref.place_ref, ...), custom_call_target="tpu_custom_call" | custom-call | flops 3000000000 | bytes 1000000 | tf_op jit(solution)/shard_map/pallas_call | solution.py:425
  54.9 0.7 collective-permute-start.11
  55.6 0.0 collective-permute-done.12.refs_1_
  55.7 0.9 collective-permute-start.13
  56.5 11.2 %shard_map.69 = (bf16[4224,128]{1,0:T(8,128)(2,1)S(1)}, bf16[4224,128]{1,0:T(8,128)(2,1)S(1)}, f32[16,8,256]{2,1,0:T(8,128)S(1)}, f32[16,8,256]{2,1,0:T(8,128)S(1)}, f32[16,128,256]{2,1,0:T(8,128)S(1)}) custom-call(s32[192]{0:T(256)S(1)} %shard_map.64.table_ref.place_ref, ...), custom_call_target="tpu_custom_call", output_to_operand_aliasing={{0}: (4, {}), {1}: (5, {}), {2}: (6, {}), {3}: (7, {}), {4}... | custom-call | flops 15000000512 | bytes 1000000 | tf_op jit(solution)/shard_map/pallas_call | solution.py:425
  67.7 0.0 collective-permute-done.11.refs_0_
  67.7 0.0 collective-permute-done.13.refs_1_
  67.8 0.0 slice-start.3
  67.8 6.9 %shard_map.70 = (bf16[4224,128]{1,0:T(8,128)(2,1)S(1)}, bf16[4224,128]{1,0:T(8,128)(2,1)S(1)}, f32[16,8,256]{2,1,0:T(8,128)S(1)}, f32[16,8,256]{2,1,0:T(8,128)S(...) custom-call(s32[192]{0:T(256)S(1)} %shard_map.64.table_ref.place_ref, ...), custom_call_target="tpu_custom_call", output_to_operand_aliasing={{0}: (5, {}), {1}: (6, {}), {2}: (7, {}), {3}: (8, {}), {4}... | custom-call | flops 3000000000 | bytes 1000000 | tf_op jit(solution)/shard_map/pallas_call | solution.py:425
  74.7 3.2 %collective-permute-start.15 = (bf16[256,512]{1,0:T(8,128)(2,1)S(1)}, bf16[256,512]{1,0:T(8,128)(2,1)S(1)}, u32[]{:S(2)}, u32[]{:S(2)}) collective-permute-start(bf16[256,512]{1,0:T(8,128)(2,1)S(1)} %get-tuple-element.73), channel_id=1, source_target_pairs={{0,6},{1,7},{2,0},{3,1},{4,2},{5,3},{6,4},{7,5},{8,14},{9,15},{10,... | collective-permute-start | bytes 786440 | tf_op jit(solution)/shard_map/ppermute | solution.py:34
  77.9 4.2 %shard_map.71 = (bf16[4224,128]{1,0:T(8,128)(2,1)S(1)}, bf16[4224,128]{1,0:T(8,128)(2,1)S(1)}, f32[16,8,256]{2,1,0:T(8,128)S(1)}, f32[16,8,256]{2,1,0:T(8,128)S(...) custom-call(s32[192]{0:T(256)S(1)} %shard_map.64.table_ref.place_ref, ...), custom_call_target="tpu_custom_call", output_to_operand_aliasing={{0}: (2, {}), {1}: (3, {}), {2}: (4, {}), {3}: (5, {}), {4}... | custom-call | flops 2000000000 | bytes 1000000 | tf_op jit(solution)/shard_map/pallas_call | solution.py:425
  82.1 1.0 collective-permute-start.14
  83.1 4.0 %shard_map.72 = (bf16[4224,128]{1,0:T(8,128)(2,1)S(1)}, bf16[4224,128]{1,0:T(8,128)(2,1)S(1)}, f32[16,8,256]{2,1,0:T(8,128)S(1)}, f32[16,8,256]{2,1,0:T(8,128)S(...) custom-call(s32[192]{0:T(256)S(1)} %shard_map.64.table_ref.place_ref, ...), custom_call_target="tpu_custom_call", output_to_operand_aliasing={{0}: (2, {}), {1}: (3, {}), {2}: (4, {}), {3}: (5, {}), {4}... | custom-call | flops 2000000000 | bytes 1000000 | tf_op jit(solution)/shard_map/pallas_call | solution.py:425
  87.1 4.0 %shard_map.73.total_ref = f32[256,4096]{1,0:T(8,128)S(1)} custom-call(s32[5]{0:T(128)S(1)} %stack.23.place_ref, bf16[256,512]{1,0:T(8,128)(2,1)S(1)} %get-tuple-element.72.a0, bf16[256,512]{1,0:T(8,128)(2,1)S(1)} %collective-permute-done.15.a1, bf16[256,512]{1,0:T(8,128)(2,1)S(1)} %collective-permute-done.16.a2, bf16[2048,4096]{1,0:T(8,128)(2,1)S(1)} %bitcast.7), custom_call_target="tpu_custom_call" | custom-call | flops 3000000000 | bytes 1000000 | tf_op jit(solution)/shard_map/pallas_call | solution.py:425
  91.1 1.3 %shard_map.75 = bf16[128,4096]{1,0:T(8,128)(2,1)S(1)} custom-call(s32[5]{0:T(128)S(1)} %stack.23.place_ref, bf16[256,512]{1,0:T(8,128)(2,1)S(1)} %collective-permute-done.14.a, bf16[2048,4096]{1,0:T(8,128)(2,1)S(1)} %bitcast.7, f32[256,4096]{1,0:T(8,128)S(1)} %shard_map.73.total_ref), custom_call_target="tpu_custom_call" | custom-call | flops 1000000000 | bytes 1000000 | tf_op jit(solution)/shard_map/pallas_call | solution.py:425
  92.4 5.5 %collective-permute-start.17 = (bf16[128,4096]{1,0:T(8,128)(2,1)S(1)}, bf16[128,4096]{1,0:T(8,128)(2,1)S(1)}, u32[]{:S(2)}, u32[]{:S(2)}) collective-permute-start(bf16[128,4096]{1,0:T(8,128)(2,1)S(1)} %shard_map.75), channel_id=1, source_target_pairs={{0,1},{1,0},{2,3},{3,2},{4,5},{5,4},{6,7},{7,6},{8,9},{9,8},{10,11... | collective-permute-start | bytes 3145736 | tf_op jit(solution)/shard_map/ppermute | solution.py:34
  97.9 1.3 %shard_map.74 = f32[128,4096]{1,0:T(8,128)S(1)} custom-call(s32[5]{0:T(128)S(1)} %stack.23.place_ref, bf16[256,512]{1,0:T(8,128)(2,1)S(1)} %collective-permute-done.14.a, bf16[2048,4096]{1,0:T(8,128)(2,1)S(1)} %bitcast.7, f32[256,4096]{1,0:T(8,128)S(1)} %shard_map.73.total_ref), custom_call_target="tpu_custom_call" | custom-call | flops 1000000000 | bytes 1000000 | tf_op jit(solution)/shard_map/pallas_call | solution.py:425
  99.1 1.0 collective-permute-done.17
  100.1 1.2 %add_convert_fusion = bf16[128,4096]{1,0:T(8,128)(2,1)} fusion(f32[128,4096]{1,0:T(8,128)S(1)} %shard_map.74, bf16[128,4096]{1,0:T(8,128)(2,1)S(1)} %collective-permute-done.17), kind=kLoop, calls=%fused_computation | loop fusion | flops 1572864 | bytes 4194304 | tf_op jit(solution)/shard_map/convert_element_type | solution.py:487
  (20 shorter events, 0.1 us)
Async XLA Ops:
  0.0 27.5 %copy-start = (bf16[256,2048]{1,0:T(8,128)(2,1)S(1)}, bf16[256,2048]{1,0:T(8,128)(2,1)}, u32[]{:S(2)}) copy-start(bf16[256,2048]{1,0:T(8,128)(2,1)} %queries_ref.1) | copy-start | bytes 3145732
  2.5 8.7 %collective-permute-start.3 = (bf16[256,256]{1,0:T(8,128)(2,1)S(1)}, bf16[256,256]{1,0:T(8,128)(2,1)S(1)}, u32[]{:S(2)}, u32[]{:S(2)}) collective-permute-start(bf16[256,256]{1,0:T(8,128)(2,1)S(1)} %get-tuple-element.45), channel_id=1, source_target_pairs={{0,2},{1,3},{2,4},{3,5},{4,6},{5,7},{6,0},{7,1},{8,10},{9,11},{10,... | collective-permute-start | bytes 393224 | tf_op jit(solution)/shard_map/ppermute | solution.py:34
  3.8 8.3 %collective-permute-start.4 = (bf16[256,256]{1,0:T(8,128)(2,1)}, bf16[256,256]{1,0:T(8,128)(2,1)S(1)}, u32[]{:S(2)}, u32[]{:S(2)}) collective-permute-start(bf16[256,256]{1,0:T(8,128)(2,1)} %get-tuple-element.46), channel_id=1, source_target_pairs={{0,4},{1,5},{2,6},{3,7},{4,0},{5,1},{6,2},{7,3},{8,12},{9,13},{10,... | collective-permute-start | bytes 393224 | tf_op jit(solution)/shard_map/ppermute | solution.py:34
  6.5 5.7 %collective-permute-start.5 = (bf16[256,256]{1,0:T(8,128)(2,1)}, bf16[256,256]{1,0:T(8,128)(2,1)S(1)}, u32[]{:S(2)}, u32[]{:S(2)}) collective-permute-start(bf16[256,256]{1,0:T(8,128)(2,1)} %get-tuple-element.47), channel_id=1, source_target_pairs={{0,6},{1,7},{2,0},{3,1},{4,2},{5,3},{6,4},{7,5},{8,14},{9,15},{10,... | collective-permute-start | bytes 393224 | tf_op jit(solution)/shard_map/ppermute | solution.py:34
  7.5 0.7 copy-start.1
  8.2 0.7 copy-start.2
  13.0 7.9 %collective-permute-start.7 = (bf16[1024,128]{1,0:T(8,128)(2,1)S(1)}, bf16[1024,128]{1,0:T(8,128)(2,1)S(1)}, u32[]{:S(2)}, u32[]{:S(2)}) collective-permute-start(bf16[1024,128]{1,0:T(8,128)(2,1)S(1)} %get-tuple-element.49.a0), channel_id=1, source_target_pairs={{0,32},{1,9},{2,34},{3,11},{4,36},{5,13},{6,38},{7,15},{8,40},{9,1... | collective-permute-start | bytes 786440 | tf_op jit(solution)/shard_map/ppermute | solution.py:34
  14.7 9.9 %collective-permute-start.8 = (bf16[1024,128]{1,0:T(8,128)(2,1)S(1)}, bf16[1024,128]{1,0:T(8,128)(2,1)S(1)}, u32[]{:S(2)}, u32[]{:S(2)}) collective-permute-start(bf16[1024,128]{1,0:T(8,128)(2,1)S(1)} %get-tuple-element.49.a0), channel_id=1, source_target_pairs={{0,64},{1,17},{2,66},{3,19},{4,68},{5,21},{6,70},{7,23},{8,72},{9,... | collective-permute-start | bytes 786440 | tf_op jit(solution)/shard_map/ppermute | solution.py:34
  18.0 6.6 %collective-permute-start.9 = (bf16[1024,128]{1,0:T(8,128)(2,1)S(1)}, bf16[1024,128]{1,0:T(8,128)(2,1)S(1)}, u32[]{:S(2)}, u32[]{:S(2)}) collective-permute-start(bf16[1024,128]{1,0:T(8,128)(2,1)S(1)} %get-tuple-element.49.a0), channel_id=1, source_target_pairs={{0,96},{1,25},{2,98},{3,27},{4,100},{5,29},{6,102},{7,31},{8,104},... | collective-permute-start | bytes 786440 | tf_op jit(solution)/shard_map/ppermute | solution.py:34
  24.7 30.2 %collective-permute-start.10 = (bf16[4096,128]{1,0:T(8,128)(2,1)S(1)}, bf16[4096,128]{1,0:T(8,128)(2,1)S(1)}, u32[]{:S(2)}, u32[]{:S(2)}) collective-permute-start(bf16[4096,128]{1,0:T(8,128)(2,1)S(1)} %shard_map.67.near.refs_2_), channel_id=1, source_target_pairs={{0,8},{1,33},{2,10},{3,35},{4,12},{5,37},{6,14},{7,39},{8,16},{9,4... | collective-permute-start | bytes 3145736 | tf_op jit(solution)/shard_map/ppermute | solution.py:34
  25.2 30.4 %collective-permute-start.12 = (bf16[4096,128]{1,0:T(8,128)(2,1)S(1)}, bf16[4096,128]{1,0:T(8,128)(2,1)S(1)}, u32[]{:S(2)}, u32[]{:S(2)}) collective-permute-start(bf16[4096,128]{1,0:T(8,128)(2,1)S(1)} %shard_map.67.near.refs_2_), channel_id=1, source_target_pairs={{0,24},{1,97},{2,26},{3,99},{4,28},{5,101},{6,30},{7,103},{8,0},{9... | collective-permute-start | bytes 3145736 | tf_op jit(solution)/shard_map/ppermute | solution.py:34
  26.2 17.2 %collective-permute-start.6 = (bf16[256,256]{1,0:T(8,128)(2,1)S(1)}, bf16[256,256]{1,0:T(8,128)(2,1)S(1)}, u32[]{:S(2)}, u32[]{:S(2)}) collective-permute-start(bf16[256,256]{1,0:T(8,128)(2,1)S(1)} %get-tuple-element.48), channel_id=1, source_target_pairs={{0,8},{1,9},{2,10},{3,11},{4,12},{5,13},{6,14},{7,15},{8,16},{9,17... | collective-permute-start | bytes 393224 | tf_op jit(solution)/shard_map/ppermute | solution.py:34
  28.1 17.5 %collective-permute-start = (bf16[256,512]{1,0:T(8,128)(2,1)S(1)}, bf16[256,512]{1,0:T(8,128)(2,1)S(1)}, u32[]{:S(2)}, u32[]{:S(2)}) collective-permute-start(bf16[256,512]{1,0:T(8,128)(2,1)S(1)} %get-tuple-element.41), channel_id=1, source_target_pairs={{0,2},{1,3},{2,4},{3,5},{4,6},{5,7},{6,0},{7,1},{8,10},{9,11},{10,... | collective-permute-start | bytes 786440 | tf_op jit(solution)/shard_map/ppermute | solution.py:34
  29.6 16.1 %collective-permute-start.1 = (bf16[256,512]{1,0:T(8,128)(2,1)S(1)}, bf16[256,512]{1,0:T(8,128)(2,1)S(1)}, u32[]{:S(2)}, u32[]{:S(2)}) collective-permute-start(bf16[256,512]{1,0:T(8,128)(2,1)S(1)} %get-tuple-element.42), channel_id=1, source_target_pairs={{0,4},{1,5},{2,6},{3,7},{4,0},{5,1},{6,2},{7,3},{8,12},{9,13},{10,... | collective-permute-start | bytes 786440 | tf_op jit(solution)/shard_map/ppermute | solution.py:34
  43.4 8.0 %collective-permute-start.2 = (bf16[256,512]{1,0:T(8,128)(2,1)S(1)}, bf16[256,512]{1,0:T(8,128)(2,1)S(1)}, u32[]{:S(2)}, u32[]{:S(2)}) collective-permute-start(bf16[256,512]{1,0:T(8,128)(2,1)S(1)} %get-tuple-element.43), channel_id=1, source_target_pairs={{0,6},{1,7},{2,0},{3,1},{4,2},{5,3},{6,4},{7,5},{8,14},{9,15},{10,... | collective-permute-start | bytes 786440 | tf_op jit(solution)/shard_map/ppermute | solution.py:34
  54.9 12.8 %collective-permute-start.11 = (bf16[2048,128]{1,0:T(8,128)(2,1)S(1)}, bf16[2048,128]{1,0:T(8,128)(2,1)S(1)}, u32[]{:S(2)}, u32[]{:S(2)}) collective-permute-start(bf16[2048,128]{1,0:T(8,128)(2,1)S(1)} %slice.8), channel_id=1, source_target_pairs={{0,8},{1,33},{2,10},{3,35},{4,12},{5,37},{6,14},{7,39},{8,16},{9,4... | collective-permute-start | bytes 1572872 | tf_op jit(solution)/shard_map/ppermute | solution.py:34
  55.7 12.1 %collective-permute-start.13 = (bf16[2048,128]{1,0:T(8,128)(2,1)S(1)}, bf16[2048,128]{1,0:T(8,128)(2,1)S(1)}, u32[]{:S(2)}, u32[]{:S(2)}) collective-permute-start(bf16[2048,128]{1,0:T(8,128)(2,1)S(1)} %slice.9), channel_id=1, source_target_pairs={{0,24},{1,97},{2,26},{3,99},{4,28},{5,101},{6,30},{7,103},{8,0},{9... | collective-permute-start | bytes 1572872 | tf_op jit(solution)/shard_map/ppermute | solution.py:34
  56.5 30.5 %slice-start = ((s8[16777216]{0:T(1024)(128)(4,1)}), s8[4194304]{0:T(1024)(128)(4,1)S(1)}, s32[]{:S(2)}) async-start(s8[16777216]{0:T(1024)(128)(4,1)} %bitcast.6), calls=%async_computation | async-start | bytes 8388608
  56.5 30.5 %slice-start.1 = ((s8[16777216]{0:T(1024)(128)(4,1)}), s8[4194304]{0:T(1024)(128)(4,1)S(1)}, s32[]{:S(2)}) async-start(s8[16777216]{0:T(1024)(128)(4,1)} %bitcast.6), calls=%async_computation.1 | async-start | bytes 8388608
  56.5 30.6 %slice-start.2 = ((s8[16777216]{0:T(1024)(128)(4,1)}), s8[4194304]{0:T(1024)(128)(4,1)S(1)}, s32[]{:S(2)}) async-start(s8[16777216]{0:T(1024)(128)(4,1)} %bitcast.6), calls=%async_computation.2 | async-start | bytes 8388608
  67.8 19.4 %slice-start.3 = ((s8[16777216]{0:T(1024)(128)(4,1)}), s8[4194304]{0:T(1024)(128)(4,1)S(1)}, s32[]{:S(2)}) async-start(s8[16777216]{0:T(1024)(128)(4,1)} %bitcast.6), calls=%async_computation.3 | async-start | bytes 8388608
  74.7 12.4 %collective-permute-start.15 = (bf16[256,512]{1,0:T(8,128)(2,1)S(1)}, bf16[256,512]{1,0:T(8,128)(2,1)S(1)}, u32[]{:S(2)}, u32[]{:S(2)}) collective-permute-start(bf16[256,512]{1,0:T(8,128)(2,1)S(1)} %get-tuple-element.73), channel_id=1, source_target_pairs={{0,6},{1,7},{2,0},{3,1},{4,2},{5,3},{6,4},{7,5},{8,14},{9,15},{10,... | collective-permute-start | bytes 786440 | tf_op jit(solution)/shard_map/ppermute | solution.py:34
  77.9 9.2 %collective-permute-start.16 = (bf16[256,512]{1,0:T(8,128)(2,1)S(1)}, bf16[256,512]{1,0:T(8,128)(2,1)S(1)}, u32[]{:S(2)}, u32[]{:S(2)}) collective-permute-start(bf16[256,512]{1,0:T(8,128)(2,1)S(1)} %get-tuple-element.74), channel_id=1, source_target_pairs={{0,4},{1,5},{2,6},{3,7},{4,0},{5,1},{6,2},{7,3},{8,12},{9,13},{10,... | collective-permute-start | bytes 786440 | tf_op jit(solution)/shard_map/ppermute | solution.py:34
  82.1 9.0 %collective-permute-start.14 = (bf16[256,512]{1,0:T(8,128)(2,1)S(1)}, bf16[256,512]{1,0:T(8,128)(2,1)S(1)}, u32[]{:S(2)}, u32[]{:S(2)}) collective-permute-start(bf16[256,512]{1,0:T(8,128)(2,1)S(1)} %get-tuple-element.66), channel_id=1, source_target_pairs={{0,2},{1,3},{2,4},{3,5},{4,6},{5,7},{6,0},{7,1},{8,10},{9,11},{10,... | collective-permute-start | bytes 786440 | tf_op jit(solution)/shard_map/ppermute | solution.py:34
  92.4 7.8 %collective-permute-start.17 = (bf16[128,4096]{1,0:T(8,128)(2,1)S(1)}, bf16[128,4096]{1,0:T(8,128)(2,1)S(1)}, u32[]{:S(2)}, u32[]{:S(2)}) collective-permute-start(bf16[128,4096]{1,0:T(8,128)(2,1)S(1)} %shard_map.75), channel_id=1, source_target_pairs={{0,1},{1,0},{2,3},{3,2},{4,5},{5,4},{6,7},{7,6},{8,9},{9,8},{10,11... | collective-permute-start | bytes 3145736 | tf_op jit(solution)/shard_map/ppermute | solution.py:34
